TPU v7x, 32 devices: a whole 2x2x4 slice. The times are simulated.
32 devices in a mesh: section: 4 (over x, core), dp: 8 (over z, y).
Axes of the slice: x: 2, y: 2, z: 4, core: 2. Of those that a mesh axis runs over, the one named last changes fastest.
Arguments:
- student_states: bfloat16 [64, 512, 1024], P('dp'), may hold values from -6 to 6
- lengths: int32 [64], P('dp'), may hold values from 64 to 512
- student_ln_gain: float32 [1024], replicated, may hold values from 0.1 to 1.9
- student_w_in: bfloat16 [1024, 4096], P(None, 'section'), may hold values from -0.1875 to 0.1875
- student_w_out: bfloat16 [4096, 1024], P('section'), may hold values from -0.09375 to 0.09375
- teacher_rows: bfloat16 [64, 4096], P('dp'), may hold values from -6 to 6
- teacher_mlp_gain: float32 [4096], replicated, may hold values from 0.1 to 1.9
- teacher_gate_up: bfloat16 [2, 4096, 12288], P(None, 'dp', 'section'), may hold values from -0.09375 to 0.09375
- teacher_down: bfloat16 [12288, 4096], P('section', 'dp'), may hold values from -0.0546875 to 0.0546875
- teacher_final_gain: float32 [4096], replicated, may hold values from 0.1 to 1.9
Outputs:
- loss: float32 [], replicated
- grad_w_in: float32 [1024, 4096], P('dp', 'section')
- grad_w_out: float32 [4096, 1024], P(('section', 'dp'))
- teacher_states: float32 [64, 4096], P('dp', 'section')
Inputs may be any that keep to these rules, and one draw needn't show every extreme that they name: Each document's first lengths tokens are real, the rest padding.
All inputs are finite; a program needn't handle non-finite values.
Results may differ from a plain program's by a relative error of at most 0.013.
The roundings to bfloat16 on the way count: a program that leaves them out, or rounds other values in their place, can miss the bound.
Values may be sent and summed in bfloat16 or wider, within the bound.
No kernel may reach another device: no remote copies, remote signals or barrier semaphores. Data moves between devices by JAX's collectives and lax.ppermute only.
A program may use at most 128 MiB of HBM per device.

v0:
```python
import jax
import jax.numpy as jnp
from jax import lax
from jax.sharding import PartitionSpec as P

student_softness = 0.05
teacher_softness = 0.02


def layer_norm(states, gain):
    values = states.astype(jnp.float32)
    center = values - jnp.mean(values, -1, keepdims=True)
    spread = jnp.mean(center * center, -1, keepdims=True)
    return (center * lax.rsqrt(spread + 1e-05) * gain).astype(jnp.bfloat16)


def gelu_exact(value):
    return 0.5 * value * (1.0 + jax.scipy.special.erf(value * 0.7071067811865476))


def gelu_slope(value):
    return (
        0.5 * (1.0 + jax.scipy.special.erf(value * 0.7071067811865476))
        + value * jnp.exp(-0.5 * value * value) * 0.3989422804014327
    )


def contrast(student_logits, teacher_logits, row_ids, col_ids):
    keep = row_ids[:, None] != col_ids[None, :]
    partner = (row_ids + 1 - 2 * (row_ids % 2))[:, None] == col_ids[None, :]
    s_exp = jnp.where(keep, jnp.exp(student_logits), 0.0)
    t_exp = jnp.where(keep, jnp.exp(teacher_logits), 0.0)
    s_total = jnp.sum(s_exp, -1, keepdims=True)
    t_total = jnp.sum(t_exp, -1, keepdims=True)
    s_prob = s_exp / s_total
    t_prob = t_exp / t_total
    s_log = student_logits - jnp.log(s_total)
    t_log = teacher_logits - jnp.log(t_total)
    terms = jnp.where(partner, -s_log, 0.0) + jnp.where(keep, t_prob * (t_log - s_log), 0.0)
    gradient_list = 2.0 * s_prob - partner.astype(jnp.float32) - t_prob
    return (gradient_list, jnp.sum(terms))


def on_device(
    student_states,
    lengths,
    student_ln_gain,
    student_w_in,
    student_w_out,
    teacher_rows,
    teacher_mlp_gain,
    teacher_gate_up,
    teacher_down,
    teacher_final_gain,
):
    dp_count = lax.axis_size("dp")
    dp_index = lax.axis_index("dp")
    section_index = lax.axis_index("section")
    local_docs = teacher_rows.shape[0]
    total_docs = local_docs * dp_count
    highest_precision = lax.Precision.HIGHEST
    rows_f = teacher_rows.astype(jnp.float32)
    inverse = lax.rsqrt(jnp.mean(rows_f * rows_f, -1, keepdims=True) + 1e-06)
    normed = (rows_f * inverse * teacher_mlp_gain).astype(jnp.bfloat16)
    col_width = teacher_gate_up.shape[1]
    hidden_width = teacher_gate_up.shape[2]
    every_row = lax.all_gather(normed, "dp", axis=0, tiled=True)
    columns = lax.dynamic_slice_in_dim(every_row, dp_index * col_width, col_width, 1)
    gate_part = jnp.dot(columns, teacher_gate_up[0], preferred_element_type=jnp.float32)
    upper_part = jnp.dot(columns, teacher_gate_up[1], preferred_element_type=jnp.float32)
    both = lax.psum_scatter(
        jnp.concatenate([gate_part, upper_part], axis=1), "dp", scatter_dimension=0, tiled=True
    )
    hidden = (jax.nn.silu(both[:, :hidden_width]) * both[:, hidden_width:]).astype(jnp.bfloat16)
    partial_out = jnp.dot(
        lax.all_gather(hidden, "dp", axis=0, tiled=True),
        teacher_down,
        preferred_element_type=jnp.float32,
    )
    per_doc = lax.all_to_all(partial_out, "dp", split_axis=0, concat_axis=1, tiled=True)
    mlp_part = lax.psum_scatter(per_doc, "section", scatter_dimension=1, tiled=True)
    part_width = mlp_part.shape[1]
    teacher_states = (
        lax.dynamic_slice_in_dim(rows_f, section_index * part_width, part_width, 1) + mlp_part
    )
    final_gain = lax.dynamic_slice_in_dim(
        teacher_final_gain, section_index * part_width, part_width, 0
    )
    scaled = teacher_states * final_gain
    teacher_square = jnp.sum(scaled * scaled, -1)
    seq_len = student_states.shape[1]
    width = student_states.shape[2]
    tokens = layer_norm(student_states, student_ln_gain).reshape(local_docs * seq_len, width)
    pre_act = jnp.dot(tokens, student_w_in, preferred_element_type=jnp.float32)
    act = gelu_exact(pre_act).astype(jnp.bfloat16).reshape(local_docs, seq_len, -1)
    positions = jnp.arange(seq_len, dtype=jnp.int32)
    mask_f = (positions[None, :] < lengths[:, None]).astype(jnp.float32)
    mask_low = mask_f.astype(jnp.bfloat16)
    counts = lengths.astype(jnp.float32)[:, None]
    pooled_act = (
        jnp.einsum("bs,bsf->bf", mask_low, act, preferred_element_type=jnp.float32) / counts
    ).astype(jnp.bfloat16)
    pooled_x = (
        jnp.einsum("bs,bse->be", mask_low, student_states, preferred_element_type=jnp.float32)
        / counts
    )
    partial_emb = jnp.dot(pooled_act, student_w_out, preferred_element_type=jnp.float32)
    emb_sum, teacher_total = lax.psum((partial_emb, teacher_square), "section")
    student_raw = pooled_x + emb_sum
    norms = jnp.sqrt(jnp.sum(student_raw * student_raw, -1, keepdims=True) + 1e-06)
    student_normalized = student_raw / norms
    teacher_normalized = scaled / jnp.sqrt(teacher_total[:, None] + 1e-06)
    all_student_rows, every_teacher = (
        lax.all_gather(student_normalized, "dp", axis=0, tiled=True),
        lax.all_gather(teacher_normalized, "dp", axis=0, tiled=True),
    )
    first_row = dp_index * local_docs
    col_ids = jnp.arange(total_docs, dtype=jnp.int32)
    teacher_gram = lax.psum(
        jnp.dot(every_teacher, every_teacher.T, precision=highest_precision), "section"
    )
    teacher_logits = teacher_gram / teacher_softness
    student_logits = (
        jnp.dot(all_student_rows, all_student_rows.T, precision=highest_precision)
        / student_softness
    )
    gradient_list, loss = contrast(student_logits, teacher_logits, col_ids, col_ids)
    symmetric = (
        lax.dynamic_slice_in_dim(gradient_list, first_row, local_docs, 0)
        + lax.dynamic_slice_in_dim(gradient_list, first_row, local_docs, 1).T
    )
    normalized_gradient = (
        jnp.dot(symmetric, all_student_rows, precision=highest_precision) / student_softness
    )
    raw_grad = (
        normalized_gradient
        - student_normalized * jnp.sum(student_normalized * normalized_gradient, -1, keepdims=True)
    ) / norms
    raw_low = raw_grad.astype(jnp.bfloat16)
    grad_out_part = jnp.dot(pooled_act.T, raw_low, preferred_element_type=jnp.float32)
    pool_grad = lax.dot_general(
        raw_low, student_w_out, (((1,), (1,)), ((), ())), preferred_element_type=jnp.float32
    )
    scale = pool_grad / counts
    slope = gelu_slope(pre_act).reshape(local_docs, seq_len, -1)
    act_grad = (
        (slope * mask_f[:, :, None] * scale[:, None, :])
        .astype(jnp.bfloat16)
        .reshape(local_docs * seq_len, -1)
    )
    grad_w_in = lax.psum_scatter(
        lax.dot_general(
            tokens, act_grad, (((0,), (0,)), ((), ())), preferred_element_type=jnp.float32
        ),
        "dp",
        scatter_dimension=0,
        tiled=True,
    )
    grad_w_out = lax.psum_scatter(grad_out_part, "dp", scatter_dimension=0, tiled=True)
    return (loss, grad_w_in, grad_w_out, teacher_states)


def solution(mesh):
    placed = (
        P("dp", None, None),
        P("dp"),
        P(),
        P(None, "section"),
        P("section", None),
        P("dp", None),
        P(),
        P(None, "dp", "section"),
        P("section", "dp"),
        P(),
    )
    return jax.shard_map(
        on_device,
        mesh=mesh,
        in_specs=placed,
        out_specs=(P(), P("dp", "section"), P(("section", "dp"), None), P("dp", "section")),
        check_vma=False,
    )
```

profile of v0, /device:TPU:0, one launch (start us, length us, event | category | flops | bytes accessed | tf_op | source)
XLA Modules:
  0.0 472.4 jit_solution(15966292794362974652)
XLA Ops:
  7.2 1.1 multiply_reduce_fusion
  8.4 0.9 multiply_convert_fusion.5
  9.3 35.3 %all_gather.13 = bf16[64,4096]{1,0:T(8,128)(2,1)} all-gather(bf16[8,4096]{1,0:T(8,128)(2,1)S(1)} %multiply_convert_fusion.5), channel_id=1, replica_groups=mesh['section'=4,'dp'=8] {'dp'}, dimensions={0}, use_global_device_ids=true | all-gather | bytes 589824 | tf_op jit(solution)/shard_map/all_gather | solution.py:67
  44.6 2.6 fusion.12
  47.2 2.6 fusion.14
  49.8 1.3 pad_maximum_fusion
  51.1 4.7 convert_reduce_fusion
  55.8 5.7 %fusion.2 = f32[8,512]{1,0:T(8,128)S(1)} fusion(bf16[8,512,1024]{2,1,0:T(8,128)(2,1)} %param.10, f32[8,512]{1,0:T(8,128)S(1)} %broadcast_multiply_fusion), kind=kLoop, calls=%fused_computation.5 | loop fusion | flops 16773120 | bytes 8421376 | tf_op jit(solution)/shard_map/reduce_sum | solution.py:13
  61.6 0.7 fusion.27
  62.2 2.8 fusion.4
  65.1 1.2 fusion.30
  66.3 2.4 copy-done.1
  68.7 16.7 %fusion.8 = (f32[4096,1024]{1,0:T(8,128)}, bf16[4096,1024]{1,0:T(8,128)(2,1)}) fusion(bf16[4096,1024]{1,0:T(8,128)(2,1)S(1)} %bitcast.56, bf16[1024,1024]{1,0:T(8,128)(2,1)S(1)} %copy-done.8), kind=kOutput, calls=%fused_computation.11 | convolution fusion | flops 8636071936 | bytes 35651584 | tf_op jit(solution)/shard_map/dot_general | solution.py:94
  85.3 32.8 %reduce-scatter.5.cloned.1.call-done = f32[8,6144]{1,0:T(8,128)} async-done(((f32[64,6144]{1,0:T(8,128)}), f32[8,6144]{1,0:T(8,128)}) %reduce-scatter.5.cloned.1.call-update) | async-done | bytes 196624 | tf_op jit(solution)/shard_map/reduce_scatter | solution.py:71
  118.1 1.0 fusion.19
  119.1 31.0 %all_gather.14 = bf16[64,3072]{1,0:T(8,128)(2,1)S(1)} all-gather(bf16[8,3072]{1,0:T(8,128)(2,1)S(1)} %fusion.19), channel_id=1, replica_groups=mesh['section'=4,'dp'=8] {'dp'}, dimensions={0}, use_global_device_ids=true | all-gather | bytes 442368 | tf_op jit(solution)/shard_map/all_gather | solution.py:76
  150.1 1.3 convolution_bitcast_fusion
  151.4 3.4 all-to-all-start
  154.8 0.0 reduce-scatter.7.cloned.1.call-start
  154.9 4.6 fusion.28
  159.4 0.7 convert_element_type.50
  160.1 0.7 dynamic_slice.17
  160.8 1.3 all-to-all-done
  162.1 0.7 copy-done.3
  162.8 0.0 reduce-scatter.9.cloned.1.call-start
  162.8 2.0 fusion.40
  164.8 17.8 %reduce-scatter.7.cloned.1.call-done = f32[8,1024]{1,0:T(8,128)} async-done(((f32[8,4096]{1,0:T(8,128)}), f32[8,1024]{1,0:T(8,128)}) %reduce-scatter.7.cloned.1.call-update) | async-done | bytes 32784 | tf_op jit(solution)/shard_map/reduce_scatter | solution.py:81
  182.6 0.9 multiply_reduce_fusion.2
  183.5 5.8 %psum.22 = f32[8]{0:T(128)S(1)} all-reduce(f32[8]{0:T(128)S(1)} %get-tuple-element.6), channel_id=1, replica_groups=mesh['section'=4,'dp'=8] {'section'}, use_global_device_ids=true, to_apply=%region_9.10 | all-reduce | flops 8 | bytes 64 | tf_op jit(solution)/shard_map/psum | solution.py:108
  189.3 0.1 multiply_divide_fusion
  189.3 31.1 %all_gather.15 = f32[64,1024]{1,0:T(8,128)S(1)} all-gather(f32[8,1024]{1,0:T(8,128)S(1)} %multiply_divide_fusion), channel_id=1, replica_groups=mesh['section'=4,'dp'=8] {'dp'}, dimensions={0}, use_global_device_ids=true | all-gather | bytes 294912 | tf_op jit(solution)/shard_map/all_gather | solution.py:115
  220.5 0.4 fusion.42
  220.9 11.1 %all-reduce = (f32[8,1024]{1,0:T(8,128)S(1)}, f32[64,64]{0,1:T(8,128)S(1)}) all-reduce(f32[8,1024]{1,0:T(8,128)S(1)} %fusion.40, f32[64,64]{0,1:T(8,128)S(1)} %fusion.42), channel_id=1, replica_groups=mesh['section'=4,'dp'=8] {'section'}, use_global_device_ids=true, to_apply=%region_2.3 | all-reduce | flops 12288 | bytes 98304 | tf_op jit(solution)/shard_map/psum | solution.py:108
  232.0 0.2 multiply_reduce_fusion.3
  232.2 0.1 broadcast_divide_fusion
  232.3 30.9 %all_gather.12 = f32[64,1024]{1,0:T(8,128)S(1)} all-gather(f32[8,1024]{1,0:T(8,128)S(1)} %broadcast_divide_fusion), channel_id=1, replica_groups=mesh['section'=4,'dp'=8] {'dp'}, dimensions={0}, use_global_device_ids=true | all-gather | bytes 294912 | tf_op jit(solution)/shard_map/all_gather | solution.py:114
  263.2 0.4 fusion.24
  263.7 1.4 subtract_subtract_fusion
  265.1 0.7 constant_dynamic-slice_fusion
  265.8 0.8 copy.22
  266.6 0.4 multiply_reduce_fusion.1
  266.9 0.1 divide_convert_fusion
  267.0 2.2 convolution_divide_fusion
  269.3 16.3 %fusion.18 = f32[1024,1024]{1,0:T(8,128)} fusion(bf16[8,512,1024]{2,1,0:T(8,128)(2,1)} %copy-done.1, f32[8,512,1024]{2,1,0:T(8,128)} %bitcast.58, f32[8,1024]{1,0:T(8,128)S(1)} %convolution_divide_fusion, f32[8,512]{1,0:T(8,128)} %get-tuple-element.12), kind=kOutput, calls=%fused_computation.24 | convolution fusion | flops 8602517504 | bytes 29409280 | tf_op jit(solution)/shard_map/dot_general | solution.py:152
  285.6 0.0 reduce-scatter.11.cloned.1.call-start
  285.6 2.7 fusion.38
  288.4 85.4 %reduce-scatter.9.cloned.1.call-done = f32[128,1024]{1,0:T(8,128)} async-done(((f32[1024,1024]{1,0:T(8,128)}), f32[128,1024]{1,0:T(8,128)}) %reduce-scatter.9.cloned.1.call-update) | async-done | bytes 524304 | tf_op jit(solution)/shard_map/reduce_scatter | solution.py:151
  373.8 92.1 %reduce-scatter.11.cloned.1.call-done = f32[128,1024]{1,0:T(8,128)} async-done(((f32[1024,1024]{1,0:T(8,128)}), f32[128,1024]{1,0:T(8,128)}) %reduce-scatter.11.cloned.1.call-update) | async-done | bytes 524304 | tf_op jit(solution)/shard_map/reduce_scatter | solution.py:159
  (36 shorter events, 0.3 us)
Async XLA Ops:
  7.2 142.9 %copy-start = (bf16[3072,512]{1,0:T(8,128)(2,1)S(1)}, bf16[3072,512]{1,0:T(8,128)(2,1)}, u32[]{:S(2)}) copy-start(bf16[3072,512]{1,0:T(8,128)(2,1)} %param.18) | copy-start | bytes 9437188
  7.2 110.9 %reduce-scatter.5.cloned.1.call-start = ((), (), s32[]{:S(2)}) async-start(), calls=%async_computation.5 | async-start | bytes 1769472 | tf_op jit(solution)/shard_map/reduce_scatter | solution.py:71
  51.1 10.5 %copy-start.7 = (s32[8]{0:T(128)S(1)}, s32[8]{0:T(128)}, u32[]{:S(2)}) copy-start(s32[8]{0:T(128)} %param.11) | copy-start | bytes 100
  51.1 11.2 %slice-start = ((s8[8388608]{0:T(1024)(128)(4,1)}), s8[4194304]{0:T(1024)(128)(4,1)S(1)}, s32[]{:S(2)}) async-start(s8[8388608]{0:T(1024)(128)(4,1)} %bitcast.53), calls=%async_computation.9 | async-start | bytes 8388608
  51.1 11.2 %copy-start.6 = (f32[1024]{0:T(1024)S(1)}, f32[1024]{0:T(1024)}, u32[]{:S(2)}) copy-start(f32[1024]{0:T(1024)} %param.12) | copy-start | bytes 12292
  55.8 6.4 %slice-start.1 = ((s8[8388608]{0:T(1024)(128)(4,1)}), s8[4194304]{0:T(1024)(128)(4,1)S(1)}, s32[]{:S(2)}) async-start(s8[8388608]{0:T(1024)(128)(4,1)} %bitcast.53), calls=%async_computation.10 | async-start | bytes 8388608
  65.1 3.6 copy-start.1
  65.1 3.6 copy-start.8
  85.3 74.1 %copy-start.2 = (bf16[8,4096]{1,0:T(8,128)(2,1)S(1)}, bf16[8,4096]{1,0:T(8,128)(2,1)}, u32[]{:S(2)}) copy-start(bf16[8,4096]{1,0:T(8,128)(2,1)} %param.15) | copy-start | bytes 196612
  151.4 10.7 %all-to-all-start = ((f32[8,8,512]{2,1,0:T(8,128)}), f32[8,8,512]{2,1,0:T(8,128)S(1)}, u32[]{:S(2)}, u32[]{:S(2)}) async-start(f32[8,8,512]{2,1,0:T(8,128)} %convolution_bitcast_fusion), calls=%async_computation.1 | async-start | bytes 262144 | tf_op jit(solution)/shard_map/all_to_all | solution.py:80
  154.8 27.8 %reduce-scatter.7.cloned.1.call-start = ((), (), s32[]{:S(2)}) async-start(), calls=%async_computation.6 | async-start | bytes 163840 | tf_op jit(solution)/shard_map/reduce_scatter | solution.py:81
  162.1 0.7 copy-start.3
  162.8 211.0 %reduce-scatter.9.cloned.1.call-start = ((), (), s32[]{:S(2)}) async-start(), calls=%async_computation.7 | async-start | bytes 4718592 | tf_op jit(solution)/shard_map/reduce_scatter | solution.py:151
  183.5 102.1 %copy-start.4 = (f32[8,1024]{1,0:T(8,128)}, f32[8,1024]{1,0:T(8,128)S(1)}, u32[]{:S(2)}) copy-start(f32[8,1024]{1,0:T(8,128)S(1)} %get-tuple-element.7) | copy-start | bytes 98308
  232.0 31.7 %copy-start.5 = (f32[64,64]{0,1:T(8,128)}, f32[64,64]{0,1:T(8,128)S(1)}, u32[]{:S(2)}) copy-start(f32[64,64]{0,1:T(8,128)S(1)} %get-tuple-element.5) | copy-start | bytes 49156
  285.6 180.3 %reduce-scatter.11.cloned.1.call-start = ((), (), s32[]{:S(2)}) async-start(), calls=%async_computation.8 | async-start | bytes 4718592 | tf_op jit(solution)/shard_map/reduce_scatter | solution.py:159
Sparse Core Ops, SparseCore 0:
  51.2 66.8 reduce-scatter.4
  162.9 19.6 reduce-scatter.6
  285.7 88.0 reduce-scatter.8
  377.9 87.9 reduce-scatter.10
where the time goes:
time: 473 us; the launch traced here: 472 us
  waiting for transfers between devices  229 us (48%)
  blocking collectives  145 us (31%)
  matrix products  53.3 us (11%)
  other arithmetic  21.7 us (5%)
  between operations  14 us (3%)
  local copies, waits for them, and re-layouts  5.31 us (1%)
    reduce_scatter x1, waiting for transfers between devices, on_device(): lax.psum_scatter(grad_out_part, 'dp', scatter_dimension=0, tiled=True)  92.1 us
    reduce_scatter x1, waiting for transfers between devices, on_device(): lax.psum_scatter(lax.dot_general(tokens, act_grad, (((0,), (0,)), ((), ()...  85.4 us
    all_gather x1, blocking collectives, on_device(): every_row = lax.all_gather(normed, 'dp', axis=0, tiled=True)  35.3 us
    reduce_scatter x1, waiting for transfers between devices, on_device(): lax.psum_scatter(jnp.concatenate([gate_part, upper_part], axis=1), 'dp',...  32.8 us
    all_gather x1, blocking collectives, on_device(): lax.all_gather(teacher_normalized, 'dp', axis=0, tiled=True)  31.1 us
    all_gather x1, blocking collectives, on_device(): lax.all_gather(hidden, 'dp', axis=0, tiled=True)  31 us
    all_gather x1, blocking collectives, on_device(): lax.all_gather(student_normalized, 'dp', axis=0, tiled=True)  30.9 us
    reduce_scatter x1, waiting for transfers between devices, on_device(): lax.psum_scatter(per_doc, 'section', scatter_dimension=1, tiled=True)  17.8 us
  transfers between devices with their start and end apart: 5, of which 5 were waited for; matrix products, arithmetic and copies ran while one was open for 9% of the time, Pallas kernels for 0%

commit v1 on v0

v1 whole, which is shorter than its diff:
```python
import jax
import jax.numpy as jnp
from jax import lax
from jax.sharding import PartitionSpec as P

student_softness = 0.05
teacher_softness = 0.02


def layer_norm(states, gain):
    values = states.astype(jnp.float32)
    center = values - jnp.mean(values, -1, keepdims=True)
    spread = jnp.mean(center * center, -1, keepdims=True)
    return (center * lax.rsqrt(spread + 1e-05) * gain).astype(jnp.bfloat16)


def gelu_exact(value):
    return 0.5 * value * (1.0 + jax.scipy.special.erf(value * 0.7071067811865476))


def gelu_slope(value):
    return (
        0.5 * (1.0 + jax.scipy.special.erf(value * 0.7071067811865476))
        + value * jnp.exp(-0.5 * value * value) * 0.3989422804014327
    )


def contrast(student_logits, teacher_logits, row_ids, col_ids):
    keep = row_ids[:, None] != col_ids[None, :]
    partner = (row_ids + 1 - 2 * (row_ids % 2))[:, None] == col_ids[None, :]
    s_exp = jnp.where(keep, jnp.exp(student_logits), 0.0)
    t_exp = jnp.where(keep, jnp.exp(teacher_logits), 0.0)
    s_total = jnp.sum(s_exp, -1, keepdims=True)
    t_total = jnp.sum(t_exp, -1, keepdims=True)
    s_prob = s_exp / s_total
    t_prob = t_exp / t_total
    s_log = student_logits - jnp.log(s_total)
    t_log = teacher_logits - jnp.log(t_total)
    terms = jnp.where(partner, -s_log, 0.0) + jnp.where(keep, t_prob * (t_log - s_log), 0.0)
    gradient_list = 2.0 * s_prob - partner.astype(jnp.float32) - t_prob
    return (gradient_list, jnp.sum(terms))


def exchange(blocks, axis):
    return lax.all_to_all(blocks, axis, 0, 0, tiled=True)


def gather(value, axis):
    count = lax.axis_size(axis)
    return exchange(jnp.broadcast_to(value[None], (count,) + value.shape), axis)


def on_device(
    student_states,
    lengths,
    student_ln_gain,
    student_w_in,
    student_w_out,
    teacher_rows,
    teacher_mlp_gain,
    teacher_gate_up,
    teacher_down,
    teacher_final_gain,
):
    f32, bf16 = jnp.float32, jnp.bfloat16
    dp_count = lax.axis_size("dp")
    section_count = lax.axis_size("section")
    dp_index = lax.axis_index("dp")
    section_index = lax.axis_index("section")
    local_docs = teacher_rows.shape[0]
    total_docs = local_docs * dp_count
    highest = lax.Precision.HIGHEST
    col_width = teacher_gate_up.shape[1]
    hidden_width = teacher_gate_up.shape[2]

    rows_f = teacher_rows.astype(f32)
    inverse = lax.rsqrt(jnp.mean(rows_f * rows_f, -1, keepdims=True) + 1e-06)
    normed = (rows_f * inverse * teacher_mlp_gain).astype(bf16)
    both_rows = jnp.stack([normed, teacher_rows]).reshape(2, local_docs, dp_count, col_width)
    columns = exchange(both_rows.transpose(2, 0, 1, 3), "dp")
    normed_columns = columns[:, 0].reshape(total_docs, col_width)
    row_columns = columns[:, 1].reshape(total_docs, col_width).astype(f32)
    gate_part = jnp.dot(normed_columns, teacher_gate_up[0], preferred_element_type=f32)
    upper_part = jnp.dot(normed_columns, teacher_gate_up[1], preferred_element_type=f32)
    parts = jnp.concatenate([gate_part.astype(bf16), upper_part.astype(bf16)], axis=1)
    parts = exchange(parts.reshape(dp_count, local_docs, 2 * hidden_width), "dp")
    both = jnp.sum(parts.astype(f32), 0)
    hidden = (jax.nn.silu(both[:, :hidden_width]) * both[:, hidden_width:]).astype(bf16)
    every_hidden = gather(hidden, "dp").reshape(total_docs, hidden_width)
    partial_out = jnp.dot(every_hidden, teacher_down, preferred_element_type=f32)
    mlp_part = jnp.sum(gather(partial_out.astype(bf16), "section").astype(f32), 0)
    states_block = row_columns + mlp_part
    final_gain = lax.dynamic_slice_in_dim(teacher_final_gain, dp_index * col_width, col_width, 0)
    scaled = states_block * final_gain
    gram_part = lax.dot_general(
        scaled, scaled, (((1,), (1,)), ((), ())), precision=highest, preferred_element_type=f32
    )
    gram = jnp.sum(gather(gram_part, "dp"), 0)
    squares = jnp.diagonal(gram)
    teacher_norms = jnp.sqrt(squares + 1e-06)
    teacher_logits = gram / (teacher_norms[:, None] * teacher_norms[None, :]) / teacher_softness
    by_block = exchange(states_block.reshape(dp_count, local_docs, col_width), "dp")
    per_section = dp_count // section_count
    own_blocks = lax.dynamic_slice_in_dim(by_block, section_index * per_section, per_section, 0)
    teacher_states = own_blocks.transpose(1, 0, 2).reshape(local_docs, per_section * col_width)

    seq_len = student_states.shape[1]
    width = student_states.shape[2]
    tokens = layer_norm(student_states, student_ln_gain).reshape(local_docs * seq_len, width)
    pre_act = jnp.dot(tokens, student_w_in, preferred_element_type=f32)
    act = gelu_exact(pre_act).astype(bf16).reshape(local_docs, seq_len, -1)
    positions = jnp.arange(seq_len, dtype=jnp.int32)
    mask_f = (positions[None, :] < lengths[:, None]).astype(f32)
    mask_low = mask_f.astype(bf16)
    counts = lengths.astype(f32)[:, None]
    pooled_act = (
        jnp.einsum("bs,bsf->bf", mask_low, act, preferred_element_type=f32) / counts
    ).astype(bf16)
    pooled_x = (
        jnp.einsum("bs,bse->be", mask_low, student_states, preferred_element_type=f32) / counts
    )
    partial_emb = jnp.dot(pooled_act, student_w_out, preferred_element_type=f32)
    student_raw = pooled_x + jnp.sum(gather(partial_emb, "section"), 0)
    all_raw = gather(student_raw, "dp").reshape(total_docs, width)
    norms = jnp.sqrt(jnp.sum(all_raw * all_raw, -1, keepdims=True) + 1e-06)
    unit = all_raw / norms
    student_logits = (
        lax.dot_general(
            unit, unit, (((1,), (1,)), ((), ())), precision=highest, preferred_element_type=f32
        )
        / student_softness
    )
    ids = jnp.arange(total_docs, dtype=jnp.int32)
    gradient_list, loss = contrast(student_logits, teacher_logits, ids, ids)
    unit_grad = (
        jnp.dot(gradient_list + gradient_list.T, unit, precision=highest) / student_softness
    )
    raw_grad = (unit_grad - unit * jnp.sum(unit * unit_grad, -1, keepdims=True)) / norms
    every_low = raw_grad.astype(bf16)
    raw_low = lax.dynamic_slice_in_dim(every_low, dp_index * local_docs, local_docs, 0)

    pooled_columns = exchange(
        pooled_act.reshape(local_docs, dp_count, -1).transpose(1, 0, 2), "dp"
    ).reshape(total_docs, -1)
    grad_w_out = lax.dot_general(
        pooled_columns, every_low, (((0,), (0,)), ((), ())), preferred_element_type=f32
    )

    pool_grad = lax.dot_general(
        raw_low, student_w_out, (((1,), (1,)), ((), ())), preferred_element_type=f32
    )
    scale = pool_grad / counts
    slope = gelu_slope(pre_act).reshape(local_docs, seq_len, -1)
    act_grad = (
        (slope * mask_f[:, :, None] * scale[:, None, :])
        .astype(bf16)
        .reshape(local_docs * seq_len, -1)
    )
    grad_part = lax.dot_general(
        tokens, act_grad, (((0,), (0,)), ((), ())), preferred_element_type=f32
    )
    grad_part = grad_part.astype(bf16).reshape(dp_count, width // dp_count, -1)
    grad_w_in = jnp.sum(exchange(grad_part, "dp").astype(f32), 0)
    return (loss, grad_w_in, grad_w_out, teacher_states)


def solution(mesh):
    placed = (
        P("dp", None, None),
        P("dp"),
        P(),
        P(None, "section"),
        P("section", None),
        P("dp", None),
        P(),
        P(None, "dp", "section"),
        P("section", "dp"),
        P(),
    )
    return jax.shard_map(
        on_device,
        mesh=mesh,
        in_specs=placed,
        out_specs=(P(), P("dp", "section"), P(("section", "dp"), None), P("dp", "section")),
        check_vma=False,
    )
```

time: 473 us -> 233 us (0.49)
  blocking collectives: 145 us -> 0 us
  waiting for transfers between devices: 229 us -> 86.7 us
  starting transfers between devices: 3.54 us -> 48.3 us
  between operations: 14 us -> 0.95 us
  other arithmetic: 21.7 us -> 30.3 us
  local copies, waits for them, and re-layouts: 5.31 us -> 11.9 us
    reduce_scatter x4 -> x0, waiting for transfers between devices: 228 us -> none  [the longest x1 92.1 us: on_device(): lax.psum_scatter(grad_out_part, 'dp', scatter_dimension=0, tiled=True)]
    all_gather x4 -> x0, blocking collectives: 128 us -> none  [the longest x1 35.3 us: on_device(): every_row = lax.all_gather(normed, 'dp', axis=0, tiled=True)]
    all_to_all x1 -> x10, waiting for transfers between devices: 1.28 us -> 86.7 us  [exchange(): return lax.all_to_all(blocks, axis, 0, 0, tiled=True)]
    all_to_all x1 -> x10, starting transfers between devices: 3.37 us -> 48.3 us  [exchange(): return lax.all_to_all(blocks, axis, 0, 0, tiled=True)]
    psum x2 -> x0, blocking collectives: 16.9 us -> none  [on_device(): emb_sum, teacher_total = lax.psum((partial_emb, teacher_square), 'section')]
    reduce_sum x2 -> x8, other arithmetic: 1.09 us -> 7.36 us  [the longest x1 2.79 us: on_device(): grad_w_in = jnp.sum(exchange(grad_part, 'dp').astype(f32), 0)]
  transfers between devices with their start and end apart: 5 -> 10, of which waited for: 5 -> 6; matrix products, arithmetic and copies ran while one was open for 9% -> 34% of each run, Pallas kernels for 0% -> 0%
where the time goes in v1:
time: 233 us; the launch traced here: 231 us
  waiting for transfers between devices  86.7 us (37%)
  matrix products  53.1 us (23%)
  starting transfers between devices  48.3 us (21%)
  other arithmetic  30.3 us (13%)
  local copies, waits for them, and re-layouts  11.9 us (5%)
    all_to_all x10, waiting for transfers between devices, exchange(): return lax.all_to_all(blocks, axis, 0, 0, tiled=True)  86.7 us
    all_to_all x10, starting transfers between devices, exchange(): return lax.all_to_all(blocks, axis, 0, 0, tiled=True)  48.3 us
    dot_general x1, matrix products, on_device(): pre_act = jnp.dot(tokens, student_w_in, preferred_element_type=f32)  17 us
    dot_general x1, matrix products, on_device(): lax.dot_general(tokens, act_grad, (((0,), (0,)), ((), ())), preferred_ele...  16.1 us
    unnamed x28, local copies, waits for them, and re-layouts  5.22 us
  transfers between devices with their start and end apart: 10, of which 6 were waited for; matrix products, arithmetic and copies ran while one was open for 34% of the time, Pallas kernels for 0%

profile of v1, /device:TPU:0, one launch (start us, length us, event | category | flops | bytes accessed | tf_op | source)
XLA Modules:
  0.0 231.2 jit_solution(12184311341276939278)
XLA Ops:
  0.6 1.1 fusion.19
  1.8 0.9 fusion.21
  2.7 1.5 maximum_bitcast_fusion.1
  4.2 7.3 %all-to-all-start.2 = ((bf16[8,2,8,512]{3,2,1,0:T(8,128)(2,1)}), bf16[8,2,8,512]{3,2,1,0:T(8,128)(2,1)S(1)}, u32[]{:S(2)}, u32[]{:S(2)}) async-start(bf16[8,2,8,512]{3,2,1,0:T(8,128)(2,1)} %maximum_bitcast_fusion.1), calls=%async_computation.2 | async-start | bytes 262144 | tf_op jit(solution)/shard_map/all_to_all | solution.py:45
  11.6 1.5 fusion.73
  13.0 1.0 convert_element_type.80
  14.1 4.6 %convert_reduce_fusion = f32[8,512]{1,0:T(8,128)S(1)} fusion(bf16[8,512,1024]{2,1,0:T(8,128)(2,1)} %param.10), kind=kLoop, calls=%fused_computation.3 | loop fusion | flops 8384512 | bytes 8404992 | tf_op jit(solution)/shard_map/reduce_sum | solution.py:12
  18.7 2.8 %fusion.2 = f32[8,512]{1,0:T(8,128)S(1)} fusion(bf16[8,512,1024]{2,1,0:T(8,128)(2,1)S(1)} %copy-done.1, f32[8,512]{1,0:T(8,128)S(1)} %broadcast_multiply_fusion), kind=kLoop, calls=%fused_computation.6 | loop fusion | flops 16773120 | bytes 8421376 | tf_op jit(solution)/shard_map/reduce_sum | solution.py:13
  21.5 2.8 %fusion.4 = bf16[8,512,1024]{2,1,0:T(8,128)(2,1)S(1)} fusion(bf16[8,512,1024]{2,1,0:T(8,128)(2,1)S(1)} %copy-done.1, f32[1024]{0:T(1024)S(1)} %copy-done.9, f32[8,512]{1,0:T(8,128)S(1)} %add_rsqrt_fusion, f32[8,512]{1,0:T(8,128)S(1)} %broadcast_multiply_fusion), kind=kLoop, calls=%fused_computation.8 | loop fusion | flops 20971520 | bytes 16814080 | tf_op jit(solution)/shard_map/convert_element_type | solution.py:14
  24.4 17.0 %fusion.8 = (f32[4096,1024]{1,0:T(8,128)}, bf16[4096,1024]{1,0:T(8,128)(2,1)S(1)}) fusion(bf16[4096,1024]{1,0:T(8,128)(2,1)S(1)} %bitcast.111, bf16[1024,1024]{1,0:T(8,128)(2,1)S(1)} %copy-done.12), kind=kOutput, calls=%fused_computation.12 | convolution fusion | flops 8636071936 | bytes 35651584 | tf_op jit(solution)/shard_map/dot_general | solution.py:110
  41.4 1.2 fusion.74
  44.1 3.3 %all-to-all-start = ((f32[4,8,1024]{2,1,0:T(8,128)}), f32[4,8,1024]{2,1,0:T(8,128)S(1)}, u32[]{:S(2)}, u32[]{:S(2)}) async-start(f32[4,8,1024]{2,1,0:T(8,128)} %broadcast_in_dim.20), calls=%async_computation | async-start | bytes 262144 | tf_op jit(solution)/shard_map/all_to_all | solution.py:45
  47.5 2.6 %convolution_convert_fusion = bf16[64,3072]{1,0:T(8,128)(2,1)S(1)} fusion(bf16[2,512,3072]{2,1,0:T(8,128)(2,1)} %param.17, bf16[8,2,8,512]{3,2,1,0:T(8,128)(2,1)S(1)} %all-to-all-done.2), kind=kOutput, calls=%fused_computation.21 | convolution fusion | flops 201523200 | bytes 3604480 | tf_op jit(solution)/shard_map/dot_general | solution.py:84
  50.0 2.6 %convolution_convert_fusion.1 = bf16[64,3072]{1,0:T(8,128)(2,1)S(1)} fusion(bf16[2,512,3072]{2,1,0:T(8,128)(2,1)} %param.17, bf16[8,2,8,512]{3,2,1,0:T(8,128)(2,1)S(1)} %all-to-all-done.2), kind=kOutput, calls=%fused_computation.22 | convolution fusion | flops 201523200 | bytes 3604480 | tf_op jit(solution)/shard_map/dot_general | solution.py:83
  52.6 0.9 maximum_bitcast_fusion
  53.5 6.0 %all-to-all-start.3 = ((bf16[8,8,6144]{2,1,0:T(8,128)(2,1)}), bf16[8,8,6144]{2,1,0:T(8,128)(2,1)}, u32[]{:S(2)}, u32[]{:S(2)}) async-start(bf16[8,8,6144]{2,1,0:T(8,128)(2,1)} %maximum_bitcast_fusion), calls=%async_computation.3 | async-start | bytes 1572864 | tf_op jit(solution)/shard_map/all_to_all | solution.py:45
  59.5 4.6 %fusion.76 = f32[8,1,1024]{2,1,0:T(1,128)S(1)} fusion(bf16[8,512,1024]{2,1,0:T(8,128)(2,1)} %param.10, bf16[8,512,1]{1,0,2:T(8,128)(2,1)S(1)} %get-tuple-element.7), kind=kOutput, calls=%fused_computation.113 | convolution fusion | flops 8388608 | bytes 8429568 | tf_op jit(solution)/shard_map/bs,bse->be/dot_general | solution.py:120
  64.2 16.2 %all-to-all-done.3 = bf16[8,8,6144]{2,1,0:T(8,128)(2,1)} async-done(((bf16[8,8,6144]{2,1,0:T(8,128)(2,1)}), bf16[8,8,6144]{2,1,0:T(8,128)(2,1)}, u32[]{:S(2)}, u32[]{:S(2)}) %all-to-all-start.3) | async-done | bytes 786464 | tf_op jit(solution)/shard_map/all_to_all | solution.py:45
  81.1 3.6 %all-to-all-start.1 = ((f32[8,8,1024]{2,1,0:T(8,128)}), f32[8,8,1024]{2,1,0:T(8,128)S(1)}, u32[]{:S(2)}, u32[]{:S(2)}) async-start(f32[8,8,1024]{2,1,0:T(8,128)} %broadcast_in_dim.21), calls=%async_computation.1 | async-start | bytes 524288 | tf_op jit(solution)/shard_map/all_to_all | solution.py:45
  84.8 1.3 convert_reduce_fusion.2
  86.1 7.8 %all-to-all-done.1 = f32[8,8,1024]{2,1,0:T(8,128)S(1)} async-done(((f32[8,8,1024]{2,1,0:T(8,128)}), f32[8,8,1024]{2,1,0:T(8,128)S(1)}, u32[]{:S(2)}, u32[]{:S(2)}) %all-to-all-start.1) | async-done | bytes 262176 | tf_op jit(solution)/shard_map/all_to_all | solution.py:45
  93.9 0.8 broadcast_in_dim.23
  94.6 4.1 %all-to-all-start.4 = ((bf16[8,8,3072]{2,1,0:T(8,128)(2,1)}), bf16[8,8,3072]{2,1,0:T(8,128)(2,1)}, u32[]{:S(2)}, u32[]{:S(2)}) async-start(bf16[8,8,3072]{2,1,0:T(8,128)(2,1)} %broadcast_in_dim.23), calls=%async_computation.4 | async-start | bytes 786432 | tf_op jit(solution)/shard_map/all_to_all | solution.py:45
  98.8 0.8 dynamic_slice.9
  100.8 8.8 %all-to-all-done.4 = bf16[8,8,3072]{2,1,0:T(8,128)(2,1)} async-done(((bf16[8,8,3072]{2,1,0:T(8,128)(2,1)}), bf16[8,8,3072]{2,1,0:T(8,128)(2,1)}, u32[]{:S(2)}, u32[]{:S(2)}) %all-to-all-start.4) | async-done | bytes 393248 | tf_op jit(solution)/shard_map/all_to_all | solution.py:45
  109.7 1.6 convolution_convert_fusion.2
  111.3 0.7 broadcast_in_dim.24
  112.0 4.1 %all-to-all-start.5 = ((bf16[4,64,512]{2,1,0:T(8,128)(2,1)}), bf16[4,64,512]{2,1,0:T(8,128)(2,1)}, u32[]{:S(2)}, u32[]{:S(2)}) async-start(bf16[4,64,512]{2,1,0:T(8,128)(2,1)} %broadcast_in_dim.24), calls=%async_computation.5 | async-start | bytes 524288 | tf_op jit(solution)/shard_map/all_to_all | solution.py:45
  117.4 4.8 %all-to-all-done.5 = bf16[4,64,512]{2,1,0:T(8,128)(2,1)} async-done(((bf16[4,64,512]{2,1,0:T(8,128)(2,1)}), bf16[4,64,512]{2,1,0:T(8,128)(2,1)}, u32[]{:S(2)}, u32[]{:S(2)}) %all-to-all-start.5) | async-done | bytes 262176 | tf_op jit(solution)/shard_map/all_to_all | solution.py:45
  122.2 1.0 convert_reduce_fusion.3
  123.8 1.2 fusion.24
  125.7 1.8 reshape.191
  127.5 4.0 %all-to-all-start.6 = ((f32[8,1,4096]{2,1,0:T(1,128)}), f32[8,1,4096]{2,1,0:T(1,128)}, u32[]{:S(2)}, u32[]{:S(2)}) async-start(f32[8,1,4096]{2,1,0:T(1,128)} %reshape.191), calls=%async_computation.6 | async-start | bytes 262144 | tf_op jit(solution)/shard_map/all_to_all | solution.py:45
  131.5 1.6 fusion.26
  133.1 5.8 %all-to-all-done.6 = f32[8,1,4096]{2,1,0:T(1,128)} async-done(((f32[8,1,4096]{2,1,0:T(1,128)}), f32[8,1,4096]{2,1,0:T(1,128)}, u32[]{:S(2)}, u32[]{:S(2)}) %all-to-all-start.6) | async-done | bytes 131104 | tf_op jit(solution)/shard_map/all_to_all | solution.py:45
  138.9 4.1 %all-to-all-start.8 = ((bf16[8,8,128]{2,1,0:T(8,128)(2,1)}), bf16[8,8,128]{2,1,0:T(8,128)(2,1)}, u32[]{:S(2)}, u32[]{:S(2)}) async-start(bf16[8,8,128]{2,1,0:T(8,128)(2,1)} %fusion.97), calls=%async_computation.8 | async-start | bytes 32768 | tf_op jit(solution)/shard_map/all_to_all | solution.py:45
  143.5 2.5 %reduce.1 = f32[8,4096]{1,0:T(8,128)} reduce(f32[8,1,4096]{2,1,0:T(1,128)} %all-to-all-done.6, f32[]{:T(128)} %broadcast.195), dimensions={1}, to_apply=%all_to_all.36.reduce_sub_computation | reduce | bytes 262148 | tf_op jit(solution)/shard_map/all_to_all | solution.py:45
  146.0 1.7 reshape.192
  147.7 1.0 reduce_sum.132
  148.8 0.8 gather_fusion
  149.7 1.4 multiply_reduce_fusion
  151.9 2.2 convolution_divide_fusion
  154.2 5.7 %all-to-all-start.9 = ((f32[8,8,512]{2,1,0:T(8,128)}), f32[8,8,512]{2,1,0:T(8,128)S(1)}, u32[]{:S(2)}, u32[]{:S(2)}) async-start(f32[8,8,512]{2,1,0:T(8,128)} %fusion.26), calls=%async_computation.9 | async-start | bytes 262144 | tf_op jit(solution)/shard_map/all_to_all | solution.py:45
  159.9 16.1 %bitcast_convert_fusion = bf16[1024,1024]{1,0:T(8,128)(2,1)} fusion(bf16[8,512,1024]{2,1,0:T(8,128)(2,1)} %copy-done.2, f32[8,512,1024]{2,1,0:T(8,128)} %bitcast.116, f32[8,1024]{1,0:T(8,128)S(1)} %convolution_divide_fusion, f32[8,512]{1,0:T(8,128)} %get-tuple-element.6), kind=kOutput, calls=%fused_computation.19 | convolution fusion | flops 8603566080 | bytes 27312128 | tf_op jit(solution)/shard_map/dot_general | solution.py:159
  176.0 6.0 %all-to-all-start.7 = ((bf16[8,128,1024]{2,1,0:T(8,128)(2,1)}), bf16[8,128,1024]{2,1,0:T(8,128)(2,1)}, u32[]{:S(2)}, u32[]{:S(2)}) async-start(bf16[8,128,1024]{2,1,0:T(8,128)(2,1)} %bitcast.112), calls=%async_computation.7 | async-start | bytes 4194304 | tf_op jit(solution)/shard_map/all_to_all | solution.py:45
  183.4 1.8 fusion.59
  185.1 43.3 %all-to-all-done.7 = bf16[8,128,1024]{2,1,0:T(8,128)(2,1)} async-done(((bf16[8,128,1024]{2,1,0:T(8,128)(2,1)}), bf16[8,128,1024]{2,1,0:T(8,128)(2,1)}, u32[]{:S(2)}, u32[]{:S(2)}) %all-to-all-start.7) | async-done | bytes 2097184 | tf_op jit(solution)/shard_map/all_to_all | solution.py:45
  228.4 2.8 %convert_reduce_fusion.1 = f32[128,1024]{1,0:T(8,128)} fusion(bf16[8,128,1024]{2,1,0:T(8,128)(2,1)} %all-to-all-done.7), kind=kLoop, calls=%fused_computation.20 | loop fusion | flops 1966080 | bytes 2621440 | tf_op jit(solution)/shard_map/reduce_sum | solution.py:163
  (60 shorter events, 9.2 us)
Async XLA Ops:
  0.6 109.0 %copy-start = (bf16[3072,512]{1,0:T(8,128)(2,1)S(1)}, bf16[3072,512]{1,0:T(8,128)(2,1)}, u32[]{:S(2)}) copy-start(bf16[3072,512]{1,0:T(8,128)(2,1)} %param.18) | copy-start | bytes 9437188
  4.2 39.2 %all-to-all-start.2 = ((bf16[8,2,8,512]{3,2,1,0:T(8,128)(2,1)}), bf16[8,2,8,512]{3,2,1,0:T(8,128)(2,1)S(1)}, u32[]{:S(2)}, u32[]{:S(2)}) async-start(bf16[8,2,8,512]{3,2,1,0:T(8,128)(2,1)} %maximum_bitcast_fusion.1), calls=%async_computation.2 | async-start | bytes 262144 | tf_op jit(solution)/shard_map/all_to_all | solution.py:45
  11.5 7.1 %copy-start.1 = (bf16[8,512,1024]{2,1,0:T(8,128)(2,1)S(1)}, bf16[8,512,1024]{2,1,0:T(8,128)(2,1)}, u32[]{:S(2)}) copy-start(bf16[8,512,1024]{2,1,0:T(8,128)(2,1)} %param.10) | copy-start | bytes 25165828
  14.1 7.4 %copy-start.9 = (f32[1024]{0:T(1024)S(1)}, f32[1024]{0:T(1024)}, u32[]{:S(2)}) copy-start(f32[1024]{0:T(1024)} %param.12) | copy-start | bytes 12292
  21.5 2.8 %copy-start.12 = (bf16[1024,1024]{1,0:T(8,128)(2,1)S(1)}, bf16[1024,1024]{1,0:T(8,128)(2,1)}, u32[]{:S(2)}) copy-start(bf16[1024,1024]{1,0:T(8,128)(2,1)} %param.13) | copy-start | bytes 6291460
  24.3 17.1 %copy-start.2 = (bf16[8,512,1024]{2,1,0:T(8,128)(2,1)}, bf16[8,512,1024]{2,1,0:T(8,128)(2,1)S(1)}, u32[]{:S(2)}) copy-start(bf16[8,512,1024]{2,1,0:T(8,128)(2,1)S(1)} %fusion.4) | copy-start | bytes 25165828
  41.4 1.6 copy-start.3
  43.4 20.7 %copy-start.7 = (bf16[8,2,8,512]{3,2,1,0:T(8,128)(2,1)}, bf16[8,2,8,512]{3,2,1,0:T(8,128)(2,1)S(1)}, u32[]{:S(2)}) copy-start(bf16[8,2,8,512]{3,2,1,0:T(8,128)(2,1)S(1)} %all-to-all-done.2) | copy-start | bytes 393220
  44.1 9.4 %all-to-all-start = ((f32[4,8,1024]{2,1,0:T(8,128)}), f32[4,8,1024]{2,1,0:T(8,128)S(1)}, u32[]{:S(2)}, u32[]{:S(2)}) async-start(f32[4,8,1024]{2,1,0:T(8,128)} %broadcast_in_dim.20), calls=%async_computation | async-start | bytes 262144 | tf_op jit(solution)/shard_map/all_to_all | solution.py:45
  53.5 26.9 %all-to-all-start.3 = ((bf16[8,8,6144]{2,1,0:T(8,128)(2,1)}), bf16[8,8,6144]{2,1,0:T(8,128)(2,1)}, u32[]{:S(2)}, u32[]{:S(2)}) async-start(bf16[8,8,6144]{2,1,0:T(8,128)(2,1)} %maximum_bitcast_fusion), calls=%async_computation.3 | async-start | bytes 1572864 | tf_op jit(solution)/shard_map/all_to_all | solution.py:45
  81.1 12.8 %all-to-all-start.1 = ((f32[8,8,1024]{2,1,0:T(8,128)}), f32[8,8,1024]{2,1,0:T(8,128)S(1)}, u32[]{:S(2)}, u32[]{:S(2)}) async-start(f32[8,8,1024]{2,1,0:T(8,128)} %broadcast_in_dim.21), calls=%async_computation.1 | async-start | bytes 524288 | tf_op jit(solution)/shard_map/all_to_all | solution.py:45
  94.6 15.0 %all-to-all-start.4 = ((bf16[8,8,3072]{2,1,0:T(8,128)(2,1)}), bf16[8,8,3072]{2,1,0:T(8,128)(2,1)}, u32[]{:S(2)}, u32[]{:S(2)}) async-start(bf16[8,8,3072]{2,1,0:T(8,128)(2,1)} %broadcast_in_dim.23), calls=%async_computation.4 | async-start | bytes 786432 | tf_op jit(solution)/shard_map/all_to_all | solution.py:45
  112.0 10.1 %all-to-all-start.5 = ((bf16[4,64,512]{2,1,0:T(8,128)(2,1)}), bf16[4,64,512]{2,1,0:T(8,128)(2,1)}, u32[]{:S(2)}, u32[]{:S(2)}) async-start(bf16[4,64,512]{2,1,0:T(8,128)(2,1)} %broadcast_in_dim.24), calls=%async_computation.5 | async-start | bytes 524288 | tf_op jit(solution)/shard_map/all_to_all | solution.py:45
  116.8 29.2 %copy-start.8 = (f32[64,64]{0,1:T(8,128)}, f32[64,64]{0,1:T(8,128)S(1)}, u32[]{:S(2)}) copy-start(f32[64,64]{0,1:T(8,128)S(1)} %copy.33) | copy-start | bytes 49156
  123.2 0.6 copy-start.4
  127.5 11.4 %all-to-all-start.6 = ((f32[8,1,4096]{2,1,0:T(1,128)}), f32[8,1,4096]{2,1,0:T(1,128)}, u32[]{:S(2)}, u32[]{:S(2)}) async-start(f32[8,1,4096]{2,1,0:T(1,128)} %reshape.191), calls=%async_computation.6 | async-start | bytes 262144 | tf_op jit(solution)/shard_map/all_to_all | solution.py:45
  138.9 15.3 %all-to-all-start.8 = ((bf16[8,8,128]{2,1,0:T(8,128)(2,1)}), bf16[8,8,128]{2,1,0:T(8,128)(2,1)}, u32[]{:S(2)}, u32[]{:S(2)}) async-start(bf16[8,8,128]{2,1,0:T(8,128)(2,1)} %fusion.97), calls=%async_computation.8 | async-start | bytes 32768 | tf_op jit(solution)/shard_map/all_to_all | solution.py:45
  151.3 0.7 copy-start.5
  154.2 21.8 %all-to-all-start.9 = ((f32[8,8,512]{2,1,0:T(8,128)}), f32[8,8,512]{2,1,0:T(8,128)S(1)}, u32[]{:S(2)}, u32[]{:S(2)}) async-start(f32[8,8,512]{2,1,0:T(8,128)} %fusion.26), calls=%async_computation.9 | async-start | bytes 262144 | tf_op jit(solution)/shard_map/all_to_all | solution.py:45
  159.9 22.1 %copy-start.11 = (f32[64]{0:T(128)S(1)}, f32[64]{0:T(128)}, u32[]{:S(2)}) copy-start(f32[64]{0:T(128)} %fusion.55) | copy-start | bytes 772
  159.9 22.7 %copy-start.10 = (s32[64]{0:T(128)S(1)}, s32[64]{0:T(128)}, u32[]{:S(2)}) copy-start(s32[64]{0:T(128)} %fusion.78) | copy-start | bytes 772
  159.9 23.4 %copy-start.6 = (bf16[64,1024]{1,0:T(8,128)(2,1)S(1)}, bf16[64,1024]{1,0:T(8,128)(2,1)}, u32[]{:S(2)}) copy-start(bf16[64,1024]{1,0:T(8,128)(2,1)} %copy-done.5) | copy-start | bytes 393220
  176.0 52.4 %all-to-all-start.7 = ((bf16[8,128,1024]{2,1,0:T(8,128)(2,1)}), bf16[8,128,1024]{2,1,0:T(8,128)(2,1)}, u32[]{:S(2)}, u32[]{:S(2)}) async-start(bf16[8,128,1024]{2,1,0:T(8,128)(2,1)} %bitcast.112), calls=%async_computation.7 | async-start | bytes 4194304 | tf_op jit(solution)/shard_map/all_to_all | solution.py:45

commit v2 on v1

v2 whole, which is shorter than its diff:
```python
import functools

import jax
import jax.numpy as jnp
from jax import lax
from jax.experimental import pallas as pl
from jax.experimental.pallas import tpu as pltpu
from jax.sharding import PartitionSpec as P


student_softness = 0.05
teacher_softness = 0.02
f32 = jnp.float32
bf16 = jnp.bfloat16
highest = lax.Precision.HIGHEST


def exchange(blocks, axis):
    return lax.all_to_all(blocks, axis, 0, 0, tiled=True)


def swap(value, axis, bit):
    members = lax.axis_size(axis)
    return lax.ppermute(value, axis, [(i, i ^ (1 << bit)) for i in range(members)])


def student_doc(rows, length, states, gain, w_in, grad, pool_act, pool_x):
    low = states[0, :rows, :]
    values = low.astype(f32)
    center = values - jnp.mean(values, -1, keepdims=True)
    spread = jnp.mean(center * center, -1, keepdims=True)
    real = lax.broadcasted_iota(jnp.int32, (rows, 1), 0) < length
    inverse = jnp.where(real, lax.rsqrt(spread + 1e-05), 0.0)
    tokens = (center * inverse * gain[...]).astype(bf16)
    real = lax.broadcasted_iota(jnp.int32, (8, rows), 1) < length
    sums = jnp.dot(real.astype(bf16), low, preferred_element_type=f32)
    count = length.astype(f32)
    pool_x[0] = sums[:1] / count
    pre_act = jnp.dot(tokens, w_in[...], preferred_element_type=f32)
    half_erf = 0.5 * (1.0 + lax.erf(pre_act * 0.7071067811865476))
    act = (pre_act * half_erf).astype(bf16)
    bell = jnp.exp(-0.5 * pre_act * pre_act)
    slope = (half_erf + pre_act * bell * 0.3989422804014327).astype(bf16)
    sums = jnp.dot(jnp.ones((8, rows), bf16), act, preferred_element_type=f32)
    pool_act[0] = sums[:1] / count
    product = lax.dot_general(
        tokens, slope, (((0,), (0,)), ((), ())), preferred_element_type=f32
    )
    grad[0] = product.astype(bf16)


def student_kernel(first_doc, lens, states, gain, w_in, after, grad, pool_act, pool_x):
    length = lens[first_doc + pl.program_id(0)]
    seq_len = states.shape[1]
    refs = (states, gain, w_in, grad, pool_act, pool_x)
    few = seq_len // 2 if seq_len % 256 == 0 else seq_len

    @pl.when(length <= few)
    def _():
        student_doc(few, length, *refs)

    @pl.when(length > few)
    def _():
        student_doc(seq_len, length, *refs)


def student_part(lengths, states, gain, w_in, after, first_doc, docs):
    seq_len, width = states.shape[1:]
    hidden = w_in.shape[1]
    return pl.pallas_call(
        functools.partial(student_kernel, first_doc),
        grid_spec=pltpu.PrefetchScalarGridSpec(
            num_scalar_prefetch=1,
            grid=(docs,),
            in_specs=[
                pl.BlockSpec((1, seq_len, width), lambda i, n: (first_doc + i, 0, 0)),
                pl.BlockSpec((1, width), lambda i, n: (0, 0)),
                pl.BlockSpec((width, hidden), lambda i, n: (0, 0)),
                pl.BlockSpec(memory_space=pl.ANY),
            ],
            out_specs=[
                pl.BlockSpec((1, width, hidden), lambda i, n: (i, 0, 0)),
                pl.BlockSpec((1, 1, hidden), lambda i, n: (i, 0, 0)),
                pl.BlockSpec((1, 1, width), lambda i, n: (i, 0, 0)),
            ],
        ),
        out_shape=[
            jax.ShapeDtypeStruct((docs, width, hidden), bf16),
            jax.ShapeDtypeStruct((docs, 1, hidden), f32),
            jax.ShapeDtypeStruct((docs, 1, width), f32),
        ],
        compiler_params=pltpu.CompilerParams(
            dimension_semantics=("arbitrary",), vmem_limit_bytes=60 << 20
        ),
        cost_estimate=pl.CostEstimate(
            flops=3 * docs * seq_len * width * hidden,
            bytes_accessed=docs * width * (seq_len + hidden) * 2,
            transcendentals=docs * seq_len * hidden,
        ),
        name="student",
    )(lengths, states, gain.reshape(1, width), w_in, after)


def gate_up_kernel(block, place, columns, gain, weights, parts, held, arrived):
    hidden = weights.shape[2]
    copies = []
    for i in range(hidden // block):
        here = pl.ds(i * block, block)
        copies.append(
            pltpu.make_async_copy(weights.at[:, :, here], held.at[:, :, here], arrived.at[i])
        )
        copies[-1].start()
    depth = columns.shape[1]
    factors = gain[:, pl.ds(pl.multiple_of(place[0] * depth, depth), depth)]
    scaled = (columns[...].astype(f32) * factors).astype(bf16)
    for i, copy in enumerate(copies):
        copy.wait()
        for side in range(2):
            part = jnp.dot(
                scaled, held[side, :, i * block : (i + 1) * block], preferred_element_type=f32
            )
            first = (2 * i + side) * block
            parts[:, first : first + block] = part.astype(bf16)


def gate_up(place, columns, gain, weights, block):
    hidden = weights.shape[2]
    vmem = pl.BlockSpec(memory_space=pltpu.VMEM)
    return pl.pallas_call(
        functools.partial(gate_up_kernel, block),
        in_specs=[
            pl.BlockSpec(memory_space=pltpu.SMEM),
            vmem,
            vmem,
            pl.BlockSpec(memory_space=pltpu.HBM),
        ],
        out_specs=vmem,
        out_shape=jax.ShapeDtypeStruct((columns.shape[0], 2 * hidden), bf16),
        scratch_shapes=[
            pltpu.VMEM(weights.shape, bf16),
            pltpu.SemaphoreType.DMA((hidden // block,)),
        ],
        compiler_params=pltpu.CompilerParams(vmem_limit_bytes=24 << 20),
        name="gate_up",
    )(place, columns, gain.reshape(1, -1), weights)


def hidden_kernel(block, parts, rows, hidden):
    row = rows[...].astype(f32)
    inverse = lax.rsqrt(jnp.mean(row * row, -1, keepdims=True) + 1e-06)
    for first in range(0, hidden.shape[2], block):
        both = jnp.sum(parts[:, :, 2 * first : 2 * (first + block)].astype(f32), 0) * inverse
        gate, upper = both[:, :block], both[:, block:]
        value = (gate / (1.0 + jnp.exp(-gate)) * upper).astype(bf16)
        for copy in range(hidden.shape[0]):
            hidden[copy, :, first : first + block] = value


def hidden_units(parts, rows, block):
    members, docs, both = parts.shape
    return pl.pallas_call(
        functools.partial(hidden_kernel, block),
        out_shape=jax.ShapeDtypeStruct((members, docs, both // 2), bf16),
        compiler_params=pltpu.CompilerParams(vmem_limit_bytes=12 << 20),
        name="hidden",
    )(parts, rows)


def down_kernel(block, hidden, weights, out, held, arrived):
    copies = []
    for i in range(weights.shape[0] // block):
        here = pl.ds(i * block, block)
        copies.append(pltpu.make_async_copy(weights.at[here], held.at[here], arrived.at[i]))
        copies[-1].start()
    total = None
    for i, copy in enumerate(copies):
        copy.wait()
        here = slice(i * block, (i + 1) * block)
        part = jnp.dot(hidden[:, here], held[here, :], preferred_element_type=f32)
        total = part if total is None else total + part
    out[...] = total


def down(hidden, weights, block):
    vmem = pl.BlockSpec(memory_space=pltpu.VMEM)
    return pl.pallas_call(
        functools.partial(down_kernel, block),
        in_specs=[vmem, pl.BlockSpec(memory_space=pltpu.HBM)],
        out_specs=vmem,
        out_shape=jax.ShapeDtypeStruct((hidden.shape[0], weights.shape[1]), f32),
        scratch_shapes=[
            pltpu.VMEM(weights.shape, bf16),
            pltpu.SemaphoreType.DMA((weights.shape[0] // block,)),
        ],
        compiler_params=pltpu.CompilerParams(vmem_limit_bytes=20 << 20),
        name="down",
    )(hidden, weights)


def states_kernel(place, kept, arrived, columns, gain, states, gram):
    value = columns[...].astype(f32) + (kept[...].astype(f32) + arrived[...].astype(f32))
    states[...] = value
    width = value.shape[1]
    scaled = value * gain[:, pl.ds(pl.multiple_of(place[0] * width, width), width)]
    product = lax.dot_general(
        scaled, scaled, (((1,), (1,)), ((), ())), precision=highest, preferred_element_type=f32
    )
    rows = gram.shape[0]
    packed = [product[i : i + rows] for i in range(0, product.shape[0], rows)]
    gram[...] = packed[0] if len(packed) == 1 else jnp.concatenate(packed, axis=1)


def packed_rows(docs):
    return docs * docs // 128 if docs < 128 and 128 % docs == 0 else docs


def teacher_block(place, kept, arrived, columns, gain):
    docs, width = columns.shape
    rows = packed_rows(docs)
    vmem = pl.BlockSpec(memory_space=pltpu.VMEM)
    return pl.pallas_call(
        states_kernel,
        in_specs=[pl.BlockSpec(memory_space=pltpu.SMEM)] + [vmem] * 4,
        out_specs=[vmem] * 2,
        out_shape=[
            jax.ShapeDtypeStruct((docs, width), f32),
            jax.ShapeDtypeStruct((rows, docs * docs // rows), f32),
        ],
        compiler_params=pltpu.CompilerParams(vmem_limit_bytes=8 << 20),
        name="teacher_block",
    )(place, kept, arrived, columns, gain.reshape(1, -1))


def embed_kernel(order, place, blocks, unit, norms, logits, raw):
    docs = blocks.shape[1]
    for i in range(blocks.shape[0]):
        member = place[0] ^ sum(((i >> k) & 1) << bit for k, bit in enumerate(order))
        raw[pl.ds(pl.multiple_of(member * docs, docs), docs), :] = blocks[i]
    value = raw[...]
    size = jnp.sqrt(jnp.sum(value * value, -1, keepdims=True) + 1e-06)
    units = value / size
    norms[...] = size
    unit[...] = units
    logits[...] = (
        lax.dot_general(
            units, units, (((1,), (1,)), ((), ())), precision=highest, preferred_element_type=f32
        )
        / student_softness
    )


def embed(place, blocks, order):
    members, each, width = blocks.shape
    docs = members * each
    vmem = pl.BlockSpec(memory_space=pltpu.VMEM)
    return pl.pallas_call(
        functools.partial(embed_kernel, order),
        in_specs=[pl.BlockSpec(memory_space=pltpu.SMEM), vmem],
        out_specs=[vmem] * 3,
        out_shape=[
            jax.ShapeDtypeStruct((docs, width), f32),
            jax.ShapeDtypeStruct((docs, 1), f32),
            jax.ShapeDtypeStruct((docs, docs), f32),
        ],
        scratch_shapes=[pltpu.VMEM((docs, width), f32)],
        compiler_params=pltpu.CompilerParams(vmem_limit_bytes=8 << 20),
        name="embed",
    )(place, blocks)


def contrast_kernel(place, lens, gram_sum, logits, unit, norms, w_out, *refs):
    loss, low, scale, raw = refs[-4:]
    gram = gram_sum[...]
    docs = logits.shape[0]
    if gram.shape[1] != docs:
        gram = jnp.concatenate(
            [gram[:, i : i + docs] for i in range(0, gram.shape[1], docs)], axis=0
        )
    row = lax.broadcasted_iota(jnp.int32, (docs, docs), 0)
    col = lax.broadcasted_iota(jnp.int32, (docs, docs), 1)
    keep = row != col
    partner = (row + 1 - 2 * (row % 2)) == col
    own = jnp.where(keep, 0.0, gram)
    sizes_down = jnp.sqrt(jnp.sum(own, 1, keepdims=True) + 1e-06)
    sizes_along = jnp.sqrt(jnp.sum(own, 0, keepdims=True) + 1e-06)
    t_logits = gram / (sizes_down * sizes_along) / teacher_softness
    s_logits = logits[...]
    t_exp = jnp.where(keep, jnp.exp(t_logits), 0.0)
    s_exp = jnp.where(keep, jnp.exp(s_logits), 0.0)
    t_down = jnp.sum(t_exp, 1, keepdims=True)
    s_down = jnp.sum(s_exp, 1, keepdims=True)
    t_along = jnp.sum(t_exp, 0, keepdims=True)
    s_along = jnp.sum(s_exp, 0, keepdims=True)
    s_log = s_logits - jnp.log(s_down)
    t_log = t_logits - jnp.log(t_down)
    terms = jnp.where(partner, -s_log, 0.0)
    terms = terms + jnp.where(keep, t_exp / t_down * (t_log - s_log), 0.0)
    loss[...] = jnp.sum(jnp.sum(terms, 1, keepdims=True), 0, keepdims=True)
    both = 2.0 * (s_exp / s_down + s_exp / s_along) - (t_exp / t_down + t_exp / t_along)
    both = both - jnp.where(partner, 2.0, 0.0)
    units = unit[...]
    unit_grad = (
        jnp.dot(both, units, precision=highest, preferred_element_type=f32) / student_softness
    )
    along = jnp.sum(units * unit_grad, -1, keepdims=True)
    raw_low = ((unit_grad - units * along) / norms[...]).astype(bf16)
    low[...] = raw_low
    raw[...] = raw_low.astype(f32)
    mine = raw[pl.ds(pl.multiple_of(place[0] * scale.shape[0], scale.shape[0]), scale.shape[0]), :]
    pool_grad = lax.dot_general(
        mine.astype(bf16), w_out[...], (((1,), (1,)), ((), ())), preferred_element_type=f32
    )
    for doc in range(scale.shape[0]):
        scale[doc : doc + 1, :] = pool_grad[doc : doc + 1, :] / lens[doc].astype(f32)


def contrast(place, lengths, gram_sum, logits, unit, norms, w_out, *after):
    total_docs, width = unit.shape
    local_docs, hidden = lengths.shape[0], w_out.shape[0]
    vmem, smem = pl.BlockSpec(memory_space=pltpu.VMEM), pl.BlockSpec(memory_space=pltpu.SMEM)
    return pl.pallas_call(
        contrast_kernel,
        in_specs=[smem] * 2 + [vmem] * 5 + [pl.BlockSpec(memory_space=pl.ANY)] * len(after),
        out_specs=[vmem] * 3,
        out_shape=[
            jax.ShapeDtypeStruct((1, 1), f32),
            jax.ShapeDtypeStruct((total_docs, width), bf16),
            jax.ShapeDtypeStruct((local_docs, hidden), f32),
        ],
        scratch_shapes=[pltpu.VMEM((total_docs, width), f32)],
        compiler_params=pltpu.CompilerParams(vmem_limit_bytes=20 << 20),
        name="contrast",
    )(place, lengths, gram_sum, logits, unit, norms, w_out, *after)


def relative(order, bits, step):
    return sum(((step >> (bits - 1 - k)) & 1) << bit for k, bit in enumerate(order))


def weigh_kernel(orders, bits, first, parts, place, scale, *refs):
    grads, outs = refs[:parts], refs[-2:]
    half, rows, group = scale.shape[1] // 2, outs[0].shape[1], 16
    for side in range(2):
        here = pl.ds(side * half, half)
        factors = scale[:, side * half : (side + 1) * half]
        member = place[0] ^ relative(orders[side], bits, first + pl.program_id(0))
        start = pl.multiple_of(member * rows, rows)

        def step(i, carry, side=side, here=here, factors=factors, start=start):
            near = pl.multiple_of(i * group, group)
            total, doc = None, 0
            for grad in grads:
                for j in range(grad.shape[0]):
                    value = grad[j, pl.ds(start + near, group), here].astype(f32)
                    term = value * factors[doc : doc + 1]
                    total = term if total is None else total + term
                    doc += 1
            outs[side][0, pl.ds(near, group), :] = total.astype(bf16)
            return carry

        lax.fori_loop(0, rows // group, step, 0)


def weigh(place, scale, grads, orders, members, first, after=()):
    width, hidden = grads[0].shape[1:]
    bits = members.bit_length() - 1
    rows, half = width // members, hidden // 2
    vmem = pl.BlockSpec(memory_space=pltpu.VMEM)
    return pl.pallas_call(
        functools.partial(weigh_kernel, orders, bits, first, len(grads)),
        grid_spec=pltpu.PrefetchScalarGridSpec(
            num_scalar_prefetch=1,
            grid=(members // 2,),
            in_specs=[pl.BlockSpec(scale.shape, lambda i, p: (0, 0))]
            + [vmem] * len(grads)
            + [pl.BlockSpec(memory_space=pl.ANY)] * len(after),
            out_specs=[pl.BlockSpec((1, rows, half), lambda i, p: (i, 0, 0))] * 2,
        ),
        out_shape=[jax.ShapeDtypeStruct((members // 2, rows, half), bf16)] * 2,
        compiler_params=pltpu.CompilerParams(
            dimension_semantics=("arbitrary",), vmem_limit_bytes=24 << 20
        ),
        name="weigh",
    )(place, scale, *grads, *after)


def halving(sent, kept, order, axis):
    for bit in order:
        arrived = swap(sent, axis, bit)
        rest = kept.shape[0] // 2
        if rest:
            sent = (kept[rest:].astype(f32) + arrived[rest:].astype(f32)).astype(bf16)
            kept = (kept[:rest].astype(f32) + arrived[:rest].astype(f32)).astype(bf16)
    return kept[0].astype(f32) + arrived[0].astype(f32)


def on_device(
    student_states,
    lengths,
    student_ln_gain,
    student_w_in,
    student_w_out,
    teacher_rows,
    teacher_mlp_gain,
    teacher_gate_up,
    teacher_down,
    teacher_final_gain,
):
    dp_count = lax.axis_size("dp")
    section_count = lax.axis_size("section")
    dp_index = lax.axis_index("dp")
    section_index = lax.axis_index("section")
    local_docs = teacher_rows.shape[0]
    total_docs = local_docs * dp_count
    col_width = teacher_gate_up.shape[1]
    hidden_width = teacher_gate_up.shape[2]
    place = dp_index.astype(jnp.int32).reshape(1)
    block = hidden_width // 6 if hidden_width % 768 == 0 else hidden_width
    student = functools.partial(
        student_part, lengths, student_states, student_ln_gain, student_w_in
    )
    cuts = (0, local_docs // 4, local_docs - local_docs // 8, local_docs)

    blocks = teacher_rows.reshape(local_docs, dp_count, col_width).transpose(1, 0, 2)
    columns = exchange(blocks, "dp").reshape(total_docs, col_width)
    first = student(teacher_rows, cuts[0], cuts[1] - cuts[0])
    parts = gate_up(place, columns, teacher_mlp_gain, teacher_gate_up, block)
    parts = parts.reshape(dp_count, local_docs, 2 * hidden_width)
    second = student(parts, cuts[1], cuts[2] - cuts[1])
    parts = exchange(parts, "dp")
    hidden = hidden_units(parts, teacher_rows, block)
    third = student(hidden, cuts[2], cuts[3] - cuts[2])
    every_hidden = exchange(hidden, "dp").reshape(total_docs, hidden_width)
    out = down(every_hidden, teacher_down, block)
    for bit in range(section_count.bit_length() - 1):
        kept = out if bit == 0 else out.astype(bf16)
        arrived = swap(kept, "section", bit)
        out = kept.astype(f32) + arrived.astype(f32)
    states_block, gram_sum = teacher_block(place, kept, arrived, columns, teacher_final_gain)
    bits = dp_count.bit_length() - 1
    for bit in range(bits):
        gram_sum = gram_sum + swap(gram_sum, "dp", bit)

    grads, acts, states = zip(first, second, third)
    pooled_act = jnp.concatenate(acts)[:, 0].astype(bf16)
    pooled_x = jnp.concatenate(states)[:, 0]
    emb_sum = jnp.dot(pooled_act, student_w_out, preferred_element_type=f32)
    for bit in range(section_count.bit_length() - 1):
        emb_sum = emb_sum + swap(emb_sum, "section", bit)
    far_first = tuple(reversed(range(bits)))
    every_raw = (pooled_x + emb_sum)[None]
    for bit in far_first:
        every_raw = jnp.concatenate([every_raw, swap(every_raw, "dp", bit)])
    unit, norms, student_logits = embed(place, every_raw, far_first)
    loss, every_low, scale = contrast(
        place, lengths, gram_sum, student_logits, unit, norms, student_w_out
    )

    orders = (tuple(range(bits)), (1, 0) + tuple(range(2, bits)))
    sent = weigh(place, scale, grads, orders, dp_count, dp_count // 2)
    kept = weigh(place, scale, grads, orders, dp_count, 0, sent)
    sides = []
    for side in range(2):
        sides.append(halving(sent[side], kept[side], orders[side], "dp"))
    grad_w_in = jnp.concatenate(sides, axis=1)
    pooled = pooled_act.reshape(local_docs, dp_count, -1).transpose(1, 0, 2).astype(f32)
    states_block = states_block.reshape(dp_count, local_docs, col_width)
    last = exchange(jnp.concatenate([states_block, pooled], axis=2), "dp")
    per_section = dp_count // section_count
    own_blocks = lax.dynamic_slice_in_dim(last, section_index * per_section, per_section, 0)
    own_blocks = own_blocks[:, :, :col_width].transpose(1, 0, 2)
    teacher_states = own_blocks.reshape(local_docs, per_section * col_width)
    pooled_columns = last[:, :, col_width:].reshape(total_docs, -1).astype(bf16)
    grad_w_out = lax.dot_general(
        pooled_columns, every_low, (((0,), (0,)), ((), ())), preferred_element_type=f32
    )
    return (loss[0, 0], grad_w_in, grad_w_out, teacher_states)


def solution(mesh):
    placed = (
        P("dp", None, None),
        P("dp"),
        P(),
        P(None, "section"),
        P("section", None),
        P("dp", None),
        P(),
        P(None, "dp", "section"),
        P("section", "dp"),
        P(),
    )

    return jax.shard_map(
        on_device,
        mesh=mesh,
        in_specs=placed,
        out_specs=(P(), P("dp", "section"), P(("section", "dp"), None), P("dp", "section")),
        check_vma=False,
    )
```

time: 233 us -> 151 us (0.65)
  waiting for transfers between devices: 86.7 us -> 31.4 us
  matrix products: 53.1 us -> 1.43 us
  Pallas kernels: 0 us -> 45 us
  other arithmetic: 30.3 us -> 4 us
  local copies, waits for them, and re-layouts: 11.9 us -> 17.8 us
    all_to_all x10 -> x4, waiting for transfers between devices: 86.7 us -> 6.91 us  [exchange(): return lax.all_to_all(blocks, axis, 0, 0, tiled=True)]
    dot_general x12 -> x1, matrix products: 51.3 us -> 0.38 us  [on_device(): emb_sum = jnp.dot(pooled_act, student_w_out, preferred_element_type=f32)]
    pallas_call x0 -> x11, Pallas kernels: none -> 45 us  [the longest x3 32 us: student_part(): pl.pallas_call(functools.partial(student_kernel, first_doc), grid_spec=pl...]
    ppermute x0 -> x16, starting transfers between devices: none -> 24.8 us  [swap(): lax.ppermute(value, axis, [(i, i ^ 1 << bit) for i in range(members)])]
    ppermute x0 -> x16, waiting for transfers between devices: none -> 24.5 us  [swap(): lax.ppermute(value, axis, [(i, i ^ 1 << bit) for i in range(members)])]
    all_to_all x10 -> x4, starting transfers between devices: 48.3 us -> 24.9 us  [exchange(): return lax.all_to_all(blocks, axis, 0, 0, tiled=True)]
    reduce_sum x12 -> x0, other arithmetic: 16 us -> none  [the longest x1 4.56 us: layer_norm(): center = values - jnp.mean(values, -1, keepdims=True)]
    unnamed x28 -> x36, local copies, waits for them, and re-layouts: 5.22 us -> 17.2 us
  transfers between devices with their start and end apart: 10 -> 20, of which waited for: 6 -> 12; matrix products, arithmetic and copies ran while one was open for 34% -> 3% of each run, Pallas kernels for 0% -> 24%
where the time goes in v2:
time: 151 us; the launch traced here: 150 us
  starting transfers between devices  49.7 us (33%)
  Pallas kernels  45 us (30%)
  waiting for transfers between devices  31.4 us (21%)
  local copies, waits for them, and re-layouts  17.8 us (12%)
  other arithmetic  4 us (3%)
    pallas_call x3, Pallas kernels, student_part(): pl.pallas_call(functools.partial(student_kernel, first_doc), grid_spec=pl...  32 us
    all_to_all x4, starting transfers between devices, exchange(): return lax.all_to_all(blocks, axis, 0, 0, tiled=True)  24.9 us
    ppermute x16, starting transfers between devices, swap(): lax.ppermute(value, axis, [(i, i ^ 1 << bit) for i in range(members)])  24.8 us
    ppermute x16, waiting for transfers between devices, swap(): lax.ppermute(value, axis, [(i, i ^ 1 << bit) for i in range(members)])  24.5 us
    unnamed x36, local copies, waits for them, and re-layouts  17.2 us
    all_to_all x4, waiting for transfers between devices, exchange(): return lax.all_to_all(blocks, axis, 0, 0, tiled=True)  6.91 us
    pallas_call x2, Pallas kernels, weigh(): pl.pallas_call(functools.partial(weigh_kernel, orders, bits, first, len(g...  4.6 us
    pallas_call x1, Pallas kernels, gate_up(): pl.pallas_call(functools.partial(gate_up_kernel, block), in_specs=[pl.Blo...  3.57 us
  transfers between devices with their start and end apart: 20, of which 12 were waited for; matrix products, arithmetic and copies ran while one was open for 3% of the time, Pallas kernels for 24%

profile of v2, /device:TPU:0, one launch (start us, length us, event | category | flops | bytes accessed | tf_op | source)
XLA Modules:
  0.0 150.3 jit_solution(10691568143331515845)
XLA Ops:
  0.6 7.3 %all-to-all-start = ((bf16[8,8,512]{2,1,0:T(8,128)(2,1)}), bf16[8,8,512]{2,1,0:T(8,128)(2,1)S(1)}, u32[]{:S(2)}, u32[]{:S(2)}) async-start(bf16[8,8,512]{2,1,0:T(8,128)(2,1)} %bitcast.42), calls=%async_computation | async-start | bytes 131072 | tf_op jit(solution)/shard_map/all_to_all | solution.py:19
  8.0 6.9 %all-to-all-done = bf16[8,8,512]{2,1,0:T(8,128)(2,1)S(1)} async-done(((bf16[8,8,512]{2,1,0:T(8,128)(2,1)}), bf16[8,8,512]{2,1,0:T(8,128)(2,1)S(1)}, u32[]{:S(2)}, u32[]{:S(2)}) %all-to-all-start) | async-done | bytes 65568 | tf_op jit(solution)/shard_map/all_to_all | solution.py:19
  14.9 2.8 %copy-done.7 = bf16[2,512,3072]{2,1,0:T(8,128)(2,1)S(1)} copy-done((bf16[2,512,3072]{2,1,0:T(8,128)(2,1)S(1)}, bf16[2,512,3072]{2,1,0:T(8,128)(2,1)}, u32[]{:S(2)}) %copy-start.7) | copy-done | bytes 6291480
  17.6 0.7 copy-done.10
  18.4 3.6 %gate_up.1 = bf16[64,6144]{1,0:T(8,128)(2,1)} custom-call(s32[1]{0:T(128)} %bitcast.place, bf16[64,512]{1,0:T(8,128)(2,1)S(1)} %bitcast.40, f32[1,4096]{1,0:T(1,128)S(1)} %bitcast.44, bf16[2,512,3072]{2,1,0:T(8,128)(2,1)S(1)} %copy-done.7), custom_call_target="tpu_custom_call" | custom-call | tf_op jit(solution)/shard_map/gate_up/pallas_call | solution.py:129
  21.9 3.6 %all-to-all-start.1 = ((bf16[8,8,6144]{2,1,0:T(8,128)(2,1)}), bf16[8,8,6144]{2,1,0:T(8,128)(2,1)S(1)}, u32[]{:S(2)}, u32[]{:S(2)}) async-start(bf16[8,8,6144]{2,1,0:T(8,128)(2,1)} %bitcast.5.after), calls=%async_computation.1 | async-start | bytes 1572864 | tf_op jit(solution)/shard_map/all_to_all | solution.py:19
  25.5 9.3 %student.3 = (bf16[2,1024,1024]{2,1,0:T(8,128)(2,1)}, f32[2,1,1024]{2,1,0:T(1,128)}, f32[2,1,1024]{2,1,0:T(1,128)}) custom-call(s32[8]{0:T(128)} %lens.7, bf16[8,512,1024]{2,1,0:T(8,128)(2,1)} %states.5, f32[1,1024]{1,0:T(1,128)} %bitcast.48, bf16[1024,1024]{1,0:T(8,128)(2,1)} %w_in.5, bf16[8,4096]{1,0:T(8,128)(2,1)} %after.1), custom_call_target="tpu_custom_call" | custom-call | flops 3221225472 | bytes 6291456 | tf_op jit(solution)/shard_map/student/pallas_call | solution.py:70
  34.8 16.7 %student.4 = (bf16[5,1024,1024]{2,1,0:T(8,128)(2,1)}, f32[5,1,1024]{2,1,0:T(1,128)}, f32[5,1,1024]{2,1,0:T(1,128)}) custom-call(s32[8]{0:T(128)} %lens.7, bf16[8,512,1024]{2,1,0:T(8,128)(2,1)} %states.5, f32[1,1024]{1,0:T(1,128)} %bitcast.49, bf16[1024,1024]{1,0:T(8,128)(2,1)} %w_in.5, bf16[8,8,6144]{2,1,0:T(8,128)(2,1)} %bitcast.5.after), custom_call_target="tpu_custom_call" | custom-call | flops 8053063680 | bytes 15728640 | tf_op jit(solution)/shard_map/student/pallas_call | solution.py:70
  51.5 0.9 hidden.1.after
  52.5 9.4 %all-to-all-start.2 = ((bf16[8,8,3072]{2,1,0:T(8,128)(2,1)}), bf16[8,8,3072]{2,1,0:T(8,128)(2,1)S(1)}, u32[]{:S(2)}, u32[]{:S(2)}) async-start(bf16[8,8,3072]{2,1,0:T(8,128)(2,1)} %hidden.1.after), calls=%async_computation.2 | async-start | bytes 786432 | tf_op jit(solution)/shard_map/all_to_all | solution.py:19
  61.9 6.0 %student.5 = (bf16[1,1024,1024]{2,1,0:T(8,128)(2,1)}, f32[1,1,1024]{2,1,0:T(1,128)}, f32[1,1,1024]{2,1,0:T(1,128)}) custom-call(s32[8]{0:T(128)} %lens.7, bf16[8,512,1024]{2,1,0:T(8,128)(2,1)} %states.5, f32[1,1024]{1,0:T(1,128)} %bitcast.50, bf16[1024,1024]{1,0:T(8,128)(2,1)} %w_in.5, bf16[8,8,3072]{2,1,0:T(8,128)(2,1)} %hidden.1.after), custom_call_target="tpu_custom_call" | custom-call | flops 1610612736 | bytes 3145728 | tf_op jit(solution)/shard_map/student/pallas_call | solution.py:70
  67.9 0.7 fusion.8
  69.0 1.2 collective-permute-done.5
  70.2 1.5 collective-permute-start.6
  71.7 2.4 %collective-permute-done.6 = f32[8,1024]{1,0:T(8,128)S(1)} collective-permute-done((f32[8,1024]{1,0:T(8,128)S(1)}, f32[8,1024]{1,0:T(8,128)S(1)}, u32[]{:S(2)}, u32[]{:S(2)}) %collective-permute-start.6) | collective-permute-done | bytes 32800 | tf_op jit(solution)/shard_map/ppermute | solution.py:24
  74.2 3.0 %collective-permute-start.7 = (f32[1,8,1024]{2,1,0:T(8,128)S(1)}, f32[1,8,1024]{2,1,0:T(8,128)S(1)}, u32[]{:S(2)}, u32[]{:S(2)}) collective-permute-start(f32[1,8,1024]{2,1,0:T(8,128)S(1)} %fusion.1), channel_id=1, source_target_pairs={{0,4},{1,5},{2,6},{3,7},{4,0},{5,1},{6,2},{7,3},{8,12},{9,13},{10,... | collective-permute-start | bytes 98312 | tf_op jit(solution)/shard_map/ppermute | solution.py:24
  77.1 1.9 %collective-permute-done.7 = f32[1,8,1024]{2,1,0:T(8,128)S(1)} collective-permute-done((f32[1,8,1024]{2,1,0:T(8,128)S(1)}, f32[1,8,1024]{2,1,0:T(8,128)S(1)}, u32[]{:S(2)}, u32[]{:S(2)}) %collective-permute-start.7) | collective-permute-done | bytes 32800 | tf_op jit(solution)/shard_map/ppermute | solution.py:24
  79.1 3.4 %collective-permute-start.8 = (f32[2,8,1024]{2,1,0:T(8,128)S(1)}, f32[2,8,1024]{2,1,0:T(8,128)S(1)}, u32[]{:S(2)}, u32[]{:S(2)}) collective-permute-start(f32[2,8,1024]{2,1,0:T(8,128)S(1)} %pad_maximum_fusion.4), channel_id=1, source_target_pairs={{0,2},{1,3},{2,0},{3,1},{4,6},{5,7},{6,4},{7,5},{8,10},{9,11},{10,... | collective-permute-start | bytes 196616 | tf_op jit(solution)/shard_map/ppermute | solution.py:24
  82.5 1.9 %copy-done.8 = bf16[3072,512]{1,0:T(8,128)(2,1)S(1)} copy-done((bf16[3072,512]{1,0:T(8,128)(2,1)S(1)}, bf16[3072,512]{1,0:T(8,128)(2,1)}, u32[]{:S(2)}) %copy-start.8) | copy-done | bytes 3145752
  84.4 1.0 down.1
  85.5 1.1 collective-permute-start.9
  86.9 1.5 %collective-permute-start.1 = (bf16[64,512]{1,0:T(8,128)(2,1)S(1)}, bf16[64,512]{1,0:T(8,128)(2,1)S(1)}, u32[]{:S(2)}, u32[]{:S(2)}) collective-permute-start(bf16[64,512]{1,0:T(8,128)(2,1)S(1)} %add_convert_fusion.8.kept), channel_id=1, source_target_pairs={{0,16},{8,24},{16,0},{24,8},{1,17},{9,25},{17,1},{25,9},{2,18},{10... | collective-permute-start | bytes 196616 | tf_op jit(solution)/shard_map/ppermute | solution.py:24
  88.4 2.8 %collective-permute-done.1.arrived = bf16[64,512]{1,0:T(8,128)(2,1)S(1)} collective-permute-done((bf16[64,512]{1,0:T(8,128)(2,1)S(1)}, bf16[64,512]{1,0:T(8,128)(2,1)S(1)}, u32[]{:S(2)}, u32[]{:S(2)}) %collective-permute-start.1) | collective-permute-done | bytes 65568 | tf_op jit(solution)/shard_map/ppermute | solution.py:24
  91.5 0.8 collective-permute-start.2
  92.3 3.0 %collective-permute-done.2 = f32[32,128]{1,0:T(8,128)S(1)} collective-permute-done((f32[32,128]{1,0:T(8,128)S(1)}, f32[32,128]{1,0:T(8,128)S(1)}, u32[]{:S(2)}, u32[]{:S(2)}) %collective-permute-start.2) | collective-permute-done | bytes 16416 | tf_op jit(solution)/shard_map/ppermute | solution.py:24
  95.9 3.2 %collective-permute-done.3 = f32[32,128]{1,0:T(8,128)S(1)} collective-permute-done((f32[32,128]{1,0:T(8,128)S(1)}, f32[32,128]{1,0:T(8,128)S(1)}, u32[]{:S(2)}, u32[]{:S(2)}) %collective-permute-start.3) | collective-permute-done | bytes 16416 | tf_op jit(solution)/shard_map/ppermute | solution.py:24
  99.0 2.5 %collective-permute-start.4 = (f32[32,128]{1,0:T(8,128)S(1)}, f32[32,128]{1,0:T(8,128)S(1)}, u32[]{:S(2)}, u32[]{:S(2)}) collective-permute-start(f32[32,128]{1,0:T(8,128)S(1)} %add.62), channel_id=1, source_target_pairs={{0,4},{1,5},{2,6},{3,7},{4,0},{5,1},{6,2},{7,3},{8,12},{9,13},{10,... | collective-permute-start | bytes 49160 | tf_op jit(solution)/shard_map/ppermute | solution.py:24
  102.1 1.8 %collective-permute-done.4 = f32[32,128]{1,0:T(8,128)S(1)} collective-permute-done((f32[32,128]{1,0:T(8,128)S(1)}, f32[32,128]{1,0:T(8,128)S(1)}, u32[]{:S(2)}, u32[]{:S(2)}) %collective-permute-start.4) | collective-permute-done | bytes 16416 | tf_op jit(solution)/shard_map/ppermute | solution.py:24
  103.9 1.6 %copy-done.6 = bf16[1024,1024]{1,0:T(8,128)(2,1)S(1)} copy-done((bf16[1024,1024]{1,0:T(8,128)(2,1)S(1)}, bf16[1024,1024]{1,0:T(8,128)(2,1)}, u32[]{:S(2)}) %copy-start.6) | copy-done | bytes 2097176
  105.5 2.1 %contrast.1 = (f32[1,1]{1,0:T(1,128)}, bf16[64,1024]{1,0:T(8,128)(2,1)S(1)}, f32[8,1024]{1,0:T(8,128)S(1)}) custom-call(s32[1]{0:T(128)} %bitcast.place, s32[8]{0:T(128)S(1)} %copy-done.12, f32[32,128]{1,0:T(8,128)S(1)} %add.63.gram_sum, f32[64,64]{1,0:T(8,128)S(1)} %get-tuple-element.32.logits, f32[64,1024]{1,0:T(8,128)S(1)} %get-tuple-element.33.unit, ...), custom_call_target="tpu_custom_call" | custom-call | tf_op jit(solution)/shard_map/contrast/pallas_call | solution.py:321
  107.5 4.0 %copy-done = bf16[5,1024,1024]{2,1,0:T(8,128)(2,1)S(1)} copy-done((bf16[5,1024,1024]{2,1,0:T(8,128)(2,1)S(1)}, bf16[5,1024,1024]{2,1,0:T(8,128)(2,1)}, u32[]{:S(2)}) %copy-start) | copy-done | bytes 10485784
  111.5 2.3 %weigh.2 = (bf16[4,128,512]{2,1,0:T(8,128)(2,1)S(1)}, bf16[4,128,512]{2,1,0:T(8,128)(2,1)S(1)}) custom-call(s32[1]{0:T(128)} %bitcast.place, f32[8,1024]{1,0:T(8,128)S(1)} %get-tuple-element.36.scale, bf16[2,1024,1024]{2,1,0:T(8,128)(2,1)S(1)} %copy-done.2, bf16[5,1024,1024]{2,1,0:T(8,128)(2,1)S(1)} %copy-done, bf16[1,1024,1024]{2,1,0:T(8,128)(2,1)S(1)} %copy-done.4), custom_call_target="tpu_custom_call" | custom-call | tf_op jit(solution)/shard_map/weigh/pallas_call | solution.py:369
  114.5 1.2 collective-permute-start.13
  115.7 0.7 pad_maximum_fusion.2
  116.4 4.7 %all-to-all-start.3 = ((f32[8,8,640]{2,1,0:T(8,128)}), f32[8,8,640]{2,1,0:T(8,128)S(1)}, u32[]{:S(2)}, u32[]{:S(2)}) async-start(f32[8,8,640]{2,1,0:T(8,128)} %pad_maximum_fusion.2), calls=%async_computation.3 | async-start | bytes 327680 | tf_op jit(solution)/shard_map/all_to_all | solution.py:19
  121.1 4.0 %copy-done.1 = bf16[5,1024,1024]{2,1,0:T(8,128)(2,1)S(1)} copy-done((bf16[5,1024,1024]{2,1,0:T(8,128)(2,1)S(1)}, bf16[5,1024,1024]{2,1,0:T(8,128)(2,1)}, u32[]{:S(2)}) %copy-start.1) | copy-done | bytes 10485784
  125.1 2.2 %copy-done.3 = bf16[2,1024,1024]{2,1,0:T(8,128)(2,1)S(1)} copy-done((bf16[2,1024,1024]{2,1,0:T(8,128)(2,1)S(1)}, bf16[2,1024,1024]{2,1,0:T(8,128)(2,1)}, u32[]{:S(2)}) %copy-start.3) | copy-done | bytes 4194328
  127.3 2.3 %weigh.3 = (bf16[4,128,512]{2,1,0:T(8,128)(2,1)S(1)}, bf16[4,128,512]{2,1,0:T(8,128)(2,1)S(1)}) custom-call(s32[1]{0:T(128)} %bitcast.place, f32[8,1024]{1,0:T(8,128)S(1)} %get-tuple-element.36.scale, bf16[2,1024,1024]{2,1,0:T(8,128)(2,1)S(1)} %copy-done.3, bf16[5,1024,1024]{2,1,0:T(8,128)(2,1)S(1)} %copy-done.1, bf16[1,1024,1024]{2,1,0:T(8,128)(2,1)S(1)} %copy-done.4, ...), custom_call_target="tpu_custom_call" | custom-call | tf_op jit(solution)/shard_map/weigh/pallas_call | solution.py:369
  129.6 1.5 add_convert_fusion.1
  131.1 2.1 %collective-permute-start.14 = (bf16[2,128,512]{2,1,0:T(8,128)(2,1)S(1)}, bf16[2,128,512]{2,1,0:T(8,128)(2,1)S(1)}, u32[]{:S(2)}, u32[]{:S(2)}) collective-permute-start(bf16[2,128,512]{2,1,0:T(8,128)(2,1)S(1)} %get-tuple-element.51), channel_id=1, source_target_pairs={{0,1},{1,0},{2,3},{3,2},{4,5},{5,4},{6,7},{7,6},{8,9},{9,8},{10,11... | collective-permute-start | bytes 786440 | tf_op jit(solution)/shard_map/ppermute | solution.py:24
  133.2 1.0 fusion.3
  134.2 1.5 collective-permute-start.11
  136.3 1.2 collective-permute-done.14
  137.6 3.0 %collective-permute-start.15 = (bf16[1,128,512]{2,1,0:T(8,128)(2,1)S(1)}, bf16[1,128,512]{2,1,0:T(8,128)(2,1)S(1)}, u32[]{:S(2)}, u32[]{:S(2)}) collective-permute-start(bf16[1,128,512]{2,1,0:T(8,128)(2,1)S(1)} %add_convert_fusion.4), channel_id=1, source_target_pairs={{0,4},{1,5},{2,6},{3,7},{4,0},{5,1},{6,2},{7,3},{8,12},{9,13},{10,... | collective-permute-start | bytes 393224 | tf_op jit(solution)/shard_map/ppermute | solution.py:24
  140.6 1.4 collective-permute-done.11
  142.1 1.9 %collective-permute-start.12 = (bf16[1,128,512]{2,1,0:T(8,128)(2,1)S(1)}, bf16[1,128,512]{2,1,0:T(8,128)(2,1)S(1)}, u32[]{:S(2)}, u32[]{:S(2)}) collective-permute-start(bf16[1,128,512]{2,1,0:T(8,128)(2,1)S(1)} %add_convert_fusion.6), channel_id=1, source_target_pairs={{0,4},{1,5},{2,6},{3,7},{4,0},{5,1},{6,2},{7,3},{8,12},{9,13},{10,... | collective-permute-start | bytes 393224 | tf_op jit(solution)/shard_map/ppermute | solution.py:24
  144.0 5.4 %collective-permute-done.12 = bf16[1,128,512]{2,1,0:T(8,128)(2,1)S(1)} collective-permute-done((bf16[1,128,512]{2,1,0:T(8,128)(2,1)S(1)}, bf16[1,128,512]{2,1,0:T(8,128)(2,1)S(1)}, u32[]{:S(2)}, u32[]{:S(2)}) %collective-permute-start.12) | collective-permute-done | bytes 131104 | tf_op jit(solution)/shard_map/ppermute | solution.py:24
  149.4 0.8 pad_maximum_fusion
  (62 shorter events, 3.7 us)
Async XLA Ops:
  0.6 14.2 %all-to-all-start = ((bf16[8,8,512]{2,1,0:T(8,128)(2,1)}), bf16[8,8,512]{2,1,0:T(8,128)(2,1)S(1)}, u32[]{:S(2)}, u32[]{:S(2)}) async-start(bf16[8,8,512]{2,1,0:T(8,128)(2,1)} %bitcast.42), calls=%async_computation | async-start | bytes 131072 | tf_op jit(solution)/shard_map/all_to_all | solution.py:19
  14.9 2.8 %copy-start.7 = (bf16[2,512,3072]{2,1,0:T(8,128)(2,1)S(1)}, bf16[2,512,3072]{2,1,0:T(8,128)(2,1)}, u32[]{:S(2)}) copy-start(bf16[2,512,3072]{2,1,0:T(8,128)(2,1)} %weights.2) | copy-start | bytes 18874372
  17.6 0.7 copy-start.10
  21.9 29.6 %all-to-all-start.1 = ((bf16[8,8,6144]{2,1,0:T(8,128)(2,1)}), bf16[8,8,6144]{2,1,0:T(8,128)(2,1)S(1)}, u32[]{:S(2)}, u32[]{:S(2)}) async-start(bf16[8,8,6144]{2,1,0:T(8,128)(2,1)} %bitcast.5.after), calls=%async_computation.1 | async-start | bytes 1572864 | tf_op jit(solution)/shard_map/all_to_all | solution.py:19
  34.8 16.8 %copy-start.9 = (bf16[8,4096]{1,0:T(8,128)(2,1)S(1)}, bf16[8,4096]{1,0:T(8,128)(2,1)}, u32[]{:S(2)}) copy-start(bf16[8,4096]{1,0:T(8,128)(2,1)} %after.1) | copy-start | bytes 196612
  52.5 30.0 %all-to-all-start.2 = ((bf16[8,8,3072]{2,1,0:T(8,128)(2,1)}), bf16[8,8,3072]{2,1,0:T(8,128)(2,1)S(1)}, u32[]{:S(2)}, u32[]{:S(2)}) async-start(bf16[8,8,3072]{2,1,0:T(8,128)(2,1)} %hidden.1.after), calls=%async_computation.2 | async-start | bytes 786432 | tf_op jit(solution)/shard_map/all_to_all | solution.py:19
  61.9 6.0 %copy-start.14 = (f32[5,1,1024]{2,1,0:T(1,128)S(1)}, f32[5,1,1024]{2,1,0:T(1,128)}, u32[]{:S(2)}) copy-start(f32[5,1,1024]{2,1,0:T(1,128)} %get-tuple-element.30) | copy-start | bytes 61444
  61.9 6.0 %copy-start.15 = (f32[2,1,1024]{2,1,0:T(1,128)S(1)}, f32[2,1,1024]{2,1,0:T(1,128)}, u32[]{:S(2)}) copy-start(f32[2,1,1024]{2,1,0:T(1,128)} %get-tuple-element.29) | copy-start | bytes 24580
  61.9 6.8 %copy-start.5 = (bf16[1024,1024]{1,0:T(8,128)(2,1)S(1)}, bf16[1024,1024]{1,0:T(8,128)(2,1)}, u32[]{:S(2)}) copy-start(bf16[1024,1024]{1,0:T(8,128)(2,1)} %w_out.1) | copy-start | bytes 6291460
  67.9 3.9 %copy-start.16 = (f32[2,1,1024]{2,1,0:T(1,128)S(1)}, f32[2,1,1024]{2,1,0:T(1,128)}, u32[]{:S(2)}) copy-start(f32[2,1,1024]{2,1,0:T(1,128)} %get-tuple-element.26) | copy-start | bytes 24580
  67.9 3.9 %copy-start.13 = (f32[5,1,1024]{2,1,0:T(1,128)S(1)}, f32[5,1,1024]{2,1,0:T(1,128)}, u32[]{:S(2)}) copy-start(f32[5,1,1024]{2,1,0:T(1,128)} %get-tuple-element.27) | copy-start | bytes 61444
  67.9 6.3 %copy-start.17 = (f32[1,1,1024]{2,1,0:T(1,128)S(1)}, f32[1,1,1024]{2,1,0:T(1,128)}, u32[]{:S(2)}) copy-start(f32[1,1,1024]{2,1,0:T(1,128)} %get-tuple-element.28) | copy-start | bytes 12292
  69.0 1.2 collective-permute-start.5
  70.2 3.9 %collective-permute-start.6 = (f32[8,1024]{1,0:T(8,128)S(1)}, f32[8,1024]{1,0:T(8,128)S(1)}, u32[]{:S(2)}, u32[]{:S(2)}) collective-permute-start(f32[8,1024]{1,0:T(8,128)S(1)} %add.64), channel_id=1, source_target_pairs={{0,16},{8,24},{16,0},{24,8},{1,17},{9,25},{17,1},{25,9},{2,18},{10... | collective-permute-start | bytes 98312 | tf_op jit(solution)/shard_map/ppermute | solution.py:24
  74.2 4.9 %collective-permute-start.7 = (f32[1,8,1024]{2,1,0:T(8,128)S(1)}, f32[1,8,1024]{2,1,0:T(8,128)S(1)}, u32[]{:S(2)}, u32[]{:S(2)}) collective-permute-start(f32[1,8,1024]{2,1,0:T(8,128)S(1)} %fusion.1), channel_id=1, source_target_pairs={{0,4},{1,5},{2,6},{3,7},{4,0},{5,1},{6,2},{7,3},{8,12},{9,13},{10,... | collective-permute-start | bytes 98312 | tf_op jit(solution)/shard_map/ppermute | solution.py:24
  79.1 6.5 %collective-permute-start.8 = (f32[2,8,1024]{2,1,0:T(8,128)S(1)}, f32[2,8,1024]{2,1,0:T(8,128)S(1)}, u32[]{:S(2)}, u32[]{:S(2)}) collective-permute-start(f32[2,8,1024]{2,1,0:T(8,128)S(1)} %pad_maximum_fusion.4), channel_id=1, source_target_pairs={{0,2},{1,3},{2,0},{3,1},{4,6},{5,7},{6,4},{7,5},{8,10},{9,11},{10,... | collective-permute-start | bytes 196616 | tf_op jit(solution)/shard_map/ppermute | solution.py:24
  82.5 1.9 %copy-start.8 = (bf16[3072,512]{1,0:T(8,128)(2,1)S(1)}, bf16[3072,512]{1,0:T(8,128)(2,1)}, u32[]{:S(2)}) copy-start(bf16[3072,512]{1,0:T(8,128)(2,1)} %weights.3) | copy-start | bytes 9437188
  84.4 6.8 %copy-start.11 = (f32[4096]{0:T(1024)S(1)}, f32[4096]{0:T(1024)}, u32[]{:S(2)}) copy-start(f32[4096]{0:T(1024)} %param.19) | copy-start | bytes 49156
  84.4 19.5 %copy-start.12 = (s32[8]{0:T(128)S(1)}, s32[8]{0:T(128)}, u32[]{:S(2)}) copy-start(s32[8]{0:T(128)} %lens.7) | copy-start | bytes 100
  84.4 23.1 %copy-start.4 = (bf16[1,1024,1024]{2,1,0:T(8,128)(2,1)S(1)}, bf16[1,1024,1024]{2,1,0:T(8,128)(2,1)}, u32[]{:S(2)}) copy-start(bf16[1,1024,1024]{2,1,0:T(8,128)(2,1)} %get-tuple-element.39.refs_2_) | copy-start | bytes 6291460
  85.4 22.1 %copy-start.2 = (bf16[2,1024,1024]{2,1,0:T(8,128)(2,1)S(1)}, bf16[2,1024,1024]{2,1,0:T(8,128)(2,1)}, u32[]{:S(2)}) copy-start(bf16[2,1024,1024]{2,1,0:T(8,128)(2,1)} %get-tuple-element.37.refs_0_) | copy-start | bytes 12582916
  85.4 1.4 collective-permute-start
  85.5 16.0 %collective-permute-start.9 = (f32[4,8,1024]{2,1,0:T(8,128)S(1)}, f32[4,8,1024]{2,1,0:T(8,128)S(1)}, u32[]{:S(2)}, u32[]{:S(2)}) collective-permute-start(f32[4,8,1024]{2,1,0:T(8,128)S(1)} %pad_maximum_fusion.3), channel_id=1, source_target_pairs={{0,1},{1,0},{2,3},{3,2},{4,5},{5,4},{6,7},{7,6},{8,9},{9,8},{10,11... | collective-permute-start | bytes 393224 | tf_op jit(solution)/shard_map/ppermute | solution.py:24
  86.9 4.3 %collective-permute-start.1 = (bf16[64,512]{1,0:T(8,128)(2,1)S(1)}, bf16[64,512]{1,0:T(8,128)(2,1)S(1)}, u32[]{:S(2)}, u32[]{:S(2)}) collective-permute-start(bf16[64,512]{1,0:T(8,128)(2,1)S(1)} %add_convert_fusion.8.kept), channel_id=1, source_target_pairs={{0,16},{8,24},{16,0},{24,8},{1,17},{9,25},{17,1},{25,9},{2,18},{10... | collective-permute-start | bytes 196616 | tf_op jit(solution)/shard_map/ppermute | solution.py:24
  91.5 3.7 %collective-permute-start.2 = (f32[32,128]{1,0:T(8,128)S(1)}, f32[32,128]{1,0:T(8,128)S(1)}, u32[]{:S(2)}, u32[]{:S(2)}) collective-permute-start(f32[32,128]{1,0:T(8,128)S(1)} %get-tuple-element.25), channel_id=1, source_target_pairs={{0,1},{1,0},{2,3},{3,2},{4,5},{5,4},{6,7},{7,6},{8,9},{9,8},{10,11... | collective-permute-start | bytes 49160 | tf_op jit(solution)/shard_map/ppermute | solution.py:24
  95.3 3.7 %collective-permute-start.3 = (f32[32,128]{1,0:T(8,128)S(1)}, f32[32,128]{1,0:T(8,128)S(1)}, u32[]{:S(2)}, u32[]{:S(2)}) collective-permute-start(f32[32,128]{1,0:T(8,128)S(1)} %add.61), channel_id=1, source_target_pairs={{0,2},{1,3},{2,0},{3,1},{4,6},{5,7},{6,4},{7,5},{8,10},{9,11},{10,... | collective-permute-start | bytes 49160 | tf_op jit(solution)/shard_map/ppermute | solution.py:24
  99.0 4.8 %collective-permute-start.4 = (f32[32,128]{1,0:T(8,128)S(1)}, f32[32,128]{1,0:T(8,128)S(1)}, u32[]{:S(2)}, u32[]{:S(2)}) collective-permute-start(f32[32,128]{1,0:T(8,128)S(1)} %add.62), channel_id=1, source_target_pairs={{0,4},{1,5},{2,6},{3,7},{4,0},{5,1},{6,2},{7,3},{8,12},{9,13},{10,... | collective-permute-start | bytes 49160 | tf_op jit(solution)/shard_map/ppermute | solution.py:24
  103.9 1.6 %copy-start.6 = (bf16[1024,1024]{1,0:T(8,128)(2,1)S(1)}, bf16[1024,1024]{1,0:T(8,128)(2,1)}, u32[]{:S(2)}) copy-start(bf16[1024,1024]{1,0:T(8,128)(2,1)} %w_out.1) | copy-start | bytes 6291460
  107.5 4.0 %copy-start = (bf16[5,1024,1024]{2,1,0:T(8,128)(2,1)S(1)}, bf16[5,1024,1024]{2,1,0:T(8,128)(2,1)}, u32[]{:S(2)}) copy-start(bf16[5,1024,1024]{2,1,0:T(8,128)(2,1)} %get-tuple-element.38.refs_1_) | copy-start | bytes 31457284
  113.8 15.8 %collective-permute-start.10 = (bf16[4,128,512]{2,1,0:T(8,128)(2,1)S(1)}, bf16[4,128,512]{2,1,0:T(8,128)(2,1)}, u32[]{:S(2)}, u32[]{:S(2)}) collective-permute-start(bf16[4,128,512]{2,1,0:T(8,128)(2,1)S(1)} %get-tuple-element.40.refs_3_), channel_id=1, source_target_pairs={{0,1},{1,0},{2,3},{3,2},{4,5},{5,4},{6,7},{7,6},{8,9},{9,8},{10,11... | collective-permute-start | bytes 1572872 | tf_op jit(solution)/shard_map/ppermute | solution.py:24
  114.5 15.1 %collective-permute-start.13 = (bf16[4,128,512]{2,1,0:T(8,128)(2,1)S(1)}, bf16[4,128,512]{2,1,0:T(8,128)(2,1)}, u32[]{:S(2)}, u32[]{:S(2)}) collective-permute-start(bf16[4,128,512]{2,1,0:T(8,128)(2,1)S(1)} %get-tuple-element.41.refs_4_), channel_id=1, source_target_pairs={{0,2},{1,3},{2,0},{3,1},{4,6},{5,7},{6,4},{7,5},{8,10},{9,11},{10,... | collective-permute-start | bytes 1572872 | tf_op jit(solution)/shard_map/ppermute | solution.py:24
  116.4 16.8 %all-to-all-start.3 = ((f32[8,8,640]{2,1,0:T(8,128)}), f32[8,8,640]{2,1,0:T(8,128)S(1)}, u32[]{:S(2)}, u32[]{:S(2)}) async-start(f32[8,8,640]{2,1,0:T(8,128)} %pad_maximum_fusion.2), calls=%async_computation.3 | async-start | bytes 327680 | tf_op jit(solution)/shard_map/all_to_all | solution.py:19
  121.1 4.0 %copy-start.1 = (bf16[5,1024,1024]{2,1,0:T(8,128)(2,1)S(1)}, bf16[5,1024,1024]{2,1,0:T(8,128)(2,1)}, u32[]{:S(2)}) copy-start(bf16[5,1024,1024]{2,1,0:T(8,128)(2,1)} %get-tuple-element.38.refs_1_) | copy-start | bytes 31457284
  125.1 2.2 %copy-start.3 = (bf16[2,1024,1024]{2,1,0:T(8,128)(2,1)S(1)}, bf16[2,1024,1024]{2,1,0:T(8,128)(2,1)}, u32[]{:S(2)}) copy-start(bf16[2,1024,1024]{2,1,0:T(8,128)(2,1)} %get-tuple-element.37.refs_0_) | copy-start | bytes 12582916
  131.1 6.4 %collective-permute-start.14 = (bf16[2,128,512]{2,1,0:T(8,128)(2,1)S(1)}, bf16[2,128,512]{2,1,0:T(8,128)(2,1)S(1)}, u32[]{:S(2)}, u32[]{:S(2)}) collective-permute-start(bf16[2,128,512]{2,1,0:T(8,128)(2,1)S(1)} %get-tuple-element.51), channel_id=1, source_target_pairs={{0,1},{1,0},{2,3},{3,2},{4,5},{5,4},{6,7},{7,6},{8,9},{9,8},{10,11... | collective-permute-start | bytes 786440 | tf_op jit(solution)/shard_map/ppermute | solution.py:24
  134.2 7.8 %collective-permute-start.11 = (bf16[2,128,512]{2,1,0:T(8,128)(2,1)S(1)}, bf16[2,128,512]{2,1,0:T(8,128)(2,1)S(1)}, u32[]{:S(2)}, u32[]{:S(2)}) collective-permute-start(bf16[2,128,512]{2,1,0:T(8,128)(2,1)S(1)} %get-tuple-element.52), channel_id=1, source_target_pairs={{0,2},{1,3},{2,0},{3,1},{4,6},{5,7},{6,4},{7,5},{8,10},{9,11},{10,... | collective-permute-start | bytes 786440 | tf_op jit(solution)/shard_map/ppermute | solution.py:24
  137.6 6.4 %collective-permute-start.15 = (bf16[1,128,512]{2,1,0:T(8,128)(2,1)S(1)}, bf16[1,128,512]{2,1,0:T(8,128)(2,1)S(1)}, u32[]{:S(2)}, u32[]{:S(2)}) collective-permute-start(bf16[1,128,512]{2,1,0:T(8,128)(2,1)S(1)} %add_convert_fusion.4), channel_id=1, source_target_pairs={{0,4},{1,5},{2,6},{3,7},{4,0},{5,1},{6,2},{7,3},{8,12},{9,13},{10,... | collective-permute-start | bytes 393224 | tf_op jit(solution)/shard_map/ppermute | solution.py:24
  142.1 7.3 %collective-permute-start.12 = (bf16[1,128,512]{2,1,0:T(8,128)(2,1)S(1)}, bf16[1,128,512]{2,1,0:T(8,128)(2,1)S(1)}, u32[]{:S(2)}, u32[]{:S(2)}) collective-permute-start(bf16[1,128,512]{2,1,0:T(8,128)(2,1)S(1)} %add_convert_fusion.6), channel_id=1, source_target_pairs={{0,4},{1,5},{2,6},{3,7},{4,0},{5,1},{6,2},{7,3},{8,12},{9,13},{10,... | collective-permute-start | bytes 393224 | tf_op jit(solution)/shard_map/ppermute | solution.py:24

commit v3 on v2

--- a/solution.py
+++ b/solution.py
@@ -41,12 +41,13 @@
     act = (pre_act * half_erf).astype(bf16)
     bell = jnp.exp(-0.5 * pre_act * pre_act)
     slope = (half_erf + pre_act * bell * 0.3989422804014327).astype(bf16)
-    sums = jnp.dot(jnp.ones((8, rows), bf16), act, preferred_element_type=f32)
-    pool_act[0] = sums[:1] / count
+    pool_act[0] = jnp.sum(act.astype(f32), 0, keepdims=True) / count
     product = lax.dot_general(
         tokens, slope, (((0,), (0,)), ((), ())), preferred_element_type=f32
     )
-    grad[0] = product.astype(bf16)
+    half = grad.shape[3]
+    for side in range(grad.shape[1]):
+        grad[0, side] = product[:, side * half : (side + 1) * half].astype(bf16)
 
 
 def student_kernel(first_doc, lens, states, gain, w_in, after, grad, pool_act, pool_x):
@@ -79,18 +80,18 @@
                 pl.BlockSpec(memory_space=pl.ANY),
             ],
             out_specs=[
-                pl.BlockSpec((1, width, hidden), lambda i, n: (i, 0, 0)),
+                pl.BlockSpec((1, 2, width, hidden // 2), lambda i, n: (i, 0, 0, 0)),
                 pl.BlockSpec((1, 1, hidden), lambda i, n: (i, 0, 0)),
                 pl.BlockSpec((1, 1, width), lambda i, n: (i, 0, 0)),
             ],
         ),
         out_shape=[
-            jax.ShapeDtypeStruct((docs, width, hidden), bf16),
+            jax.ShapeDtypeStruct((docs, 2, width, hidden // 2), bf16),
             jax.ShapeDtypeStruct((docs, 1, hidden), f32),
             jax.ShapeDtypeStruct((docs, 1, width), f32),
         ],
         compiler_params=pltpu.CompilerParams(
-            dimension_semantics=("arbitrary",), vmem_limit_bytes=60 << 20
+            dimension_semantics=("arbitrary",), vmem_limit_bytes=59 << 20
         ),
         cost_estimate=pl.CostEstimate(
             flops=3 * docs * seq_len * width * hidden,
@@ -140,7 +141,7 @@
             pltpu.VMEM(weights.shape, bf16),
             pltpu.SemaphoreType.DMA((hidden // block,)),
         ],
-        compiler_params=pltpu.CompilerParams(vmem_limit_bytes=24 << 20),
+        compiler_params=pltpu.CompilerParams(vmem_limit_bytes=59 << 20),
         name="gate_up",
     )(place, columns, gain.reshape(1, -1), weights)
 
@@ -166,33 +167,15 @@
     )(parts, rows)
 
 
-def down_kernel(block, hidden, weights, out, held, arrived):
-    copies = []
-    for i in range(weights.shape[0] // block):
-        here = pl.ds(i * block, block)
-        copies.append(pltpu.make_async_copy(weights.at[here], held.at[here], arrived.at[i]))
-        copies[-1].start()
-    total = None
-    for i, copy in enumerate(copies):
-        copy.wait()
-        here = slice(i * block, (i + 1) * block)
-        part = jnp.dot(hidden[:, here], held[here, :], preferred_element_type=f32)
-        total = part if total is None else total + part
-    out[...] = total
-
-
-def down(hidden, weights, block):
-    vmem = pl.BlockSpec(memory_space=pltpu.VMEM)
-    return pl.pallas_call(
-        functools.partial(down_kernel, block),
-        in_specs=[vmem, pl.BlockSpec(memory_space=pltpu.HBM)],
-        out_specs=vmem,
+def down_kernel(hidden, weights, out):
+    out[...] = jnp.dot(hidden[...], weights[...], preferred_element_type=f32)
+
+
+def down(hidden, weights):
+    return pl.pallas_call(
+        down_kernel,
         out_shape=jax.ShapeDtypeStruct((hidden.shape[0], weights.shape[1]), f32),
-        scratch_shapes=[
-            pltpu.VMEM(weights.shape, bf16),
-            pltpu.SemaphoreType.DMA((weights.shape[0] // block,)),
-        ],
-        compiler_params=pltpu.CompilerParams(vmem_limit_bytes=20 << 20),
+        compiler_params=pltpu.CompilerParams(vmem_limit_bytes=12 << 20),
         name="down",
     )(hidden, weights)
 
@@ -268,9 +251,71 @@
     )(place, blocks)
 
 
-def contrast_kernel(place, lens, gram_sum, logits, unit, norms, w_out, *refs):
-    loss, low, scale, raw = refs[-4:]
-    gram = gram_sum[...]
+def relative(order, step):
+    return sum(((step >> (len(order) - 1 - k)) & 1) << bit for k, bit in enumerate(order))
+
+
+def fetch(plan, place, grads, held, arrived):
+    orders, first = plan
+    rows = held[0].shape[-2]
+    copies = []
+    for side, order in enumerate(orders):
+        for i in range(held[0].shape[1]):
+            member = place[0] ^ relative(order, first + i)
+            here = pl.ds(pl.multiple_of(member * rows, rows), rows)
+            group = [
+                pltpu.make_async_copy(
+                    grad.at[:, side, here, :],
+                    buffer.at[side, i],
+                    arrived.at[part, side, i],
+                )
+                for part, (grad, buffer) in enumerate(zip(grads, held))
+            ]
+            for copy in group:
+                copy.start()
+            copies.append((side, i, group))
+    return copies
+
+
+def weigh_fetched(copies, scale, held, outs):
+    half, rows = held[0].shape[-1], held[0].shape[-2]
+    lines = 16
+    for side, i, group in copies:
+        for copy in group:
+            copy.wait()
+        factors = scale[:, side * half : (side + 1) * half]
+
+        def step(line, carry, side=side, i=i, factors=factors):
+            here = pl.ds(pl.multiple_of(line * lines, lines), lines)
+            total, doc = None, 0
+            for buffer in held:
+                for j in range(buffer.shape[2]):
+                    term = buffer[side, i, j, here, :].astype(f32) * factors[doc : doc + 1]
+                    total = term if total is None else total + term
+                    doc += 1
+            outs[side][i, here, :] = total.astype(bf16)
+            return carry
+
+        lax.fori_loop(0, rows // lines, step, 0)
+
+
+def block_shapes(grads, members):
+    width, half = grads[0].shape[2:]
+    rows, count = width // members, members // 2
+    buffers = [pltpu.VMEM((2, count, grad.shape[0], rows, half), bf16) for grad in grads]
+    arrived = pltpu.SemaphoreType.DMA((len(grads), 2, count))
+    return buffers, arrived, [jax.ShapeDtypeStruct((count, rows, half), bf16)] * 2
+
+
+def contrast_kernel(plan, place, lens, gram_kept, gram_arrived, logits, unit, norms, w_out, *refs):
+    parts = (len(refs) - 9) // 2
+    grads, refs = refs[:parts], refs[parts:]
+    (loss, low, scale), outs, (raw, weights), refs = refs[:3], refs[3:5], refs[5:7], refs[7:]
+    held, (weights_here, arrived) = refs[:-2], refs[-2:]
+    copy = pltpu.make_async_copy(w_out, weights, weights_here)
+    copy.start()
+    copies = fetch(plan, place, grads, held, arrived)
+    gram = gram_kept[...] + gram_arrived[...]
     docs = logits.shape[0]
     if gram.shape[1] != docs:
         gram = jnp.concatenate(
@@ -307,79 +352,55 @@
     low[...] = raw_low
     raw[...] = raw_low.astype(f32)
     mine = raw[pl.ds(pl.multiple_of(place[0] * scale.shape[0], scale.shape[0]), scale.shape[0]), :]
+    copy.wait()
     pool_grad = lax.dot_general(
-        mine.astype(bf16), w_out[...], (((1,), (1,)), ((), ())), preferred_element_type=f32
+        mine.astype(bf16), weights[...], (((1,), (1,)), ((), ())), preferred_element_type=f32
     )
     for doc in range(scale.shape[0]):
         scale[doc : doc + 1, :] = pool_grad[doc : doc + 1, :] / lens[doc].astype(f32)
-
-
-def contrast(place, lengths, gram_sum, logits, unit, norms, w_out, *after):
+    weigh_fetched(copies, scale, held, outs)
+
+
+def contrast(place, lengths, gram_kept, gram_arrived, logits, unit, norms, w_out, grads, orders, members):
     total_docs, width = unit.shape
     local_docs, hidden = lengths.shape[0], w_out.shape[0]
+    buffers, arrived, sums = block_shapes(grads, members)
     vmem, smem = pl.BlockSpec(memory_space=pltpu.VMEM), pl.BlockSpec(memory_space=pltpu.SMEM)
-    return pl.pallas_call(
-        contrast_kernel,
-        in_specs=[smem] * 2 + [vmem] * 5 + [pl.BlockSpec(memory_space=pl.ANY)] * len(after),
-        out_specs=[vmem] * 3,
+    hbm = pl.BlockSpec(memory_space=pltpu.HBM)
+    return pl.pallas_call(
+        functools.partial(contrast_kernel, (orders, members // 2)),
+        in_specs=[smem] * 2 + [vmem] * 5 + [hbm] * (1 + len(grads)),
+        out_specs=[vmem] * 5,
         out_shape=[
             jax.ShapeDtypeStruct((1, 1), f32),
             jax.ShapeDtypeStruct((total_docs, width), bf16),
             jax.ShapeDtypeStruct((local_docs, hidden), f32),
-        ],
-        scratch_shapes=[pltpu.VMEM((total_docs, width), f32)],
-        compiler_params=pltpu.CompilerParams(vmem_limit_bytes=20 << 20),
+        ]
+        + sums,
+        scratch_shapes=[pltpu.VMEM((total_docs, width), f32), pltpu.VMEM(w_out.shape, bf16)]
+        + buffers
+        + [pltpu.SemaphoreType.DMA, arrived],
+        compiler_params=pltpu.CompilerParams(vmem_limit_bytes=50 << 20),
         name="contrast",
-    )(place, lengths, gram_sum, logits, unit, norms, w_out, *after)
-
-
-def relative(order, bits, step):
-    return sum(((step >> (bits - 1 - k)) & 1) << bit for k, bit in enumerate(order))
-
-
-def weigh_kernel(orders, bits, first, parts, place, scale, *refs):
-    grads, outs = refs[:parts], refs[-2:]
-    half, rows, group = scale.shape[1] // 2, outs[0].shape[1], 16
-    for side in range(2):
-        here = pl.ds(side * half, half)
-        factors = scale[:, side * half : (side + 1) * half]
-        member = place[0] ^ relative(orders[side], bits, first + pl.program_id(0))
-        start = pl.multiple_of(member * rows, rows)
-
-        def step(i, carry, side=side, here=here, factors=factors, start=start):
-            near = pl.multiple_of(i * group, group)
-            total, doc = None, 0
-            for grad in grads:
-                for j in range(grad.shape[0]):
-                    value = grad[j, pl.ds(start + near, group), here].astype(f32)
-                    term = value * factors[doc : doc + 1]
-                    total = term if total is None else total + term
-                    doc += 1
-            outs[side][0, pl.ds(near, group), :] = total.astype(bf16)
-            return carry
-
-        lax.fori_loop(0, rows // group, step, 0)
-
-
-def weigh(place, scale, grads, orders, members, first, after=()):
-    width, hidden = grads[0].shape[1:]
-    bits = members.bit_length() - 1
-    rows, half = width // members, hidden // 2
-    vmem = pl.BlockSpec(memory_space=pltpu.VMEM)
-    return pl.pallas_call(
-        functools.partial(weigh_kernel, orders, bits, first, len(grads)),
-        grid_spec=pltpu.PrefetchScalarGridSpec(
-            num_scalar_prefetch=1,
-            grid=(members // 2,),
-            in_specs=[pl.BlockSpec(scale.shape, lambda i, p: (0, 0))]
-            + [vmem] * len(grads)
-            + [pl.BlockSpec(memory_space=pl.ANY)] * len(after),
-            out_specs=[pl.BlockSpec((1, rows, half), lambda i, p: (i, 0, 0))] * 2,
-        ),
-        out_shape=[jax.ShapeDtypeStruct((members // 2, rows, half), bf16)] * 2,
-        compiler_params=pltpu.CompilerParams(
-            dimension_semantics=("arbitrary",), vmem_limit_bytes=24 << 20
-        ),
+    )(place, lengths, gram_kept, gram_arrived, logits, unit, norms, w_out, *grads)
+
+
+def weigh_kernel(plan, parts, place, scale, *refs):
+    grads, outs, held, arrived = refs[:parts], refs[-3 - parts : -1 - parts], refs[-1 - parts : -1], refs[-1]
+    weigh_fetched(fetch(plan, place, grads, held, arrived), scale, held, outs)
+
+
+def weigh(place, scale, grads, orders, members, after):
+    buffers, arrived, sums = block_shapes(grads, members)
+    vmem, smem = pl.BlockSpec(memory_space=pltpu.VMEM), pl.BlockSpec(memory_space=pltpu.SMEM)
+    hbm, kept = pl.BlockSpec(memory_space=pltpu.HBM), pl.BlockSpec(memory_space=pl.ANY)
+    return pl.pallas_call(
+        functools.partial(weigh_kernel, (orders, 0), len(grads)),
+        in_specs=[smem, vmem] + [hbm] * len(grads) + [kept] * len(after),
+        out_specs=[vmem] * 2,
+        out_shape=sums,
+        scratch_shapes=buffers + [arrived],
+        compiler_params=pltpu.CompilerParams(vmem_limit_bytes=50 << 20),
         name="weigh",
     )(place, scale, *grads, *after)
 
@@ -419,19 +440,18 @@
     student = functools.partial(
         student_part, lengths, student_states, student_ln_gain, student_w_in
     )
-    cuts = (0, local_docs // 4, local_docs - local_docs // 8, local_docs)
+    early = local_docs // 4
 
     blocks = teacher_rows.reshape(local_docs, dp_count, col_width).transpose(1, 0, 2)
     columns = exchange(blocks, "dp").reshape(total_docs, col_width)
-    first = student(teacher_rows, cuts[0], cuts[1] - cuts[0])
+    first = student(teacher_rows, 0, early)
     parts = gate_up(place, columns, teacher_mlp_gain, teacher_gate_up, block)
     parts = parts.reshape(dp_count, local_docs, 2 * hidden_width)
-    second = student(parts, cuts[1], cuts[2] - cuts[1])
+    second = student(parts, early, local_docs - early)
     parts = exchange(parts, "dp")
     hidden = hidden_units(parts, teacher_rows, block)
-    third = student(hidden, cuts[2], cuts[3] - cuts[2])
     every_hidden = exchange(hidden, "dp").reshape(total_docs, hidden_width)
-    out = down(every_hidden, teacher_down, block)
+    out = down(every_hidden, teacher_down)
     for bit in range(section_count.bit_length() - 1):
         kept = out if bit == 0 else out.astype(bf16)
         arrived = swap(kept, "section", bit)
@@ -439,9 +459,11 @@
     states_block, gram_sum = teacher_block(place, kept, arrived, columns, teacher_final_gain)
     bits = dp_count.bit_length() - 1
     for bit in range(bits):
-        gram_sum = gram_sum + swap(gram_sum, "dp", bit)
-
-    grads, acts, states = zip(first, second, third)
+        gram_kept = gram_sum
+        gram_arrived = swap(gram_sum, "dp", bit)
+        gram_sum = gram_kept + gram_arrived
+
+    grads, acts, states = zip(first, second)
     pooled_act = jnp.concatenate(acts)[:, 0].astype(bf16)
     pooled_x = jnp.concatenate(states)[:, 0]
     emb_sum = jnp.dot(pooled_act, student_w_out, preferred_element_type=f32)
@@ -452,13 +474,22 @@
     for bit in far_first:
         every_raw = jnp.concatenate([every_raw, swap(every_raw, "dp", bit)])
     unit, norms, student_logits = embed(place, every_raw, far_first)
-    loss, every_low, scale = contrast(
-        place, lengths, gram_sum, student_logits, unit, norms, student_w_out
-    )
-
     orders = (tuple(range(bits)), (1, 0) + tuple(range(2, bits)))
-    sent = weigh(place, scale, grads, orders, dp_count, dp_count // 2)
-    kept = weigh(place, scale, grads, orders, dp_count, 0, sent)
+    loss, every_low, scale, *sent = contrast(
+        place,
+        lengths,
+        gram_kept,
+        gram_arrived,
+        student_logits,
+        unit,
+        norms,
+        student_w_out,
+        grads,
+        orders,
+        dp_count,
+    )
+
+    kept = weigh(place, scale, grads, orders, dp_count, sent)
     sides = []
     for side in range(2):
         sides.append(halving(sent[side], kept[side], orders[side], "dp"))

time: 151 us -> 136 us (0.901)
  local copies, waits for them, and re-layouts: 17.8 us -> 3.19 us
  waiting for transfers between devices: 31.4 us -> 37.9 us
  starting transfers between devices: 49.7 us -> 46 us
  Pallas kernels: 45 us -> 42.9 us
    unnamed x36 -> x20, local copies, waits for them, and re-layouts: 17.2 us -> 2.56 us
    pallas_call x3 -> x2, Pallas kernels: 32 us -> 26.5 us  [student_part(): pl.pallas_call(functools.partial(student_kernel, first_doc), grid_spec=pl...]
    ppermute x16, starting transfers between devices: 24.8 us -> 20.7 us  [swap(): lax.ppermute(value, axis, [(i, i ^ 1 << bit) for i in range(members)])]
    ppermute x16, waiting for transfers between devices: 24.5 us -> 27.8 us  [swap(): lax.ppermute(value, axis, [(i, i ^ 1 << bit) for i in range(members)])]
    all_to_all x4, waiting for transfers between devices: 6.91 us -> 10.1 us  [exchange(): return lax.all_to_all(blocks, axis, 0, 0, tiled=True)]
    pallas_call x4 -> x3, Pallas kernels: 7.69 us -> 9.72 us  [the longest x1 5.24 us: contrast(): pl.pallas_call(functools.partial(contrast_kernel, (orders, members // 2))...]
  transfers between devices with their start and end apart: 20 -> 20, of which waited for: 12 -> 14; matrix products, arithmetic and copies ran while one was open for 3% -> 3% of each run, Pallas kernels for 24% -> 24%
where the time goes in v3:
time: 136 us; the launch traced here: 135 us
  starting transfers between devices  46 us (34%)
  Pallas kernels  42.9 us (32%)
  waiting for transfers between devices  37.9 us (28%)
  local copies, waits for them, and re-layouts  3.19 us (2%)
  other arithmetic  2.84 us (2%)
  matrix products  1.43 us (1%)
    ppermute x16, waiting for transfers between devices, swap(): lax.ppermute(value, axis, [(i, i ^ 1 << bit) for i in range(members)])  27.8 us
    pallas_call x2, Pallas kernels, student_part(): pl.pallas_call(functools.partial(student_kernel, first_doc), grid_spec=pl...  26.5 us
    all_to_all x4, starting transfers between devices, exchange(): return lax.all_to_all(blocks, axis, 0, 0, tiled=True)  25.3 us
    ppermute x16, starting transfers between devices, swap(): lax.ppermute(value, axis, [(i, i ^ 1 << bit) for i in range(members)])  20.7 us
    all_to_all x4, waiting for transfers between devices, exchange(): return lax.all_to_all(blocks, axis, 0, 0, tiled=True)  10.1 us
    pallas_call x1, Pallas kernels, contrast(): pl.pallas_call(functools.partial(contrast_kernel, (orders, members // 2))...  5.24 us
    pallas_call x1, Pallas kernels, gate_up(): pl.pallas_call(functools.partial(gate_up_kernel, block), in_specs=[pl.Blo...  4.93 us
    pallas_call x1, Pallas kernels, weigh(): pl.pallas_call(functools.partial(weigh_kernel, (orders, 0), len(grads)),...  3.82 us
  transfers between devices with their start and end apart: 20, of which 14 were waited for; matrix products, arithmetic and copies ran while one was open for 3% of the time, Pallas kernels for 24%

profile of v3, /device:TPU:0, one launch (start us, length us, event | category | flops | bytes accessed | tf_op | source)
XLA Modules:
  0.0 135.1 jit_solution(8346263249635097971)
XLA Ops:
  0.6 7.3 %all-to-all-start = ((bf16[8,8,512]{2,1,0:T(8,128)(2,1)}), bf16[8,8,512]{2,1,0:T(8,128)(2,1)S(1)}, u32[]{:S(2)}, u32[]{:S(2)}) async-start(bf16[8,8,512]{2,1,0:T(8,128)(2,1)} %bitcast.41), calls=%async_computation | async-start | bytes 131072 | tf_op jit(solution)/shard_map/all_to_all | solution.py:19
  8.0 6.9 %all-to-all-done = bf16[8,8,512]{2,1,0:T(8,128)(2,1)S(1)} async-done(((bf16[8,8,512]{2,1,0:T(8,128)(2,1)}), bf16[8,8,512]{2,1,0:T(8,128)(2,1)S(1)}, u32[]{:S(2)}, u32[]{:S(2)}) %all-to-all-start) | async-done | bytes 65568 | tf_op jit(solution)/shard_map/all_to_all | solution.py:19
  14.9 0.6 copy-done.2
  15.5 4.9 %gate_up.1 = bf16[64,6144]{1,0:T(8,128)(2,1)} custom-call(s32[1]{0:T(128)} %bitcast.place, bf16[64,512]{1,0:T(8,128)(2,1)} %bitcast.39, f32[1,4096]{1,0:T(1,128)} %bitcast.48, bf16[2,512,3072]{2,1,0:T(8,128)(2,1)} %weights.2), custom_call_target="tpu_custom_call" | custom-call | tf_op jit(solution)/shard_map/gate_up/pallas_call | solution.py:130
  20.4 3.6 %all-to-all-start.1 = ((bf16[8,8,6144]{2,1,0:T(8,128)(2,1)}), bf16[8,8,6144]{2,1,0:T(8,128)(2,1)S(1)}, u32[]{:S(2)}, u32[]{:S(2)}) async-start(bf16[8,8,6144]{2,1,0:T(8,128)(2,1)} %bitcast.44), calls=%async_computation.1 | async-start | bytes 1572864 | tf_op jit(solution)/shard_map/all_to_all | solution.py:19
  24.0 8.7 %student.2 = (bf16[2,2,1024,512]{3,2,1,0:T(8,128)(2,1)}, f32[2,1,1024]{2,1,0:T(1,128)}, f32[2,1,1024]{2,1,0:T(1,128)}) custom-call(s32[8]{0:T(128)} %lens.5, bf16[8,512,1024]{2,1,0:T(8,128)(2,1)} %states.3, f32[1,1024]{1,0:T(1,128)} %bitcast.49, bf16[1024,1024]{1,0:T(8,128)(2,1)} %w_in.3, bf16[8,4096]{1,0:T(8,128)(2,1)} %after.1), custom_call_target="tpu_custom_call" | custom-call | flops 3221225472 | bytes 6291456 | tf_op jit(solution)/shard_map/student/pallas_call | solution.py:71
  32.7 17.7 %student.3 = (bf16[6,2,1024,512]{3,2,1,0:T(8,128)(2,1)}, f32[6,1,1024]{2,1,0:T(1,128)}, f32[6,1,1024]{2,1,0:T(1,128)}) custom-call(s32[8]{0:T(128)} %lens.5, bf16[8,512,1024]{2,1,0:T(8,128)(2,1)} %states.3, f32[1,1024]{1,0:T(1,128)} %bitcast.50, bf16[1024,1024]{1,0:T(8,128)(2,1)} %w_in.3, bf16[8,8,6144]{2,1,0:T(8,128)(2,1)} %bitcast.45), custom_call_target="tpu_custom_call" | custom-call | flops 9663676416 | bytes 18874368 | tf_op jit(solution)/shard_map/student/pallas_call | solution.py:71
  50.5 0.8 fusion.8
  51.3 0.9 hidden.1
  52.2 9.5 %all-to-all-start.2 = ((bf16[8,8,3072]{2,1,0:T(8,128)(2,1)}), bf16[8,8,3072]{2,1,0:T(8,128)(2,1)S(1)}, u32[]{:S(2)}, u32[]{:S(2)}) async-start(bf16[8,8,3072]{2,1,0:T(8,128)(2,1)} %hidden.1), calls=%async_computation.2 | async-start | bytes 786432 | tf_op jit(solution)/shard_map/all_to_all | solution.py:19
  61.8 0.4 fusion.5
  62.2 1.2 collective-permute-done.5
  63.4 1.5 %collective-permute-start.6 = (f32[8,1024]{1,0:T(8,128)S(1)}, f32[8,1024]{1,0:T(8,128)S(1)}, u32[]{:S(2)}, u32[]{:S(2)}) collective-permute-start(f32[8,1024]{1,0:T(8,128)S(1)} %add.60), channel_id=1, source_target_pairs={{0,16},{8,24},{16,0},{24,8},{1,17},{9,25},{17,1},{25,9},{2,18},{10... | collective-permute-start | bytes 98312 | tf_op jit(solution)/shard_map/ppermute | solution.py:24
  64.9 2.4 %collective-permute-done.6 = f32[8,1024]{1,0:T(8,128)S(1)} collective-permute-done((f32[8,1024]{1,0:T(8,128)S(1)}, f32[8,1024]{1,0:T(8,128)S(1)}, u32[]{:S(2)}, u32[]{:S(2)}) %collective-permute-start.6) | collective-permute-done | bytes 32800 | tf_op jit(solution)/shard_map/ppermute | solution.py:24
  67.3 3.0 %collective-permute-start.7 = (f32[1,8,1024]{2,1,0:T(8,128)S(1)}, f32[1,8,1024]{2,1,0:T(8,128)S(1)}, u32[]{:S(2)}, u32[]{:S(2)}) collective-permute-start(f32[1,8,1024]{2,1,0:T(8,128)S(1)} %fusion.1), channel_id=1, source_target_pairs={{0,4},{1,5},{2,6},{3,7},{4,0},{5,1},{6,2},{7,3},{8,12},{9,13},{10,... | collective-permute-start | bytes 98312 | tf_op jit(solution)/shard_map/ppermute | solution.py:24
  70.3 2.5 %collective-permute-done.7 = f32[1,8,1024]{2,1,0:T(8,128)S(1)} collective-permute-done((f32[1,8,1024]{2,1,0:T(8,128)S(1)}, f32[1,8,1024]{2,1,0:T(8,128)S(1)}, u32[]{:S(2)}, u32[]{:S(2)}) %collective-permute-start.7) | collective-permute-done | bytes 32800 | tf_op jit(solution)/shard_map/ppermute | solution.py:24
  72.8 1.4 %collective-permute-start.8 = (f32[2,8,1024]{2,1,0:T(8,128)S(1)}, f32[2,8,1024]{2,1,0:T(8,128)S(1)}, u32[]{:S(2)}, u32[]{:S(2)}) collective-permute-start(f32[2,8,1024]{2,1,0:T(8,128)S(1)} %pad_maximum_fusion.4), channel_id=1, source_target_pairs={{0,2},{1,3},{2,0},{3,1},{4,6},{5,7},{6,4},{7,5},{8,10},{9,11},{10,... | collective-permute-start | bytes 196616 | tf_op jit(solution)/shard_map/ppermute | solution.py:24
  74.3 1.9 %copy-done.1 = bf16[3072,512]{1,0:T(8,128)(2,1)S(1)} copy-done((bf16[3072,512]{1,0:T(8,128)(2,1)S(1)}, bf16[3072,512]{1,0:T(8,128)(2,1)}, u32[]{:S(2)}) %copy-start.1) | copy-done | bytes 3145752
  76.1 0.7 down.1
  76.9 0.2 collective-permute-done.8
  77.1 1.5 %collective-permute-start.9 = (f32[4,8,1024]{2,1,0:T(8,128)S(1)}, f32[4,8,1024]{2,1,0:T(8,128)S(1)}, u32[]{:S(2)}, u32[]{:S(2)}) collective-permute-start(f32[4,8,1024]{2,1,0:T(8,128)S(1)} %pad_maximum_fusion.3), channel_id=1, source_target_pairs={{0,1},{1,0},{2,3},{3,2},{4,5},{5,4},{6,7},{7,6},{8,9},{9,8},{10,11... | collective-permute-start | bytes 393224 | tf_op jit(solution)/shard_map/ppermute | solution.py:24
  78.7 1.5 %collective-permute-start.1 = (bf16[64,512]{1,0:T(8,128)(2,1)S(1)}, bf16[64,512]{1,0:T(8,128)(2,1)S(1)}, u32[]{:S(2)}, u32[]{:S(2)}) collective-permute-start(bf16[64,512]{1,0:T(8,128)(2,1)S(1)} %add_convert_fusion.8.kept), channel_id=1, source_target_pairs={{0,16},{8,24},{16,0},{24,8},{1,17},{9,25},{17,1},{25,9},{2,18},{10... | collective-permute-start | bytes 196616 | tf_op jit(solution)/shard_map/ppermute | solution.py:24
  80.2 2.8 %collective-permute-done.1.arrived = bf16[64,512]{1,0:T(8,128)(2,1)S(1)} collective-permute-done((bf16[64,512]{1,0:T(8,128)(2,1)S(1)}, bf16[64,512]{1,0:T(8,128)(2,1)S(1)}, u32[]{:S(2)}, u32[]{:S(2)}) %collective-permute-start.1) | collective-permute-done | bytes 65568 | tf_op jit(solution)/shard_map/ppermute | solution.py:24
  83.0 0.3 teacher_block.1
  83.3 1.1 collective-permute-start.2
  84.4 2.7 %collective-permute-done.2 = f32[32,128]{1,0:T(8,128)S(1)} collective-permute-done((f32[32,128]{1,0:T(8,128)S(1)}, f32[32,128]{1,0:T(8,128)S(1)}, u32[]{:S(2)}, u32[]{:S(2)}) %collective-permute-start.2) | collective-permute-done | bytes 16416 | tf_op jit(solution)/shard_map/ppermute | solution.py:24
  87.1 1.4 %collective-permute-start.3 = (f32[32,128]{1,0:T(8,128)S(1)}, f32[32,128]{1,0:T(8,128)S(1)}, u32[]{:S(2)}, u32[]{:S(2)}) collective-permute-start(f32[32,128]{1,0:T(8,128)S(1)} %add.58), channel_id=1, source_target_pairs={{0,2},{1,3},{2,0},{3,1},{4,6},{5,7},{6,4},{7,5},{8,10},{9,11},{10,... | collective-permute-start | bytes 49160 | tf_op jit(solution)/shard_map/ppermute | solution.py:24
  88.5 2.3 %collective-permute-done.3 = f32[32,128]{1,0:T(8,128)S(1)} collective-permute-done((f32[32,128]{1,0:T(8,128)S(1)}, f32[32,128]{1,0:T(8,128)S(1)}, u32[]{:S(2)}, u32[]{:S(2)}) %collective-permute-start.3) | collective-permute-done | bytes 16416 | tf_op jit(solution)/shard_map/ppermute | solution.py:24
  90.8 2.5 %collective-permute-start.4 = (f32[32,128]{1,0:T(8,128)S(1)}, f32[32,128]{1,0:T(8,128)S(1)}, u32[]{:S(2)}, u32[]{:S(2)}) collective-permute-start(f32[32,128]{1,0:T(8,128)S(1)} %add.59.gram_kept), channel_id=1, source_target_pairs={{0,4},{1,5},{2,6},{3,7},{4,0},{5,1},{6,2},{7,3},{8,12},{9,13},{10,... | collective-permute-start | bytes 49160 | tf_op jit(solution)/shard_map/ppermute | solution.py:24
  93.4 0.5 embed.1
  93.9 1.6 %collective-permute-done.4.gram_arrived = f32[32,128]{1,0:T(8,128)S(1)} collective-permute-done((f32[32,128]{1,0:T(8,128)S(1)}, f32[32,128]{1,0:T(8,128)S(1)}, u32[]{:S(2)}, u32[]{:S(2)}) %collective-permute-start.4) | collective-permute-done | bytes 16416 | tf_op jit(solution)/shard_map/ppermute | solution.py:24
  95.5 5.2 %contrast.1 = (f32[1,1]{1,0:T(1,128)}, bf16[64,1024]{1,0:T(8,128)(2,1)S(1)}, f32[8,1024]{1,0:T(8,128)S(1)}, bf16[4,128,512]{2,1,0:T(8,128)(2,1)S(1)}, bf16[4,128,512]{2,1,0:T(8,128)(2,1)S(1)}) custom-call(s32[1]{0:T(128)} %bitcast.place, s32[8]{0:T(128)S(1)} %copy-done.6, f32[32,128]{1,0:T(8,128)S(1)} %add.59.gram_kept, ...), custom_call_target="tpu_custom_call" | custom-call | tf_op jit(solution)/shard_map/contrast/pallas_call | solution.py:370
  100.7 1.1 collective-permute-start.10
  101.9 0.9 collective-permute-start.13
  102.8 0.7 pad_maximum_fusion.2
  103.5 4.9 %all-to-all-start.3 = ((f32[8,8,640]{2,1,0:T(8,128)}), f32[8,8,640]{2,1,0:T(8,128)S(1)}, u32[]{:S(2)}, u32[]{:S(2)}) async-start(f32[8,8,640]{2,1,0:T(8,128)} %pad_maximum_fusion.2), calls=%async_computation.3 | async-start | bytes 327680 | tf_op jit(solution)/shard_map/all_to_all | solution.py:19
  108.4 3.8 %weigh.1 = (bf16[4,128,512]{2,1,0:T(8,128)(2,1)S(1)}, bf16[4,128,512]{2,1,0:T(8,128)(2,1)S(1)}) custom-call(s32[1]{0:T(128)} %bitcast.place, f32[8,1024]{1,0:T(8,128)S(1)} %get-tuple-element.33.scale, bf16[2,2,1024,512]{3,2,1,0:T(8,128)(2,1)} %get-tuple-element.30.refs_0_, bf16[6,2,1024,512]{3,2,1,0:T(8,128)(2,1)} %get-tuple-element.31.refs_1_, ...), custom_call_target="tpu_custom_call" | custom-call | tf_op jit(solution)/shard_map/weigh/pallas_call | solution.py:397
  112.3 0.5 collective-permute-done.13
  112.8 0.3 add_convert_fusion.1
  113.1 1.5 %collective-permute-start.14 = (bf16[2,128,512]{2,1,0:T(8,128)(2,1)S(1)}, bf16[2,128,512]{2,1,0:T(8,128)(2,1)S(1)}, u32[]{:S(2)}, u32[]{:S(2)}) collective-permute-start(bf16[2,128,512]{2,1,0:T(8,128)(2,1)S(1)} %get-tuple-element.45), channel_id=1, source_target_pairs={{0,1},{1,0},{2,3},{3,2},{4,5},{5,4},{6,7},{7,6},{8,9},{9,8},{10,11... | collective-permute-start | bytes 786440 | tf_op jit(solution)/shard_map/ppermute | solution.py:24
  114.6 3.2 %all-to-all-done.3 = f32[8,8,640]{2,1,0:T(8,128)S(1)} async-done(((f32[8,8,640]{2,1,0:T(8,128)}), f32[8,8,640]{2,1,0:T(8,128)S(1)}, u32[]{:S(2)}, u32[]{:S(2)}) %all-to-all-start.3) | async-done | bytes 163872 | tf_op jit(solution)/shard_map/all_to_all | solution.py:19
  117.8 1.0 fusion.3
  118.8 0.4 collective-permute-start.11
  119.3 0.6 constant_dynamic-slice_fusion
  119.9 2.5 %collective-permute-start.15 = (bf16[1,128,512]{2,1,0:T(8,128)(2,1)S(1)}, bf16[1,128,512]{2,1,0:T(8,128)(2,1)S(1)}, u32[]{:S(2)}, u32[]{:S(2)}) collective-permute-start(bf16[1,128,512]{2,1,0:T(8,128)(2,1)S(1)} %add_convert_fusion.4), channel_id=1, source_target_pairs={{0,4},{1,5},{2,6},{3,7},{4,0},{5,1},{6,2},{7,3},{8,12},{9,13},{10,... | collective-permute-start | bytes 393224 | tf_op jit(solution)/shard_map/ppermute | solution.py:24
  122.4 5.4 %collective-permute-done.11 = bf16[2,128,512]{2,1,0:T(8,128)(2,1)S(1)} collective-permute-done((bf16[2,128,512]{2,1,0:T(8,128)(2,1)S(1)}, bf16[2,128,512]{2,1,0:T(8,128)(2,1)S(1)}, u32[]{:S(2)}, u32[]{:S(2)}) %collective-permute-start.11) | collective-permute-done | bytes 262176 | tf_op jit(solution)/shard_map/ppermute | solution.py:24
  128.0 6.2 %collective-permute-done.12 = bf16[1,128,512]{2,1,0:T(8,128)(2,1)S(1)} collective-permute-done((bf16[1,128,512]{2,1,0:T(8,128)(2,1)S(1)}, bf16[1,128,512]{2,1,0:T(8,128)(2,1)S(1)}, u32[]{:S(2)}, u32[]{:S(2)}) %collective-permute-start.12) | collective-permute-done | bytes 131104 | tf_op jit(solution)/shard_map/ppermute | solution.py:24
  134.2 0.8 pad_maximum_fusion
  (43 shorter events, 0.5 us)
Async XLA Ops:
  0.6 14.2 %all-to-all-start = ((bf16[8,8,512]{2,1,0:T(8,128)(2,1)}), bf16[8,8,512]{2,1,0:T(8,128)(2,1)S(1)}, u32[]{:S(2)}, u32[]{:S(2)}) async-start(bf16[8,8,512]{2,1,0:T(8,128)(2,1)} %bitcast.41), calls=%async_computation | async-start | bytes 131072 | tf_op jit(solution)/shard_map/all_to_all | solution.py:19
  14.9 0.6 copy-start.2
  20.4 30.9 %all-to-all-start.1 = ((bf16[8,8,6144]{2,1,0:T(8,128)(2,1)}), bf16[8,8,6144]{2,1,0:T(8,128)(2,1)S(1)}, u32[]{:S(2)}, u32[]{:S(2)}) async-start(bf16[8,8,6144]{2,1,0:T(8,128)(2,1)} %bitcast.44), calls=%async_computation.1 | async-start | bytes 1572864 | tf_op jit(solution)/shard_map/all_to_all | solution.py:19
  32.7 17.8 %copy-start.8 = (f32[2,1,1024]{2,1,0:T(1,128)S(1)}, f32[2,1,1024]{2,1,0:T(1,128)}, u32[]{:S(2)}) copy-start(f32[2,1,1024]{2,1,0:T(1,128)} %get-tuple-element.25) | copy-start | bytes 24580
  32.7 18.6 %copy-start.4 = (bf16[8,4096]{1,0:T(8,128)(2,1)S(1)}, bf16[8,4096]{1,0:T(8,128)(2,1)}, u32[]{:S(2)}) copy-start(bf16[8,4096]{1,0:T(8,128)(2,1)} %after.1) | copy-start | bytes 196612
  32.7 29.1 %copy-start = (bf16[1024,1024]{1,0:T(8,128)(2,1)S(1)}, bf16[1024,1024]{1,0:T(8,128)(2,1)}, u32[]{:S(2)}) copy-start(bf16[1024,1024]{1,0:T(8,128)(2,1)} %w_out.1) | copy-start | bytes 6291460
  50.5 14.4 %copy-start.9 = (f32[2,1,1024]{2,1,0:T(1,128)S(1)}, f32[2,1,1024]{2,1,0:T(1,128)}, u32[]{:S(2)}) copy-start(f32[2,1,1024]{2,1,0:T(1,128)} %get-tuple-element.23) | copy-start | bytes 24580
  50.5 14.5 %copy-start.7 = (f32[6,1,1024]{2,1,0:T(1,128)S(1)}, f32[6,1,1024]{2,1,0:T(1,128)}, u32[]{:S(2)}) copy-start(f32[6,1,1024]{2,1,0:T(1,128)} %get-tuple-element.24) | copy-start | bytes 73732
  52.2 22.0 %all-to-all-start.2 = ((bf16[8,8,3072]{2,1,0:T(8,128)(2,1)}), bf16[8,8,3072]{2,1,0:T(8,128)(2,1)S(1)}, u32[]{:S(2)}, u32[]{:S(2)}) async-start(bf16[8,8,3072]{2,1,0:T(8,128)(2,1)} %hidden.1), calls=%async_computation.2 | async-start | bytes 786432 | tf_op jit(solution)/shard_map/all_to_all | solution.py:19
  61.8 21.2 %copy-start.3 = (bf16[8,8,512]{2,1,0:T(8,128)(2,1)S(1)}, bf16[8,8,512]{2,1,0:T(8,128)(2,1)}, u32[]{:S(2)}) copy-start(bf16[8,8,512]{2,1,0:T(8,128)(2,1)} %copy-done.2) | copy-start | bytes 196612
  61.8 21.2 %copy-start.5 = (f32[4096]{0:T(1024)S(1)}, f32[4096]{0:T(1024)}, u32[]{:S(2)}) copy-start(f32[4096]{0:T(1024)} %param.19) | copy-start | bytes 49156
  62.2 33.3 %copy-start.6 = (s32[8]{0:T(128)S(1)}, s32[8]{0:T(128)}, u32[]{:S(2)}) copy-start(s32[8]{0:T(128)} %lens.5) | copy-start | bytes 100
  62.2 1.2 collective-permute-start.5
  63.4 3.9 %collective-permute-start.6 = (f32[8,1024]{1,0:T(8,128)S(1)}, f32[8,1024]{1,0:T(8,128)S(1)}, u32[]{:S(2)}, u32[]{:S(2)}) collective-permute-start(f32[8,1024]{1,0:T(8,128)S(1)} %add.60), channel_id=1, source_target_pairs={{0,16},{8,24},{16,0},{24,8},{1,17},{9,25},{17,1},{25,9},{2,18},{10... | collective-permute-start | bytes 98312 | tf_op jit(solution)/shard_map/ppermute | solution.py:24
  67.3 5.5 %collective-permute-start.7 = (f32[1,8,1024]{2,1,0:T(8,128)S(1)}, f32[1,8,1024]{2,1,0:T(8,128)S(1)}, u32[]{:S(2)}, u32[]{:S(2)}) collective-permute-start(f32[1,8,1024]{2,1,0:T(8,128)S(1)} %fusion.1), channel_id=1, source_target_pairs={{0,4},{1,5},{2,6},{3,7},{4,0},{5,1},{6,2},{7,3},{8,12},{9,13},{10,... | collective-permute-start | bytes 98312 | tf_op jit(solution)/shard_map/ppermute | solution.py:24
  72.8 4.3 %collective-permute-start.8 = (f32[2,8,1024]{2,1,0:T(8,128)S(1)}, f32[2,8,1024]{2,1,0:T(8,128)S(1)}, u32[]{:S(2)}, u32[]{:S(2)}) collective-permute-start(f32[2,8,1024]{2,1,0:T(8,128)S(1)} %pad_maximum_fusion.4), channel_id=1, source_target_pairs={{0,2},{1,3},{2,0},{3,1},{4,6},{5,7},{6,4},{7,5},{8,10},{9,11},{10,... | collective-permute-start | bytes 196616 | tf_op jit(solution)/shard_map/ppermute | solution.py:24
  74.2 1.9 %copy-start.1 = (bf16[3072,512]{1,0:T(8,128)(2,1)S(1)}, bf16[3072,512]{1,0:T(8,128)(2,1)}, u32[]{:S(2)}) copy-start(bf16[3072,512]{1,0:T(8,128)(2,1)} %weights.3) | copy-start | bytes 9437188
  76.8 1.8 %collective-permute-start = (f32[64,512]{1,0:T(8,128)S(1)}, f32[64,512]{1,0:T(8,128)S(1)}, u32[]{:S(2)}, u32[]{:S(2)}) collective-permute-start(f32[64,512]{1,0:T(8,128)S(1)} %down.1), channel_id=1, source_target_pairs={{0,8},{8,0},{16,24},{24,16},{1,9},{9,1},{17,25},{25,17},{2,10},{10... | collective-permute-start | bytes 393224 | tf_op jit(solution)/shard_map/ppermute | solution.py:24
  77.1 16.3 %collective-permute-start.9 = (f32[4,8,1024]{2,1,0:T(8,128)S(1)}, f32[4,8,1024]{2,1,0:T(8,128)S(1)}, u32[]{:S(2)}, u32[]{:S(2)}) collective-permute-start(f32[4,8,1024]{2,1,0:T(8,128)S(1)} %pad_maximum_fusion.3), channel_id=1, source_target_pairs={{0,1},{1,0},{2,3},{3,2},{4,5},{5,4},{6,7},{7,6},{8,9},{9,8},{10,11... | collective-permute-start | bytes 393224 | tf_op jit(solution)/shard_map/ppermute | solution.py:24
  78.7 4.3 %collective-permute-start.1 = (bf16[64,512]{1,0:T(8,128)(2,1)S(1)}, bf16[64,512]{1,0:T(8,128)(2,1)S(1)}, u32[]{:S(2)}, u32[]{:S(2)}) collective-permute-start(bf16[64,512]{1,0:T(8,128)(2,1)S(1)} %add_convert_fusion.8.kept), channel_id=1, source_target_pairs={{0,16},{8,24},{16,0},{24,8},{1,17},{9,25},{17,1},{25,9},{2,18},{10... | collective-permute-start | bytes 196616 | tf_op jit(solution)/shard_map/ppermute | solution.py:24
  83.3 3.7 %collective-permute-start.2 = (f32[32,128]{1,0:T(8,128)S(1)}, f32[32,128]{1,0:T(8,128)S(1)}, u32[]{:S(2)}, u32[]{:S(2)}) collective-permute-start(f32[32,128]{1,0:T(8,128)S(1)} %get-tuple-element.22), channel_id=1, source_target_pairs={{0,1},{1,0},{2,3},{3,2},{4,5},{5,4},{6,7},{7,6},{8,9},{9,8},{10,11... | collective-permute-start | bytes 49160 | tf_op jit(solution)/shard_map/ppermute | solution.py:24
  87.1 3.7 %collective-permute-start.3 = (f32[32,128]{1,0:T(8,128)S(1)}, f32[32,128]{1,0:T(8,128)S(1)}, u32[]{:S(2)}, u32[]{:S(2)}) collective-permute-start(f32[32,128]{1,0:T(8,128)S(1)} %add.58), channel_id=1, source_target_pairs={{0,2},{1,3},{2,0},{3,1},{4,6},{5,7},{6,4},{7,5},{8,10},{9,11},{10,... | collective-permute-start | bytes 49160 | tf_op jit(solution)/shard_map/ppermute | solution.py:24
  90.8 4.6 %collective-permute-start.4 = (f32[32,128]{1,0:T(8,128)S(1)}, f32[32,128]{1,0:T(8,128)S(1)}, u32[]{:S(2)}, u32[]{:S(2)}) collective-permute-start(f32[32,128]{1,0:T(8,128)S(1)} %add.59.gram_kept), channel_id=1, source_target_pairs={{0,4},{1,5},{2,6},{3,7},{4,0},{5,1},{6,2},{7,3},{8,12},{9,13},{10,... | collective-permute-start | bytes 49160 | tf_op jit(solution)/shard_map/ppermute | solution.py:24
  100.7 11.6 %collective-permute-start.10 = (bf16[4,128,512]{2,1,0:T(8,128)(2,1)S(1)}, bf16[4,128,512]{2,1,0:T(8,128)(2,1)S(1)}, u32[]{:S(2)}, u32[]{:S(2)}) collective-permute-start(bf16[4,128,512]{2,1,0:T(8,128)(2,1)S(1)} %get-tuple-element.34.refs_2_), channel_id=1, source_target_pairs={{0,1},{1,0},{2,3},{3,2},{4,5},{5,4},{6,7},{7,6},{8,9},{9,8},{10,11... | collective-permute-start | bytes 1572872 | tf_op jit(solution)/shard_map/ppermute | solution.py:24
  101.9 10.9 %collective-permute-start.13 = (bf16[4,128,512]{2,1,0:T(8,128)(2,1)S(1)}, bf16[4,128,512]{2,1,0:T(8,128)(2,1)S(1)}, u32[]{:S(2)}, u32[]{:S(2)}) collective-permute-start(bf16[4,128,512]{2,1,0:T(8,128)(2,1)S(1)} %get-tuple-element.35.refs_3_), channel_id=1, source_target_pairs={{0,2},{1,3},{2,0},{3,1},{4,6},{5,7},{6,4},{7,5},{8,10},{9,11},{10,... | collective-permute-start | bytes 1572872 | tf_op jit(solution)/shard_map/ppermute | solution.py:24
  103.5 14.3 %all-to-all-start.3 = ((f32[8,8,640]{2,1,0:T(8,128)}), f32[8,8,640]{2,1,0:T(8,128)S(1)}, u32[]{:S(2)}, u32[]{:S(2)}) async-start(f32[8,8,640]{2,1,0:T(8,128)} %pad_maximum_fusion.2), calls=%async_computation.3 | async-start | bytes 327680 | tf_op jit(solution)/shard_map/all_to_all | solution.py:19
  113.1 6.8 %collective-permute-start.14 = (bf16[2,128,512]{2,1,0:T(8,128)(2,1)S(1)}, bf16[2,128,512]{2,1,0:T(8,128)(2,1)S(1)}, u32[]{:S(2)}, u32[]{:S(2)}) collective-permute-start(bf16[2,128,512]{2,1,0:T(8,128)(2,1)S(1)} %get-tuple-element.45), channel_id=1, source_target_pairs={{0,1},{1,0},{2,3},{3,2},{4,5},{5,4},{6,7},{7,6},{8,9},{9,8},{10,11... | collective-permute-start | bytes 786440 | tf_op jit(solution)/shard_map/ppermute | solution.py:24
  118.8 9.0 %collective-permute-start.11 = (bf16[2,128,512]{2,1,0:T(8,128)(2,1)S(1)}, bf16[2,128,512]{2,1,0:T(8,128)(2,1)S(1)}, u32[]{:S(2)}, u32[]{:S(2)}) collective-permute-start(bf16[2,128,512]{2,1,0:T(8,128)(2,1)S(1)} %get-tuple-element.46), channel_id=1, source_target_pairs={{0,2},{1,3},{2,0},{3,1},{4,6},{5,7},{6,4},{7,5},{8,10},{9,11},{10,... | collective-permute-start | bytes 786440 | tf_op jit(solution)/shard_map/ppermute | solution.py:24
  119.9 8.0 %collective-permute-start.15 = (bf16[1,128,512]{2,1,0:T(8,128)(2,1)S(1)}, bf16[1,128,512]{2,1,0:T(8,128)(2,1)S(1)}, u32[]{:S(2)}, u32[]{:S(2)}) collective-permute-start(bf16[1,128,512]{2,1,0:T(8,128)(2,1)S(1)} %add_convert_fusion.4), channel_id=1, source_target_pairs={{0,4},{1,5},{2,6},{3,7},{4,0},{5,1},{6,2},{7,3},{8,12},{9,13},{10,... | collective-permute-start | bytes 393224 | tf_op jit(solution)/shard_map/ppermute | solution.py:24
  127.8 6.3 %collective-permute-start.12 = (bf16[1,128,512]{2,1,0:T(8,128)(2,1)S(1)}, bf16[1,128,512]{2,1,0:T(8,128)(2,1)S(1)}, u32[]{:S(2)}, u32[]{:S(2)}) collective-permute-start(bf16[1,128,512]{2,1,0:T(8,128)(2,1)S(1)} %add_convert_fusion.6), channel_id=1, source_target_pairs={{0,4},{1,5},{2,6},{3,7},{4,0},{5,1},{6,2},{7,3},{8,12},{9,13},{10,... | collective-permute-start | bytes 393224 | tf_op jit(solution)/shard_map/ppermute | solution.py:24

commit v4 on v3

--- a/solution.py
+++ b/solution.py
@@ -54,15 +54,12 @@
     length = lens[first_doc + pl.program_id(0)]
     seq_len = states.shape[1]
     refs = (states, gain, w_in, grad, pool_act, pool_x)
-    few = seq_len // 2 if seq_len % 256 == 0 else seq_len
-
-    @pl.when(length <= few)
-    def _():
-        student_doc(few, length, *refs)
-
-    @pl.when(length > few)
-    def _():
-        student_doc(seq_len, length, *refs)
+    lines = 128 if seq_len % 128 == 0 else seq_len
+    for rows in range(lines, seq_len + 1, lines):
+
+        @pl.when((length > rows - lines) & (length <= rows))
+        def _(rows=rows):
+            student_doc(rows, length, *refs)
 
 
 def student_part(lengths, states, gain, w_in, after, first_doc, docs):

time: 136 us -> 135 us (level)
  transfers between devices with their start and end apart: 20 -> 20, of which waited for: 14 -> 14; matrix products, arithmetic and copies ran while one was open for 3% -> 3% of each run, Pallas kernels for 24% -> 23%
where the time goes in v4:
time: 135 us; the launch traced here: 134 us
  starting transfers between devices  46.4 us (34%)
  Pallas kernels  41.9 us (31%)
  waiting for transfers between devices  37.9 us (28%)
  local copies, waits for them, and re-layouts  3.19 us (2%)
  other arithmetic  2.84 us (2%)
  matrix products  1.42 us (1%)
    ppermute x16, waiting for transfers between devices, swap(): lax.ppermute(value, axis, [(i, i ^ 1 << bit) for i in range(members)])  27.8 us
    all_to_all x4, starting transfers between devices, exchange(): return lax.all_to_all(blocks, axis, 0, 0, tiled=True)  25.7 us
    pallas_call x2, Pallas kernels, student_part(): pl.pallas_call(functools.partial(student_kernel, first_doc), grid_spec=pl...  25.5 us
    ppermute x16, starting transfers between devices, swap(): lax.ppermute(value, axis, [(i, i ^ 1 << bit) for i in range(members)])  20.6 us
    all_to_all x4, waiting for transfers between devices, exchange(): return lax.all_to_all(blocks, axis, 0, 0, tiled=True)  10.1 us
    pallas_call x1, Pallas kernels, contrast(): pl.pallas_call(functools.partial(contrast_kernel, (orders, members // 2))...  5.24 us
    pallas_call x1, Pallas kernels, gate_up(): pl.pallas_call(functools.partial(gate_up_kernel, block), in_specs=[pl.Blo...  4.93 us
    pallas_call x1, Pallas kernels, weigh(): pl.pallas_call(functools.partial(weigh_kernel, (orders, 0), len(grads)),...  3.82 us
  transfers between devices with their start and end apart: 20, of which 14 were waited for; matrix products, arithmetic and copies ran while one was open for 3% of the time, Pallas kernels for 23%

profile of v4, /device:TPU:0, one launch (start us, length us, event | category | flops | bytes accessed | tf_op | source)
XLA Modules:
  0.0 134.5 jit_solution(1809191785526843960)
XLA Ops:
  0.6 7.3 %all-to-all-start = ((bf16[8,8,512]{2,1,0:T(8,128)(2,1)}), bf16[8,8,512]{2,1,0:T(8,128)(2,1)S(1)}, u32[]{:S(2)}, u32[]{:S(2)}) async-start(bf16[8,8,512]{2,1,0:T(8,128)(2,1)} %bitcast.41), calls=%async_computation | async-start | bytes 131072 | tf_op jit(solution)/shard_map/all_to_all | solution.py:19
  8.0 6.9 %all-to-all-done = bf16[8,8,512]{2,1,0:T(8,128)(2,1)S(1)} async-done(((bf16[8,8,512]{2,1,0:T(8,128)(2,1)}), bf16[8,8,512]{2,1,0:T(8,128)(2,1)S(1)}, u32[]{:S(2)}, u32[]{:S(2)}) %all-to-all-start) | async-done | bytes 65568 | tf_op jit(solution)/shard_map/all_to_all | solution.py:19
  14.9 0.6 copy-done.2
  15.5 4.9 %gate_up.1 = bf16[64,6144]{1,0:T(8,128)(2,1)} custom-call(s32[1]{0:T(128)} %bitcast.place, bf16[64,512]{1,0:T(8,128)(2,1)} %bitcast.39, f32[1,4096]{1,0:T(1,128)} %bitcast.48, bf16[2,512,3072]{2,1,0:T(8,128)(2,1)} %weights.2), custom_call_target="tpu_custom_call" | custom-call | tf_op jit(solution)/shard_map/gate_up/pallas_call | solution.py:127
  20.4 3.6 %all-to-all-start.1 = ((bf16[8,8,6144]{2,1,0:T(8,128)(2,1)}), bf16[8,8,6144]{2,1,0:T(8,128)(2,1)S(1)}, u32[]{:S(2)}, u32[]{:S(2)}) async-start(bf16[8,8,6144]{2,1,0:T(8,128)(2,1)} %bitcast.44), calls=%async_computation.1 | async-start | bytes 1572864 | tf_op jit(solution)/shard_map/all_to_all | solution.py:19
  24.0 7.9 %student.2 = (bf16[2,2,1024,512]{3,2,1,0:T(8,128)(2,1)}, f32[2,1,1024]{2,1,0:T(1,128)}, f32[2,1,1024]{2,1,0:T(1,128)}) custom-call(s32[8]{0:T(128)} %lens.5, bf16[8,512,1024]{2,1,0:T(8,128)(2,1)} %states.3, f32[1,1024]{1,0:T(1,128)} %bitcast.49, bf16[1024,1024]{1,0:T(8,128)(2,1)} %w_in.3, bf16[8,4096]{1,0:T(8,128)(2,1)} %after.1), custom_call_target="tpu_custom_call" | custom-call | flops 3221225472 | bytes 6291456 | tf_op jit(solution)/shard_map/student/pallas_call | solution.py:68
  31.9 17.6 %student.3 = (bf16[6,2,1024,512]{3,2,1,0:T(8,128)(2,1)}, f32[6,1,1024]{2,1,0:T(1,128)}, f32[6,1,1024]{2,1,0:T(1,128)}) custom-call(s32[8]{0:T(128)} %lens.5, bf16[8,512,1024]{2,1,0:T(8,128)(2,1)} %states.3, f32[1,1024]{1,0:T(1,128)} %bitcast.50, bf16[1024,1024]{1,0:T(8,128)(2,1)} %w_in.3, bf16[8,8,6144]{2,1,0:T(8,128)(2,1)} %bitcast.45), custom_call_target="tpu_custom_call" | custom-call | flops 9663676416 | bytes 18874368 | tf_op jit(solution)/shard_map/student/pallas_call | solution.py:68
  49.5 0.8 fusion.8
  50.3 0.9 hidden.1
  51.3 9.9 %all-to-all-start.2 = ((bf16[8,8,3072]{2,1,0:T(8,128)(2,1)}), bf16[8,8,3072]{2,1,0:T(8,128)(2,1)S(1)}, u32[]{:S(2)}, u32[]{:S(2)}) async-start(bf16[8,8,3072]{2,1,0:T(8,128)(2,1)} %hidden.1), calls=%async_computation.2 | async-start | bytes 786432 | tf_op jit(solution)/shard_map/all_to_all | solution.py:19
  61.2 0.4 fusion.5
  61.6 1.2 collective-permute-done.5
  62.8 1.5 %collective-permute-start.6 = (f32[8,1024]{1,0:T(8,128)S(1)}, f32[8,1024]{1,0:T(8,128)S(1)}, u32[]{:S(2)}, u32[]{:S(2)}) collective-permute-start(f32[8,1024]{1,0:T(8,128)S(1)} %add.60), channel_id=1, source_target_pairs={{0,16},{8,24},{16,0},{24,8},{1,17},{9,25},{17,1},{25,9},{2,18},{10... | collective-permute-start | bytes 98312 | tf_op jit(solution)/shard_map/ppermute | solution.py:24
  64.4 2.4 %collective-permute-done.6 = f32[8,1024]{1,0:T(8,128)S(1)} collective-permute-done((f32[8,1024]{1,0:T(8,128)S(1)}, f32[8,1024]{1,0:T(8,128)S(1)}, u32[]{:S(2)}, u32[]{:S(2)}) %collective-permute-start.6) | collective-permute-done | bytes 32800 | tf_op jit(solution)/shard_map/ppermute | solution.py:24
  66.8 3.0 %collective-permute-start.7 = (f32[1,8,1024]{2,1,0:T(8,128)S(1)}, f32[1,8,1024]{2,1,0:T(8,128)S(1)}, u32[]{:S(2)}, u32[]{:S(2)}) collective-permute-start(f32[1,8,1024]{2,1,0:T(8,128)S(1)} %fusion.1), channel_id=1, source_target_pairs={{0,4},{1,5},{2,6},{3,7},{4,0},{5,1},{6,2},{7,3},{8,12},{9,13},{10,... | collective-permute-start | bytes 98312 | tf_op jit(solution)/shard_map/ppermute | solution.py:24
  69.7 2.5 %collective-permute-done.7 = f32[1,8,1024]{2,1,0:T(8,128)S(1)} collective-permute-done((f32[1,8,1024]{2,1,0:T(8,128)S(1)}, f32[1,8,1024]{2,1,0:T(8,128)S(1)}, u32[]{:S(2)}, u32[]{:S(2)}) %collective-permute-start.7) | collective-permute-done | bytes 32800 | tf_op jit(solution)/shard_map/ppermute | solution.py:24
  72.2 1.4 %collective-permute-start.8 = (f32[2,8,1024]{2,1,0:T(8,128)S(1)}, f32[2,8,1024]{2,1,0:T(8,128)S(1)}, u32[]{:S(2)}, u32[]{:S(2)}) collective-permute-start(f32[2,8,1024]{2,1,0:T(8,128)S(1)} %pad_maximum_fusion.4), channel_id=1, source_target_pairs={{0,2},{1,3},{2,0},{3,1},{4,6},{5,7},{6,4},{7,5},{8,10},{9,11},{10,... | collective-permute-start | bytes 196616 | tf_op jit(solution)/shard_map/ppermute | solution.py:24
  73.7 1.9 %copy-done.1 = bf16[3072,512]{1,0:T(8,128)(2,1)S(1)} copy-done((bf16[3072,512]{1,0:T(8,128)(2,1)S(1)}, bf16[3072,512]{1,0:T(8,128)(2,1)}, u32[]{:S(2)}) %copy-start.1) | copy-done | bytes 3145752
  75.6 0.7 down.1
  76.3 0.2 collective-permute-done.8
  76.5 1.5 %collective-permute-start.9 = (f32[4,8,1024]{2,1,0:T(8,128)S(1)}, f32[4,8,1024]{2,1,0:T(8,128)S(1)}, u32[]{:S(2)}, u32[]{:S(2)}) collective-permute-start(f32[4,8,1024]{2,1,0:T(8,128)S(1)} %pad_maximum_fusion.3), channel_id=1, source_target_pairs={{0,1},{1,0},{2,3},{3,2},{4,5},{5,4},{6,7},{7,6},{8,9},{9,8},{10,11... | collective-permute-start | bytes 393224 | tf_op jit(solution)/shard_map/ppermute | solution.py:24
  78.1 1.6 %collective-permute-start.1 = (bf16[64,512]{1,0:T(8,128)(2,1)S(1)}, bf16[64,512]{1,0:T(8,128)(2,1)S(1)}, u32[]{:S(2)}, u32[]{:S(2)}) collective-permute-start(bf16[64,512]{1,0:T(8,128)(2,1)S(1)} %add_convert_fusion.8.kept), channel_id=1, source_target_pairs={{0,16},{8,24},{16,0},{24,8},{1,17},{9,25},{17,1},{25,9},{2,18},{10... | collective-permute-start | bytes 196616 | tf_op jit(solution)/shard_map/ppermute | solution.py:24
  79.6 2.8 %collective-permute-done.1.arrived = bf16[64,512]{1,0:T(8,128)(2,1)S(1)} collective-permute-done((bf16[64,512]{1,0:T(8,128)(2,1)S(1)}, bf16[64,512]{1,0:T(8,128)(2,1)S(1)}, u32[]{:S(2)}, u32[]{:S(2)}) %collective-permute-start.1) | collective-permute-done | bytes 65568 | tf_op jit(solution)/shard_map/ppermute | solution.py:24
  82.4 0.4 teacher_block.1
  82.8 1.1 collective-permute-start.2
  83.8 2.7 %collective-permute-done.2 = f32[32,128]{1,0:T(8,128)S(1)} collective-permute-done((f32[32,128]{1,0:T(8,128)S(1)}, f32[32,128]{1,0:T(8,128)S(1)}, u32[]{:S(2)}, u32[]{:S(2)}) %collective-permute-start.2) | collective-permute-done | bytes 16416 | tf_op jit(solution)/shard_map/ppermute | solution.py:24
  86.5 1.4 %collective-permute-start.3 = (f32[32,128]{1,0:T(8,128)S(1)}, f32[32,128]{1,0:T(8,128)S(1)}, u32[]{:S(2)}, u32[]{:S(2)}) collective-permute-start(f32[32,128]{1,0:T(8,128)S(1)} %add.58), channel_id=1, source_target_pairs={{0,2},{1,3},{2,0},{3,1},{4,6},{5,7},{6,4},{7,5},{8,10},{9,11},{10,... | collective-permute-start | bytes 49160 | tf_op jit(solution)/shard_map/ppermute | solution.py:24
  87.9 2.3 %collective-permute-done.3 = f32[32,128]{1,0:T(8,128)S(1)} collective-permute-done((f32[32,128]{1,0:T(8,128)S(1)}, f32[32,128]{1,0:T(8,128)S(1)}, u32[]{:S(2)}, u32[]{:S(2)}) %collective-permute-start.3) | collective-permute-done | bytes 16416 | tf_op jit(solution)/shard_map/ppermute | solution.py:24
  90.3 2.5 %collective-permute-start.4 = (f32[32,128]{1,0:T(8,128)S(1)}, f32[32,128]{1,0:T(8,128)S(1)}, u32[]{:S(2)}, u32[]{:S(2)}) collective-permute-start(f32[32,128]{1,0:T(8,128)S(1)} %add.59.gram_kept), channel_id=1, source_target_pairs={{0,4},{1,5},{2,6},{3,7},{4,0},{5,1},{6,2},{7,3},{8,12},{9,13},{10,... | collective-permute-start | bytes 49160 | tf_op jit(solution)/shard_map/ppermute | solution.py:24
  92.8 0.5 embed.1
  93.3 1.6 %collective-permute-done.4.gram_arrived = f32[32,128]{1,0:T(8,128)S(1)} collective-permute-done((f32[32,128]{1,0:T(8,128)S(1)}, f32[32,128]{1,0:T(8,128)S(1)}, u32[]{:S(2)}, u32[]{:S(2)}) %collective-permute-start.4) | collective-permute-done | bytes 16416 | tf_op jit(solution)/shard_map/ppermute | solution.py:24
  94.9 5.2 %contrast.1 = (f32[1,1]{1,0:T(1,128)}, bf16[64,1024]{1,0:T(8,128)(2,1)S(1)}, f32[8,1024]{1,0:T(8,128)S(1)}, bf16[4,128,512]{2,1,0:T(8,128)(2,1)S(1)}, bf16[4,128,512]{2,1,0:T(8,128)(2,1)S(1)}) custom-call(s32[1]{0:T(128)} %bitcast.place, s32[8]{0:T(128)S(1)} %copy-done.6, f32[32,128]{1,0:T(8,128)S(1)} %add.59.gram_kept, ...), custom_call_target="tpu_custom_call" | custom-call | tf_op jit(solution)/shard_map/contrast/pallas_call | solution.py:367
  100.2 1.1 collective-permute-start.10
  101.3 0.9 collective-permute-start.13
  102.2 0.7 pad_maximum_fusion.2
  102.9 4.9 %all-to-all-start.3 = ((f32[8,8,640]{2,1,0:T(8,128)}), f32[8,8,640]{2,1,0:T(8,128)S(1)}, u32[]{:S(2)}, u32[]{:S(2)}) async-start(f32[8,8,640]{2,1,0:T(8,128)} %pad_maximum_fusion.2), calls=%async_computation.3 | async-start | bytes 327680 | tf_op jit(solution)/shard_map/all_to_all | solution.py:19
  107.8 3.8 %weigh.1 = (bf16[4,128,512]{2,1,0:T(8,128)(2,1)S(1)}, bf16[4,128,512]{2,1,0:T(8,128)(2,1)S(1)}) custom-call(s32[1]{0:T(128)} %bitcast.place, f32[8,1024]{1,0:T(8,128)S(1)} %get-tuple-element.33.scale, bf16[2,2,1024,512]{3,2,1,0:T(8,128)(2,1)} %get-tuple-element.30.refs_0_, bf16[6,2,1024,512]{3,2,1,0:T(8,128)(2,1)} %get-tuple-element.31.refs_1_, ...), custom_call_target="tpu_custom_call" | custom-call | tf_op jit(solution)/shard_map/weigh/pallas_call | solution.py:394
  111.7 0.5 collective-permute-done.13
  112.2 0.3 add_convert_fusion.1
  112.5 1.5 %collective-permute-start.14 = (bf16[2,128,512]{2,1,0:T(8,128)(2,1)S(1)}, bf16[2,128,512]{2,1,0:T(8,128)(2,1)S(1)}, u32[]{:S(2)}, u32[]{:S(2)}) collective-permute-start(bf16[2,128,512]{2,1,0:T(8,128)(2,1)S(1)} %get-tuple-element.45), channel_id=1, source_target_pairs={{0,1},{1,0},{2,3},{3,2},{4,5},{5,4},{6,7},{7,6},{8,9},{9,8},{10,11... | collective-permute-start | bytes 786440 | tf_op jit(solution)/shard_map/ppermute | solution.py:24
  114.0 3.2 %all-to-all-done.3 = f32[8,8,640]{2,1,0:T(8,128)S(1)} async-done(((f32[8,8,640]{2,1,0:T(8,128)}), f32[8,8,640]{2,1,0:T(8,128)S(1)}, u32[]{:S(2)}, u32[]{:S(2)}) %all-to-all-start.3) | async-done | bytes 163872 | tf_op jit(solution)/shard_map/all_to_all | solution.py:19
  117.2 1.0 fusion.3
  118.2 0.4 collective-permute-start.11
  118.7 0.6 constant_dynamic-slice_fusion
  119.3 2.5 %collective-permute-start.15 = (bf16[1,128,512]{2,1,0:T(8,128)(2,1)S(1)}, bf16[1,128,512]{2,1,0:T(8,128)(2,1)S(1)}, u32[]{:S(2)}, u32[]{:S(2)}) collective-permute-start(bf16[1,128,512]{2,1,0:T(8,128)(2,1)S(1)} %add_convert_fusion.4), channel_id=1, source_target_pairs={{0,4},{1,5},{2,6},{3,7},{4,0},{5,1},{6,2},{7,3},{8,12},{9,13},{10,... | collective-permute-start | bytes 393224 | tf_op jit(solution)/shard_map/ppermute | solution.py:24
  121.8 5.4 %collective-permute-done.11 = bf16[2,128,512]{2,1,0:T(8,128)(2,1)S(1)} collective-permute-done((bf16[2,128,512]{2,1,0:T(8,128)(2,1)S(1)}, bf16[2,128,512]{2,1,0:T(8,128)(2,1)S(1)}, u32[]{:S(2)}, u32[]{:S(2)}) %collective-permute-start.11) | collective-permute-done | bytes 262176 | tf_op jit(solution)/shard_map/ppermute | solution.py:24
  127.4 6.2 %collective-permute-done.12 = bf16[1,128,512]{2,1,0:T(8,128)(2,1)S(1)} collective-permute-done((bf16[1,128,512]{2,1,0:T(8,128)(2,1)S(1)}, bf16[1,128,512]{2,1,0:T(8,128)(2,1)S(1)}, u32[]{:S(2)}, u32[]{:S(2)}) %collective-permute-start.12) | collective-permute-done | bytes 131104 | tf_op jit(solution)/shard_map/ppermute | solution.py:24
  133.6 0.8 pad_maximum_fusion
  (43 shorter events, 0.5 us)
Async XLA Ops:
  0.6 14.2 %all-to-all-start = ((bf16[8,8,512]{2,1,0:T(8,128)(2,1)}), bf16[8,8,512]{2,1,0:T(8,128)(2,1)S(1)}, u32[]{:S(2)}, u32[]{:S(2)}) async-start(bf16[8,8,512]{2,1,0:T(8,128)(2,1)} %bitcast.41), calls=%async_computation | async-start | bytes 131072 | tf_op jit(solution)/shard_map/all_to_all | solution.py:19
  14.9 0.6 copy-start.2
  20.4 29.9 %all-to-all-start.1 = ((bf16[8,8,6144]{2,1,0:T(8,128)(2,1)}), bf16[8,8,6144]{2,1,0:T(8,128)(2,1)S(1)}, u32[]{:S(2)}, u32[]{:S(2)}) async-start(bf16[8,8,6144]{2,1,0:T(8,128)(2,1)} %bitcast.44), calls=%async_computation.1 | async-start | bytes 1572864 | tf_op jit(solution)/shard_map/all_to_all | solution.py:19
  31.9 17.6 %copy-start.8 = (f32[2,1,1024]{2,1,0:T(1,128)S(1)}, f32[2,1,1024]{2,1,0:T(1,128)}, u32[]{:S(2)}) copy-start(f32[2,1,1024]{2,1,0:T(1,128)} %get-tuple-element.25) | copy-start | bytes 24580
  31.9 18.4 %copy-start.4 = (bf16[8,4096]{1,0:T(8,128)(2,1)S(1)}, bf16[8,4096]{1,0:T(8,128)(2,1)}, u32[]{:S(2)}) copy-start(bf16[8,4096]{1,0:T(8,128)(2,1)} %after.1) | copy-start | bytes 196612
  31.9 29.3 %copy-start = (bf16[1024,1024]{1,0:T(8,128)(2,1)S(1)}, bf16[1024,1024]{1,0:T(8,128)(2,1)}, u32[]{:S(2)}) copy-start(bf16[1024,1024]{1,0:T(8,128)(2,1)} %w_out.1) | copy-start | bytes 6291460
  49.5 14.9 %copy-start.9 = (f32[2,1,1024]{2,1,0:T(1,128)S(1)}, f32[2,1,1024]{2,1,0:T(1,128)}, u32[]{:S(2)}) copy-start(f32[2,1,1024]{2,1,0:T(1,128)} %get-tuple-element.23) | copy-start | bytes 24580
  49.5 14.9 %copy-start.7 = (f32[6,1,1024]{2,1,0:T(1,128)S(1)}, f32[6,1,1024]{2,1,0:T(1,128)}, u32[]{:S(2)}) copy-start(f32[6,1,1024]{2,1,0:T(1,128)} %get-tuple-element.24) | copy-start | bytes 73732
  51.3 22.4 %all-to-all-start.2 = ((bf16[8,8,3072]{2,1,0:T(8,128)(2,1)}), bf16[8,8,3072]{2,1,0:T(8,128)(2,1)S(1)}, u32[]{:S(2)}, u32[]{:S(2)}) async-start(bf16[8,8,3072]{2,1,0:T(8,128)(2,1)} %hidden.1), calls=%async_computation.2 | async-start | bytes 786432 | tf_op jit(solution)/shard_map/all_to_all | solution.py:19
  61.2 21.2 %copy-start.3 = (bf16[8,8,512]{2,1,0:T(8,128)(2,1)S(1)}, bf16[8,8,512]{2,1,0:T(8,128)(2,1)}, u32[]{:S(2)}) copy-start(bf16[8,8,512]{2,1,0:T(8,128)(2,1)} %copy-done.2) | copy-start | bytes 196612
  61.2 21.2 %copy-start.5 = (f32[4096]{0:T(1024)S(1)}, f32[4096]{0:T(1024)}, u32[]{:S(2)}) copy-start(f32[4096]{0:T(1024)} %param.19) | copy-start | bytes 49156
  61.6 33.3 %copy-start.6 = (s32[8]{0:T(128)S(1)}, s32[8]{0:T(128)}, u32[]{:S(2)}) copy-start(s32[8]{0:T(128)} %lens.5) | copy-start | bytes 100
  61.6 1.2 collective-permute-start.5
  62.8 3.9 %collective-permute-start.6 = (f32[8,1024]{1,0:T(8,128)S(1)}, f32[8,1024]{1,0:T(8,128)S(1)}, u32[]{:S(2)}, u32[]{:S(2)}) collective-permute-start(f32[8,1024]{1,0:T(8,128)S(1)} %add.60), channel_id=1, source_target_pairs={{0,16},{8,24},{16,0},{24,8},{1,17},{9,25},{17,1},{25,9},{2,18},{10... | collective-permute-start | bytes 98312 | tf_op jit(solution)/shard_map/ppermute | solution.py:24
  66.8 5.5 %collective-permute-start.7 = (f32[1,8,1024]{2,1,0:T(8,128)S(1)}, f32[1,8,1024]{2,1,0:T(8,128)S(1)}, u32[]{:S(2)}, u32[]{:S(2)}) collective-permute-start(f32[1,8,1024]{2,1,0:T(8,128)S(1)} %fusion.1), channel_id=1, source_target_pairs={{0,4},{1,5},{2,6},{3,7},{4,0},{5,1},{6,2},{7,3},{8,12},{9,13},{10,... | collective-permute-start | bytes 98312 | tf_op jit(solution)/shard_map/ppermute | solution.py:24
  72.2 4.3 %collective-permute-start.8 = (f32[2,8,1024]{2,1,0:T(8,128)S(1)}, f32[2,8,1024]{2,1,0:T(8,128)S(1)}, u32[]{:S(2)}, u32[]{:S(2)}) collective-permute-start(f32[2,8,1024]{2,1,0:T(8,128)S(1)} %pad_maximum_fusion.4), channel_id=1, source_target_pairs={{0,2},{1,3},{2,0},{3,1},{4,6},{5,7},{6,4},{7,5},{8,10},{9,11},{10,... | collective-permute-start | bytes 196616 | tf_op jit(solution)/shard_map/ppermute | solution.py:24
  73.7 1.9 %copy-start.1 = (bf16[3072,512]{1,0:T(8,128)(2,1)S(1)}, bf16[3072,512]{1,0:T(8,128)(2,1)}, u32[]{:S(2)}) copy-start(bf16[3072,512]{1,0:T(8,128)(2,1)} %weights.3) | copy-start | bytes 9437188
  76.2 1.8 %collective-permute-start = (f32[64,512]{1,0:T(8,128)S(1)}, f32[64,512]{1,0:T(8,128)S(1)}, u32[]{:S(2)}, u32[]{:S(2)}) collective-permute-start(f32[64,512]{1,0:T(8,128)S(1)} %down.1), channel_id=1, source_target_pairs={{0,8},{8,0},{16,24},{24,16},{1,9},{9,1},{17,25},{25,17},{2,10},{10... | collective-permute-start | bytes 393224 | tf_op jit(solution)/shard_map/ppermute | solution.py:24
  76.5 16.3 %collective-permute-start.9 = (f32[4,8,1024]{2,1,0:T(8,128)S(1)}, f32[4,8,1024]{2,1,0:T(8,128)S(1)}, u32[]{:S(2)}, u32[]{:S(2)}) collective-permute-start(f32[4,8,1024]{2,1,0:T(8,128)S(1)} %pad_maximum_fusion.3), channel_id=1, source_target_pairs={{0,1},{1,0},{2,3},{3,2},{4,5},{5,4},{6,7},{7,6},{8,9},{9,8},{10,11... | collective-permute-start | bytes 393224 | tf_op jit(solution)/shard_map/ppermute | solution.py:24
  78.1 4.3 %collective-permute-start.1 = (bf16[64,512]{1,0:T(8,128)(2,1)S(1)}, bf16[64,512]{1,0:T(8,128)(2,1)S(1)}, u32[]{:S(2)}, u32[]{:S(2)}) collective-permute-start(bf16[64,512]{1,0:T(8,128)(2,1)S(1)} %add_convert_fusion.8.kept), channel_id=1, source_target_pairs={{0,16},{8,24},{16,0},{24,8},{1,17},{9,25},{17,1},{25,9},{2,18},{10... | collective-permute-start | bytes 196616 | tf_op jit(solution)/shard_map/ppermute | solution.py:24
  82.8 3.7 %collective-permute-start.2 = (f32[32,128]{1,0:T(8,128)S(1)}, f32[32,128]{1,0:T(8,128)S(1)}, u32[]{:S(2)}, u32[]{:S(2)}) collective-permute-start(f32[32,128]{1,0:T(8,128)S(1)} %get-tuple-element.22), channel_id=1, source_target_pairs={{0,1},{1,0},{2,3},{3,2},{4,5},{5,4},{6,7},{7,6},{8,9},{9,8},{10,11... | collective-permute-start | bytes 49160 | tf_op jit(solution)/shard_map/ppermute | solution.py:24
  86.5 3.7 %collective-permute-start.3 = (f32[32,128]{1,0:T(8,128)S(1)}, f32[32,128]{1,0:T(8,128)S(1)}, u32[]{:S(2)}, u32[]{:S(2)}) collective-permute-start(f32[32,128]{1,0:T(8,128)S(1)} %add.58), channel_id=1, source_target_pairs={{0,2},{1,3},{2,0},{3,1},{4,6},{5,7},{6,4},{7,5},{8,10},{9,11},{10,... | collective-permute-start | bytes 49160 | tf_op jit(solution)/shard_map/ppermute | solution.py:24
  90.3 4.6 %collective-permute-start.4 = (f32[32,128]{1,0:T(8,128)S(1)}, f32[32,128]{1,0:T(8,128)S(1)}, u32[]{:S(2)}, u32[]{:S(2)}) collective-permute-start(f32[32,128]{1,0:T(8,128)S(1)} %add.59.gram_kept), channel_id=1, source_target_pairs={{0,4},{1,5},{2,6},{3,7},{4,0},{5,1},{6,2},{7,3},{8,12},{9,13},{10,... | collective-permute-start | bytes 49160 | tf_op jit(solution)/shard_map/ppermute | solution.py:24
  100.2 11.5 %collective-permute-start.10 = (bf16[4,128,512]{2,1,0:T(8,128)(2,1)S(1)}, bf16[4,128,512]{2,1,0:T(8,128)(2,1)S(1)}, u32[]{:S(2)}, u32[]{:S(2)}) collective-permute-start(bf16[4,128,512]{2,1,0:T(8,128)(2,1)S(1)} %get-tuple-element.34.refs_2_), channel_id=1, source_target_pairs={{0,1},{1,0},{2,3},{3,2},{4,5},{5,4},{6,7},{7,6},{8,9},{9,8},{10,11... | collective-permute-start | bytes 1572872 | tf_op jit(solution)/shard_map/ppermute | solution.py:24
  101.3 10.9 %collective-permute-start.13 = (bf16[4,128,512]{2,1,0:T(8,128)(2,1)S(1)}, bf16[4,128,512]{2,1,0:T(8,128)(2,1)S(1)}, u32[]{:S(2)}, u32[]{:S(2)}) collective-permute-start(bf16[4,128,512]{2,1,0:T(8,128)(2,1)S(1)} %get-tuple-element.35.refs_3_), channel_id=1, source_target_pairs={{0,2},{1,3},{2,0},{3,1},{4,6},{5,7},{6,4},{7,5},{8,10},{9,11},{10,... | collective-permute-start | bytes 1572872 | tf_op jit(solution)/shard_map/ppermute | solution.py:24
  102.9 14.3 %all-to-all-start.3 = ((f32[8,8,640]{2,1,0:T(8,128)}), f32[8,8,640]{2,1,0:T(8,128)S(1)}, u32[]{:S(2)}, u32[]{:S(2)}) async-start(f32[8,8,640]{2,1,0:T(8,128)} %pad_maximum_fusion.2), calls=%async_computation.3 | async-start | bytes 327680 | tf_op jit(solution)/shard_map/all_to_all | solution.py:19
  112.5 6.8 %collective-permute-start.14 = (bf16[2,128,512]{2,1,0:T(8,128)(2,1)S(1)}, bf16[2,128,512]{2,1,0:T(8,128)(2,1)S(1)}, u32[]{:S(2)}, u32[]{:S(2)}) collective-permute-start(bf16[2,128,512]{2,1,0:T(8,128)(2,1)S(1)} %get-tuple-element.45), channel_id=1, source_target_pairs={{0,1},{1,0},{2,3},{3,2},{4,5},{5,4},{6,7},{7,6},{8,9},{9,8},{10,11... | collective-permute-start | bytes 786440 | tf_op jit(solution)/shard_map/ppermute | solution.py:24
  118.2 9.0 %collective-permute-start.11 = (bf16[2,128,512]{2,1,0:T(8,128)(2,1)S(1)}, bf16[2,128,512]{2,1,0:T(8,128)(2,1)S(1)}, u32[]{:S(2)}, u32[]{:S(2)}) collective-permute-start(bf16[2,128,512]{2,1,0:T(8,128)(2,1)S(1)} %get-tuple-element.46), channel_id=1, source_target_pairs={{0,2},{1,3},{2,0},{3,1},{4,6},{5,7},{6,4},{7,5},{8,10},{9,11},{10,... | collective-permute-start | bytes 786440 | tf_op jit(solution)/shard_map/ppermute | solution.py:24
  119.3 8.0 %collective-permute-start.15 = (bf16[1,128,512]{2,1,0:T(8,128)(2,1)S(1)}, bf16[1,128,512]{2,1,0:T(8,128)(2,1)S(1)}, u32[]{:S(2)}, u32[]{:S(2)}) collective-permute-start(bf16[1,128,512]{2,1,0:T(8,128)(2,1)S(1)} %add_convert_fusion.4), channel_id=1, source_target_pairs={{0,4},{1,5},{2,6},{3,7},{4,0},{5,1},{6,2},{7,3},{8,12},{9,13},{10,... | collective-permute-start | bytes 393224 | tf_op jit(solution)/shard_map/ppermute | solution.py:24
  127.2 6.3 %collective-permute-start.12 = (bf16[1,128,512]{2,1,0:T(8,128)(2,1)S(1)}, bf16[1,128,512]{2,1,0:T(8,128)(2,1)S(1)}, u32[]{:S(2)}, u32[]{:S(2)}) collective-permute-start(bf16[1,128,512]{2,1,0:T(8,128)(2,1)S(1)} %add_convert_fusion.6), channel_id=1, source_target_pairs={{0,4},{1,5},{2,6},{3,7},{4,0},{5,1},{6,2},{7,3},{8,12},{9,13},{10,... | collective-permute-start | bytes 393224 | tf_op jit(solution)/shard_map/ppermute | solution.py:24

commit v5 on v4

--- a/solution.py
+++ b/solution.py
@@ -402,6 +402,24 @@
     )(place, scale, *grads, *after)
 
 
+def finish_kernel(*refs):
+    out = refs[-1]
+    half = out.shape[1] // 2
+    for side in range(2):
+        kept, arrived = refs[2 * side : 2 * side + 2]
+        out[:, side * half : (side + 1) * half] = kept[0].astype(f32) + arrived[0].astype(f32)
+
+
+def finish(sides):
+    _, rows, half = sides[0][0].shape
+    return pl.pallas_call(
+        finish_kernel,
+        out_shape=jax.ShapeDtypeStruct((rows, 2 * half), f32),
+        compiler_params=pltpu.CompilerParams(vmem_limit_bytes=8 << 20),
+        name="finish",
+    )(*sides[0], *sides[1])
+
+
 def halving(sent, kept, order, axis):
     for bit in order:
         arrived = swap(sent, axis, bit)
@@ -409,7 +427,7 @@
         if rest:
             sent = (kept[rest:].astype(f32) + arrived[rest:].astype(f32)).astype(bf16)
             kept = (kept[:rest].astype(f32) + arrived[:rest].astype(f32)).astype(bf16)
-    return kept[0].astype(f32) + arrived[0].astype(f32)
+    return kept, arrived
 
 
 def on_device(
@@ -490,7 +508,7 @@
     sides = []
     for side in range(2):
         sides.append(halving(sent[side], kept[side], orders[side], "dp"))
-    grad_w_in = jnp.concatenate(sides, axis=1)
+    grad_w_in = finish(sides)
     pooled = pooled_act.reshape(local_docs, dp_count, -1).transpose(1, 0, 2).astype(f32)
     states_block = states_block.reshape(dp_count, local_docs, col_width)
     last = exchange(jnp.concatenate([states_block, pooled], axis=2), "dp")

time: 135 us -> 134 us (level)
  waiting for transfers between devices: 37.9 us -> 34.6 us
  starting transfers between devices: 46.4 us -> 48.6 us
    ppermute x16, waiting for transfers between devices: 27.8 us -> 25.1 us  [swap(): lax.ppermute(value, axis, [(i, i ^ 1 << bit) for i in range(members)])]
    ppermute x16, starting transfers between devices: 20.6 us -> 23.3 us  [swap(): lax.ppermute(value, axis, [(i, i ^ 1 << bit) for i in range(members)])]
where the time goes in v5:
time: 134 us; the launch traced here: 133 us
  starting transfers between devices  48.6 us (36%)
  Pallas kernels  42.7 us (32%)
  waiting for transfers between devices  34.6 us (26%)
  local copies, waits for them, and re-layouts  3.19 us (2%)
  other arithmetic  1.99 us (1%)
  matrix products  1.42 us (1%)
    pallas_call x2, Pallas kernels, student_part(): pl.pallas_call(functools.partial(student_kernel, first_doc), grid_spec=pl...  25.5 us
    all_to_all x4, starting transfers between devices, exchange(): return lax.all_to_all(blocks, axis, 0, 0, tiled=True)  25.3 us
    ppermute x16, waiting for transfers between devices, swap(): lax.ppermute(value, axis, [(i, i ^ 1 << bit) for i in range(members)])  25.1 us
    ppermute x16, starting transfers between devices, swap(): lax.ppermute(value, axis, [(i, i ^ 1 << bit) for i in range(members)])  23.3 us
    all_to_all x4, waiting for transfers between devices, exchange(): return lax.all_to_all(blocks, axis, 0, 0, tiled=True)  9.53 us
    pallas_call x1, Pallas kernels, contrast(): pl.pallas_call(functools.partial(contrast_kernel, (orders, members // 2))...  5.24 us
    pallas_call x1, Pallas kernels, gate_up(): pl.pallas_call(functools.partial(gate_up_kernel, block), in_specs=[pl.Blo...  4.93 us
    pallas_call x1, Pallas kernels, weigh(): pl.pallas_call(functools.partial(weigh_kernel, (orders, 0), len(grads)),...  3.81 us
  transfers between devices with their start and end apart: 20, of which 14 were waited for; matrix products, arithmetic and copies ran while one was open for 3% of the time, Pallas kernels for 23%

profile of v5, /device:TPU:0, one launch (start us, length us, event | category | flops | bytes accessed | tf_op | source)
XLA Modules:
  0.0 133.3 jit_solution(12532275974806198847)
XLA Ops:
  0.6 7.3 %all-to-all-start = ((bf16[8,8,512]{2,1,0:T(8,128)(2,1)}), bf16[8,8,512]{2,1,0:T(8,128)(2,1)S(1)}, u32[]{:S(2)}, u32[]{:S(2)}) async-start(bf16[8,8,512]{2,1,0:T(8,128)(2,1)} %bitcast.37), calls=%async_computation | async-start | bytes 131072 | tf_op jit(solution)/shard_map/all_to_all | solution.py:19
  8.0 6.9 %all-to-all-done = bf16[8,8,512]{2,1,0:T(8,128)(2,1)S(1)} async-done(((bf16[8,8,512]{2,1,0:T(8,128)(2,1)}), bf16[8,8,512]{2,1,0:T(8,128)(2,1)S(1)}, u32[]{:S(2)}, u32[]{:S(2)}) %all-to-all-start) | async-done | bytes 65568 | tf_op jit(solution)/shard_map/all_to_all | solution.py:19
  14.9 0.6 copy-done.2
  15.5 4.9 %gate_up.1 = bf16[64,6144]{1,0:T(8,128)(2,1)} custom-call(s32[1]{0:T(128)} %bitcast.place, bf16[64,512]{1,0:T(8,128)(2,1)} %bitcast.35, f32[1,4096]{1,0:T(1,128)} %bitcast.44, bf16[2,512,3072]{2,1,0:T(8,128)(2,1)} %weights.2), custom_call_target="tpu_custom_call" | custom-call | tf_op jit(solution)/shard_map/gate_up/pallas_call | solution.py:127
  20.4 3.6 %all-to-all-start.1 = ((bf16[8,8,6144]{2,1,0:T(8,128)(2,1)}), bf16[8,8,6144]{2,1,0:T(8,128)(2,1)S(1)}, u32[]{:S(2)}, u32[]{:S(2)}) async-start(bf16[8,8,6144]{2,1,0:T(8,128)(2,1)} %bitcast.40), calls=%async_computation.1 | async-start | bytes 1572864 | tf_op jit(solution)/shard_map/all_to_all | solution.py:19
  24.0 7.9 %student.2 = (bf16[2,2,1024,512]{3,2,1,0:T(8,128)(2,1)}, f32[2,1,1024]{2,1,0:T(1,128)}, f32[2,1,1024]{2,1,0:T(1,128)}) custom-call(s32[8]{0:T(128)} %lens.5, bf16[8,512,1024]{2,1,0:T(8,128)(2,1)} %states.3, f32[1,1024]{1,0:T(1,128)} %bitcast.45, bf16[1024,1024]{1,0:T(8,128)(2,1)} %w_in.3, bf16[8,4096]{1,0:T(8,128)(2,1)} %after.1), custom_call_target="tpu_custom_call" | custom-call | flops 3221225472 | bytes 6291456 | tf_op jit(solution)/shard_map/student/pallas_call | solution.py:68
  31.9 17.6 %student.3 = (bf16[6,2,1024,512]{3,2,1,0:T(8,128)(2,1)}, f32[6,1,1024]{2,1,0:T(1,128)}, f32[6,1,1024]{2,1,0:T(1,128)}) custom-call(s32[8]{0:T(128)} %lens.5, bf16[8,512,1024]{2,1,0:T(8,128)(2,1)} %states.3, f32[1,1024]{1,0:T(1,128)} %bitcast.46, bf16[1024,1024]{1,0:T(8,128)(2,1)} %w_in.3, bf16[8,8,6144]{2,1,0:T(8,128)(2,1)} %bitcast.41), custom_call_target="tpu_custom_call" | custom-call | flops 9663676416 | bytes 18874368 | tf_op jit(solution)/shard_map/student/pallas_call | solution.py:68
  49.5 0.8 fusion.8
  50.3 0.9 hidden.1
  51.3 9.9 %all-to-all-start.2 = ((bf16[8,8,3072]{2,1,0:T(8,128)(2,1)}), bf16[8,8,3072]{2,1,0:T(8,128)(2,1)S(1)}, u32[]{:S(2)}, u32[]{:S(2)}) async-start(bf16[8,8,3072]{2,1,0:T(8,128)(2,1)} %hidden.1), calls=%async_computation.2 | async-start | bytes 786432 | tf_op jit(solution)/shard_map/all_to_all | solution.py:19
  61.2 0.4 fusion.5
  61.6 1.2 collective-permute-done.5
  62.8 1.5 %collective-permute-start.6 = (f32[8,1024]{1,0:T(8,128)S(1)}, f32[8,1024]{1,0:T(8,128)S(1)}, u32[]{:S(2)}, u32[]{:S(2)}) collective-permute-start(f32[8,1024]{1,0:T(8,128)S(1)} %add.48), channel_id=1, source_target_pairs={{0,16},{8,24},{16,0},{24,8},{1,17},{9,25},{17,1},{25,9},{2,18},{10... | collective-permute-start | bytes 98312 | tf_op jit(solution)/shard_map/ppermute | solution.py:24
  64.4 2.4 %collective-permute-done.6 = f32[8,1024]{1,0:T(8,128)S(1)} collective-permute-done((f32[8,1024]{1,0:T(8,128)S(1)}, f32[8,1024]{1,0:T(8,128)S(1)}, u32[]{:S(2)}, u32[]{:S(2)}) %collective-permute-start.6) | collective-permute-done | bytes 32800 | tf_op jit(solution)/shard_map/ppermute | solution.py:24
  66.8 3.0 %collective-permute-start.7 = (f32[1,8,1024]{2,1,0:T(8,128)S(1)}, f32[1,8,1024]{2,1,0:T(8,128)S(1)}, u32[]{:S(2)}, u32[]{:S(2)}) collective-permute-start(f32[1,8,1024]{2,1,0:T(8,128)S(1)} %fusion.1), channel_id=1, source_target_pairs={{0,4},{1,5},{2,6},{3,7},{4,0},{5,1},{6,2},{7,3},{8,12},{9,13},{10,... | collective-permute-start | bytes 98312 | tf_op jit(solution)/shard_map/ppermute | solution.py:24
  69.8 2.5 %collective-permute-done.7 = f32[1,8,1024]{2,1,0:T(8,128)S(1)} collective-permute-done((f32[1,8,1024]{2,1,0:T(8,128)S(1)}, f32[1,8,1024]{2,1,0:T(8,128)S(1)}, u32[]{:S(2)}, u32[]{:S(2)}) %collective-permute-start.7) | collective-permute-done | bytes 32800 | tf_op jit(solution)/shard_map/ppermute | solution.py:24
  72.2 1.4 %collective-permute-start.8 = (f32[2,8,1024]{2,1,0:T(8,128)S(1)}, f32[2,8,1024]{2,1,0:T(8,128)S(1)}, u32[]{:S(2)}, u32[]{:S(2)}) collective-permute-start(f32[2,8,1024]{2,1,0:T(8,128)S(1)} %pad_maximum_fusion.3), channel_id=1, source_target_pairs={{0,2},{1,3},{2,0},{3,1},{4,6},{5,7},{6,4},{7,5},{8,10},{9,11},{10,... | collective-permute-start | bytes 196616 | tf_op jit(solution)/shard_map/ppermute | solution.py:24
  73.7 1.9 %copy-done.1 = bf16[3072,512]{1,0:T(8,128)(2,1)S(1)} copy-done((bf16[3072,512]{1,0:T(8,128)(2,1)S(1)}, bf16[3072,512]{1,0:T(8,128)(2,1)}, u32[]{:S(2)}) %copy-start.1) | copy-done | bytes 3145752
  75.6 0.6 down.1
  76.5 1.5 %collective-permute-start.9 = (f32[4,8,1024]{2,1,0:T(8,128)S(1)}, f32[4,8,1024]{2,1,0:T(8,128)S(1)}, u32[]{:S(2)}, u32[]{:S(2)}) collective-permute-start(f32[4,8,1024]{2,1,0:T(8,128)S(1)} %pad_maximum_fusion.2), channel_id=1, source_target_pairs={{0,1},{1,0},{2,3},{3,2},{4,5},{5,4},{6,7},{7,6},{8,9},{9,8},{10,11... | collective-permute-start | bytes 393224 | tf_op jit(solution)/shard_map/ppermute | solution.py:24
  78.1 1.6 %collective-permute-start.1 = (bf16[64,512]{1,0:T(8,128)(2,1)S(1)}, bf16[64,512]{1,0:T(8,128)(2,1)S(1)}, u32[]{:S(2)}, u32[]{:S(2)}) collective-permute-start(bf16[64,512]{1,0:T(8,128)(2,1)S(1)} %add_convert_fusion.8.kept), channel_id=1, source_target_pairs={{0,16},{8,24},{16,0},{24,8},{1,17},{9,25},{17,1},{25,9},{2,18},{10... | collective-permute-start | bytes 196616 | tf_op jit(solution)/shard_map/ppermute | solution.py:24
  79.6 2.8 %collective-permute-done.1.arrived = bf16[64,512]{1,0:T(8,128)(2,1)S(1)} collective-permute-done((bf16[64,512]{1,0:T(8,128)(2,1)S(1)}, bf16[64,512]{1,0:T(8,128)(2,1)S(1)}, u32[]{:S(2)}, u32[]{:S(2)}) %collective-permute-start.1) | collective-permute-done | bytes 65568 | tf_op jit(solution)/shard_map/ppermute | solution.py:24
  82.4 0.3 teacher_block.1
  82.8 1.1 collective-permute-start.2
  83.8 2.7 %collective-permute-done.2 = f32[32,128]{1,0:T(8,128)S(1)} collective-permute-done((f32[32,128]{1,0:T(8,128)S(1)}, f32[32,128]{1,0:T(8,128)S(1)}, u32[]{:S(2)}, u32[]{:S(2)}) %collective-permute-start.2) | collective-permute-done | bytes 16416 | tf_op jit(solution)/shard_map/ppermute | solution.py:24
  86.5 1.4 %collective-permute-start.3 = (f32[32,128]{1,0:T(8,128)S(1)}, f32[32,128]{1,0:T(8,128)S(1)}, u32[]{:S(2)}, u32[]{:S(2)}) collective-permute-start(f32[32,128]{1,0:T(8,128)S(1)} %add.46), channel_id=1, source_target_pairs={{0,2},{1,3},{2,0},{3,1},{4,6},{5,7},{6,4},{7,5},{8,10},{9,11},{10,... | collective-permute-start | bytes 49160 | tf_op jit(solution)/shard_map/ppermute | solution.py:24
  87.9 2.3 %collective-permute-done.3 = f32[32,128]{1,0:T(8,128)S(1)} collective-permute-done((f32[32,128]{1,0:T(8,128)S(1)}, f32[32,128]{1,0:T(8,128)S(1)}, u32[]{:S(2)}, u32[]{:S(2)}) %collective-permute-start.3) | collective-permute-done | bytes 16416 | tf_op jit(solution)/shard_map/ppermute | solution.py:24
  90.3 2.5 %collective-permute-start.4 = (f32[32,128]{1,0:T(8,128)S(1)}, f32[32,128]{1,0:T(8,128)S(1)}, u32[]{:S(2)}, u32[]{:S(2)}) collective-permute-start(f32[32,128]{1,0:T(8,128)S(1)} %add.47.gram_kept), channel_id=1, source_target_pairs={{0,4},{1,5},{2,6},{3,7},{4,0},{5,1},{6,2},{7,3},{8,12},{9,13},{10,... | collective-permute-start | bytes 49160 | tf_op jit(solution)/shard_map/ppermute | solution.py:24
  92.8 0.5 embed.1
  93.3 1.6 %collective-permute-done.4.gram_arrived = f32[32,128]{1,0:T(8,128)S(1)} collective-permute-done((f32[32,128]{1,0:T(8,128)S(1)}, f32[32,128]{1,0:T(8,128)S(1)}, u32[]{:S(2)}, u32[]{:S(2)}) %collective-permute-start.4) | collective-permute-done | bytes 16416 | tf_op jit(solution)/shard_map/ppermute | solution.py:24
  94.9 5.2 %contrast.1 = (f32[1,1]{1,0:T(1,128)}, bf16[64,1024]{1,0:T(8,128)(2,1)S(1)}, f32[8,1024]{1,0:T(8,128)S(1)}, bf16[4,128,512]{2,1,0:T(8,128)(2,1)S(1)}, bf16[4,128,512]{2,1,0:T(8,128)(2,1)S(1)}) custom-call(s32[1]{0:T(128)} %bitcast.place, s32[8]{0:T(128)S(1)} %copy-done.6, f32[32,128]{1,0:T(8,128)S(1)} %add.47.gram_kept, ...), custom_call_target="tpu_custom_call" | custom-call | tf_op jit(solution)/shard_map/contrast/pallas_call | solution.py:367
  100.1 1.1 collective-permute-start.10
  101.3 1.0 collective-permute-start.13
  102.2 3.8 %weigh.1 = (bf16[4,128,512]{2,1,0:T(8,128)(2,1)S(1)}, bf16[4,128,512]{2,1,0:T(8,128)(2,1)S(1)}) custom-call(s32[1]{0:T(128)} %bitcast.place, f32[8,1024]{1,0:T(8,128)S(1)} %get-tuple-element.33.scale, bf16[2,2,1024,512]{3,2,1,0:T(8,128)(2,1)} %get-tuple-element.30.refs_0_, bf16[6,2,1024,512]{3,2,1,0:T(8,128)(2,1)} %get-tuple-element.31.refs_1_, ...), custom_call_target="tpu_custom_call" | custom-call | tf_op jit(solution)/shard_map/weigh/pallas_call | solution.py:394
  106.0 4.9 %collective-permute-done.10 = bf16[4,128,512]{2,1,0:T(8,128)(2,1)S(1)} collective-permute-done((bf16[4,128,512]{2,1,0:T(8,128)(2,1)S(1)}, bf16[4,128,512]{2,1,0:T(8,128)(2,1)S(1)}, u32[]{:S(2)}, u32[]{:S(2)}) %collective-permute-start.10) | collective-permute-done | bytes 524320 | tf_op jit(solution)/shard_map/ppermute | solution.py:24
  110.9 1.7 %collective-permute-done.13 = bf16[4,128,512]{2,1,0:T(8,128)(2,1)S(1)} collective-permute-done((bf16[4,128,512]{2,1,0:T(8,128)(2,1)S(1)}, bf16[4,128,512]{2,1,0:T(8,128)(2,1)S(1)}, u32[]{:S(2)}, u32[]{:S(2)}) %collective-permute-start.13) | collective-permute-done | bytes 524320 | tf_op jit(solution)/shard_map/ppermute | solution.py:24
  112.9 0.4 collective-permute-start.14
  113.4 2.0 %collective-permute-start.11 = (bf16[2,128,512]{2,1,0:T(8,128)(2,1)S(1)}, bf16[2,128,512]{2,1,0:T(8,128)(2,1)S(1)}, u32[]{:S(2)}, u32[]{:S(2)}) collective-permute-start(bf16[2,128,512]{2,1,0:T(8,128)(2,1)S(1)} %get-tuple-element.50), channel_id=1, source_target_pairs={{0,2},{1,3},{2,0},{3,1},{4,6},{5,7},{6,4},{7,5},{8,10},{9,11},{10,... | collective-permute-start | bytes 786440 | tf_op jit(solution)/shard_map/ppermute | solution.py:24
  115.3 0.7 pad_maximum_fusion.1
  116.0 4.4 %all-to-all-start.3 = ((f32[8,8,640]{2,1,0:T(8,128)}), f32[8,8,640]{2,1,0:T(8,128)S(1)}, u32[]{:S(2)}, u32[]{:S(2)}) async-start(f32[8,8,640]{2,1,0:T(8,128)} %pad_maximum_fusion.1), calls=%async_computation.3 | async-start | bytes 327680 | tf_op jit(solution)/shard_map/all_to_all | solution.py:19
  120.5 3.0 %collective-permute-start.15 = (bf16[1,128,512]{2,1,0:T(8,128)(2,1)S(1)}, bf16[1,128,512]{2,1,0:T(8,128)(2,1)S(1)}, u32[]{:S(2)}, u32[]{:S(2)}) collective-permute-start(bf16[1,128,512]{2,1,0:T(8,128)(2,1)S(1)} %get-tuple-element.46), channel_id=1, source_target_pairs={{0,4},{1,5},{2,6},{3,7},{4,0},{5,1},{6,2},{7,3},{8,12},{9,13},{10,... | collective-permute-start | bytes 393224 | tf_op jit(solution)/shard_map/ppermute | solution.py:24
  123.6 1.8 %collective-permute-start.12 = (bf16[1,128,512]{2,1,0:T(8,128)(2,1)S(1)}, bf16[1,128,512]{2,1,0:T(8,128)(2,1)S(1)}, u32[]{:S(2)}, u32[]{:S(2)}) collective-permute-start(bf16[1,128,512]{2,1,0:T(8,128)(2,1)S(1)} %get-tuple-element.48), channel_id=1, source_target_pairs={{0,4},{1,5},{2,6},{3,7},{4,0},{5,1},{6,2},{7,3},{8,12},{9,13},{10,... | collective-permute-start | bytes 393224 | tf_op jit(solution)/shard_map/ppermute | solution.py:24
  125.4 2.6 %all-to-all-done.3 = f32[8,8,640]{2,1,0:T(8,128)S(1)} async-done(((f32[8,8,640]{2,1,0:T(8,128)}), f32[8,8,640]{2,1,0:T(8,128)S(1)}, u32[]{:S(2)}, u32[]{:S(2)}) %all-to-all-start.3) | async-done | bytes 163872 | tf_op jit(solution)/shard_map/all_to_all | solution.py:19
  128.0 1.0 fusion.3
  129.0 0.6 constant_dynamic-slice_fusion
  129.7 1.4 %collective-permute-done.15.refs_3_ = bf16[1,128,512]{2,1,0:T(8,128)(2,1)S(1)} collective-permute-done((bf16[1,128,512]{2,1,0:T(8,128)(2,1)S(1)}, bf16[1,128,512]{2,1,0:T(8,128)(2,1)S(1)}, u32[]{:S(2)}, u32[]{:S(2)}) %collective-permute-start.15) | collective-permute-done | bytes 131104 | tf_op jit(solution)/shard_map/ppermute | solution.py:24
  131.1 1.4 %collective-permute-done.12.refs_1_ = bf16[1,128,512]{2,1,0:T(8,128)(2,1)S(1)} collective-permute-done((bf16[1,128,512]{2,1,0:T(8,128)(2,1)S(1)}, bf16[1,128,512]{2,1,0:T(8,128)(2,1)S(1)}, u32[]{:S(2)}, u32[]{:S(2)}) %collective-permute-start.12) | collective-permute-done | bytes 131104 | tf_op jit(solution)/shard_map/ppermute | solution.py:24
  132.5 0.8 finish.1
  (41 shorter events, 0.9 us)
Async XLA Ops:
  0.6 14.2 %all-to-all-start = ((bf16[8,8,512]{2,1,0:T(8,128)(2,1)}), bf16[8,8,512]{2,1,0:T(8,128)(2,1)S(1)}, u32[]{:S(2)}, u32[]{:S(2)}) async-start(bf16[8,8,512]{2,1,0:T(8,128)(2,1)} %bitcast.37), calls=%async_computation | async-start | bytes 131072 | tf_op jit(solution)/shard_map/all_to_all | solution.py:19
  14.9 0.6 copy-start.2
  20.4 29.9 %all-to-all-start.1 = ((bf16[8,8,6144]{2,1,0:T(8,128)(2,1)}), bf16[8,8,6144]{2,1,0:T(8,128)(2,1)S(1)}, u32[]{:S(2)}, u32[]{:S(2)}) async-start(bf16[8,8,6144]{2,1,0:T(8,128)(2,1)} %bitcast.40), calls=%async_computation.1 | async-start | bytes 1572864 | tf_op jit(solution)/shard_map/all_to_all | solution.py:19
  31.9 17.6 %copy-start.8 = (f32[2,1,1024]{2,1,0:T(1,128)S(1)}, f32[2,1,1024]{2,1,0:T(1,128)}, u32[]{:S(2)}) copy-start(f32[2,1,1024]{2,1,0:T(1,128)} %get-tuple-element.25) | copy-start | bytes 24580
  31.9 18.4 %copy-start.4 = (bf16[8,4096]{1,0:T(8,128)(2,1)S(1)}, bf16[8,4096]{1,0:T(8,128)(2,1)}, u32[]{:S(2)}) copy-start(bf16[8,4096]{1,0:T(8,128)(2,1)} %after.1) | copy-start | bytes 196612
  31.9 29.3 %copy-start = (bf16[1024,1024]{1,0:T(8,128)(2,1)S(1)}, bf16[1024,1024]{1,0:T(8,128)(2,1)}, u32[]{:S(2)}) copy-start(bf16[1024,1024]{1,0:T(8,128)(2,1)} %w_out.1) | copy-start | bytes 6291460
  49.5 14.8 %copy-start.9 = (f32[2,1,1024]{2,1,0:T(1,128)S(1)}, f32[2,1,1024]{2,1,0:T(1,128)}, u32[]{:S(2)}) copy-start(f32[2,1,1024]{2,1,0:T(1,128)} %get-tuple-element.23) | copy-start | bytes 24580
  49.5 14.8 %copy-start.7 = (f32[6,1,1024]{2,1,0:T(1,128)S(1)}, f32[6,1,1024]{2,1,0:T(1,128)}, u32[]{:S(2)}) copy-start(f32[6,1,1024]{2,1,0:T(1,128)} %get-tuple-element.24) | copy-start | bytes 73732
  51.3 22.4 %all-to-all-start.2 = ((bf16[8,8,3072]{2,1,0:T(8,128)(2,1)}), bf16[8,8,3072]{2,1,0:T(8,128)(2,1)S(1)}, u32[]{:S(2)}, u32[]{:S(2)}) async-start(bf16[8,8,3072]{2,1,0:T(8,128)(2,1)} %hidden.1), calls=%async_computation.2 | async-start | bytes 786432 | tf_op jit(solution)/shard_map/all_to_all | solution.py:19
  61.2 21.2 %copy-start.3 = (bf16[8,8,512]{2,1,0:T(8,128)(2,1)S(1)}, bf16[8,8,512]{2,1,0:T(8,128)(2,1)}, u32[]{:S(2)}) copy-start(bf16[8,8,512]{2,1,0:T(8,128)(2,1)} %copy-done.2) | copy-start | bytes 196612
  61.2 21.2 %copy-start.5 = (f32[4096]{0:T(1024)S(1)}, f32[4096]{0:T(1024)}, u32[]{:S(2)}) copy-start(f32[4096]{0:T(1024)} %param.19) | copy-start | bytes 49156
  61.6 33.3 %copy-start.6 = (s32[8]{0:T(128)S(1)}, s32[8]{0:T(128)}, u32[]{:S(2)}) copy-start(s32[8]{0:T(128)} %lens.5) | copy-start | bytes 100
  61.6 1.2 collective-permute-start.5
  62.8 3.9 %collective-permute-start.6 = (f32[8,1024]{1,0:T(8,128)S(1)}, f32[8,1024]{1,0:T(8,128)S(1)}, u32[]{:S(2)}, u32[]{:S(2)}) collective-permute-start(f32[8,1024]{1,0:T(8,128)S(1)} %add.48), channel_id=1, source_target_pairs={{0,16},{8,24},{16,0},{24,8},{1,17},{9,25},{17,1},{25,9},{2,18},{10... | collective-permute-start | bytes 98312 | tf_op jit(solution)/shard_map/ppermute | solution.py:24
  66.8 5.5 %collective-permute-start.7 = (f32[1,8,1024]{2,1,0:T(8,128)S(1)}, f32[1,8,1024]{2,1,0:T(8,128)S(1)}, u32[]{:S(2)}, u32[]{:S(2)}) collective-permute-start(f32[1,8,1024]{2,1,0:T(8,128)S(1)} %fusion.1), channel_id=1, source_target_pairs={{0,4},{1,5},{2,6},{3,7},{4,0},{5,1},{6,2},{7,3},{8,12},{9,13},{10,... | collective-permute-start | bytes 98312 | tf_op jit(solution)/shard_map/ppermute | solution.py:24
  72.2 4.3 %collective-permute-start.8 = (f32[2,8,1024]{2,1,0:T(8,128)S(1)}, f32[2,8,1024]{2,1,0:T(8,128)S(1)}, u32[]{:S(2)}, u32[]{:S(2)}) collective-permute-start(f32[2,8,1024]{2,1,0:T(8,128)S(1)} %pad_maximum_fusion.3), channel_id=1, source_target_pairs={{0,2},{1,3},{2,0},{3,1},{4,6},{5,7},{6,4},{7,5},{8,10},{9,11},{10,... | collective-permute-start | bytes 196616 | tf_op jit(solution)/shard_map/ppermute | solution.py:24
  73.7 1.9 %copy-start.1 = (bf16[3072,512]{1,0:T(8,128)(2,1)S(1)}, bf16[3072,512]{1,0:T(8,128)(2,1)}, u32[]{:S(2)}) copy-start(bf16[3072,512]{1,0:T(8,128)(2,1)} %weights.3) | copy-start | bytes 9437188
  76.2 1.8 %collective-permute-start = (f32[64,512]{1,0:T(8,128)S(1)}, f32[64,512]{1,0:T(8,128)S(1)}, u32[]{:S(2)}, u32[]{:S(2)}) collective-permute-start(f32[64,512]{1,0:T(8,128)S(1)} %down.1), channel_id=1, source_target_pairs={{0,8},{8,0},{16,24},{24,16},{1,9},{9,1},{17,25},{25,17},{2,10},{10... | collective-permute-start | bytes 393224 | tf_op jit(solution)/shard_map/ppermute | solution.py:24
  76.5 16.3 %collective-permute-start.9 = (f32[4,8,1024]{2,1,0:T(8,128)S(1)}, f32[4,8,1024]{2,1,0:T(8,128)S(1)}, u32[]{:S(2)}, u32[]{:S(2)}) collective-permute-start(f32[4,8,1024]{2,1,0:T(8,128)S(1)} %pad_maximum_fusion.2), channel_id=1, source_target_pairs={{0,1},{1,0},{2,3},{3,2},{4,5},{5,4},{6,7},{7,6},{8,9},{9,8},{10,11... | collective-permute-start | bytes 393224 | tf_op jit(solution)/shard_map/ppermute | solution.py:24
  78.1 4.3 %collective-permute-start.1 = (bf16[64,512]{1,0:T(8,128)(2,1)S(1)}, bf16[64,512]{1,0:T(8,128)(2,1)S(1)}, u32[]{:S(2)}, u32[]{:S(2)}) collective-permute-start(bf16[64,512]{1,0:T(8,128)(2,1)S(1)} %add_convert_fusion.8.kept), channel_id=1, source_target_pairs={{0,16},{8,24},{16,0},{24,8},{1,17},{9,25},{17,1},{25,9},{2,18},{10... | collective-permute-start | bytes 196616 | tf_op jit(solution)/shard_map/ppermute | solution.py:24
  82.8 3.7 %collective-permute-start.2 = (f32[32,128]{1,0:T(8,128)S(1)}, f32[32,128]{1,0:T(8,128)S(1)}, u32[]{:S(2)}, u32[]{:S(2)}) collective-permute-start(f32[32,128]{1,0:T(8,128)S(1)} %get-tuple-element.22), channel_id=1, source_target_pairs={{0,1},{1,0},{2,3},{3,2},{4,5},{5,4},{6,7},{7,6},{8,9},{9,8},{10,11... | collective-permute-start | bytes 49160 | tf_op jit(solution)/shard_map/ppermute | solution.py:24
  86.5 3.7 %collective-permute-start.3 = (f32[32,128]{1,0:T(8,128)S(1)}, f32[32,128]{1,0:T(8,128)S(1)}, u32[]{:S(2)}, u32[]{:S(2)}) collective-permute-start(f32[32,128]{1,0:T(8,128)S(1)} %add.46), channel_id=1, source_target_pairs={{0,2},{1,3},{2,0},{3,1},{4,6},{5,7},{6,4},{7,5},{8,10},{9,11},{10,... | collective-permute-start | bytes 49160 | tf_op jit(solution)/shard_map/ppermute | solution.py:24
  90.3 4.6 %collective-permute-start.4 = (f32[32,128]{1,0:T(8,128)S(1)}, f32[32,128]{1,0:T(8,128)S(1)}, u32[]{:S(2)}, u32[]{:S(2)}) collective-permute-start(f32[32,128]{1,0:T(8,128)S(1)} %add.47.gram_kept), channel_id=1, source_target_pairs={{0,4},{1,5},{2,6},{3,7},{4,0},{5,1},{6,2},{7,3},{8,12},{9,13},{10,... | collective-permute-start | bytes 49160 | tf_op jit(solution)/shard_map/ppermute | solution.py:24
  100.1 10.8 %collective-permute-start.10 = (bf16[4,128,512]{2,1,0:T(8,128)(2,1)S(1)}, bf16[4,128,512]{2,1,0:T(8,128)(2,1)S(1)}, u32[]{:S(2)}, u32[]{:S(2)}) collective-permute-start(bf16[4,128,512]{2,1,0:T(8,128)(2,1)S(1)} %get-tuple-element.34.refs_2_), channel_id=1, source_target_pairs={{0,1},{1,0},{2,3},{3,2},{4,5},{5,4},{6,7},{7,6},{8,9},{9,8},{10,11... | collective-permute-start | bytes 1572872 | tf_op jit(solution)/shard_map/ppermute | solution.py:24
  101.3 11.4 %collective-permute-start.13 = (bf16[4,128,512]{2,1,0:T(8,128)(2,1)S(1)}, bf16[4,128,512]{2,1,0:T(8,128)(2,1)S(1)}, u32[]{:S(2)}, u32[]{:S(2)}) collective-permute-start(bf16[4,128,512]{2,1,0:T(8,128)(2,1)S(1)} %get-tuple-element.35.refs_3_), channel_id=1, source_target_pairs={{0,2},{1,3},{2,0},{3,1},{4,6},{5,7},{6,4},{7,5},{8,10},{9,11},{10,... | collective-permute-start | bytes 1572872 | tf_op jit(solution)/shard_map/ppermute | solution.py:24
  112.9 7.5 %collective-permute-start.14 = (bf16[2,128,512]{2,1,0:T(8,128)(2,1)S(1)}, bf16[2,128,512]{2,1,0:T(8,128)(2,1)S(1)}, u32[]{:S(2)}, u32[]{:S(2)}) collective-permute-start(bf16[2,128,512]{2,1,0:T(8,128)(2,1)S(1)} %get-tuple-element.43), channel_id=1, source_target_pairs={{0,1},{1,0},{2,3},{3,2},{4,5},{5,4},{6,7},{7,6},{8,9},{9,8},{10,11... | collective-permute-start | bytes 786440 | tf_op jit(solution)/shard_map/ppermute | solution.py:24
  113.4 10.1 %collective-permute-start.11 = (bf16[2,128,512]{2,1,0:T(8,128)(2,1)S(1)}, bf16[2,128,512]{2,1,0:T(8,128)(2,1)S(1)}, u32[]{:S(2)}, u32[]{:S(2)}) collective-permute-start(bf16[2,128,512]{2,1,0:T(8,128)(2,1)S(1)} %get-tuple-element.50), channel_id=1, source_target_pairs={{0,2},{1,3},{2,0},{3,1},{4,6},{5,7},{6,4},{7,5},{8,10},{9,11},{10,... | collective-permute-start | bytes 786440 | tf_op jit(solution)/shard_map/ppermute | solution.py:24
  116.0 12.0 %all-to-all-start.3 = ((f32[8,8,640]{2,1,0:T(8,128)}), f32[8,8,640]{2,1,0:T(8,128)S(1)}, u32[]{:S(2)}, u32[]{:S(2)}) async-start(f32[8,8,640]{2,1,0:T(8,128)} %pad_maximum_fusion.1), calls=%async_computation.3 | async-start | bytes 327680 | tf_op jit(solution)/shard_map/all_to_all | solution.py:19
  120.5 10.6 %collective-permute-start.15 = (bf16[1,128,512]{2,1,0:T(8,128)(2,1)S(1)}, bf16[1,128,512]{2,1,0:T(8,128)(2,1)S(1)}, u32[]{:S(2)}, u32[]{:S(2)}) collective-permute-start(bf16[1,128,512]{2,1,0:T(8,128)(2,1)S(1)} %get-tuple-element.46), channel_id=1, source_target_pairs={{0,4},{1,5},{2,6},{3,7},{4,0},{5,1},{6,2},{7,3},{8,12},{9,13},{10,... | collective-permute-start | bytes 393224 | tf_op jit(solution)/shard_map/ppermute | solution.py:24
  123.6 8.9 %collective-permute-start.12 = (bf16[1,128,512]{2,1,0:T(8,128)(2,1)S(1)}, bf16[1,128,512]{2,1,0:T(8,128)(2,1)S(1)}, u32[]{:S(2)}, u32[]{:S(2)}) collective-permute-start(bf16[1,128,512]{2,1,0:T(8,128)(2,1)S(1)} %get-tuple-element.48), channel_id=1, source_target_pairs={{0,4},{1,5},{2,6},{3,7},{4,0},{5,1},{6,2},{7,3},{8,12},{9,13},{10,... | collective-permute-start | bytes 393224 | tf_op jit(solution)/shard_map/ppermute | solution.py:24
